TPU v7x, 32 devices: a whole 2x2x4 slice. The times are simulated.
32 devices in a mesh: ty: 8 (over y, x, core), tx: 4 (over z).
Axes of the slice: x: 2, y: 2, z: 4, core: 2. Of those that a mesh axis runs over, the one named last changes fastest.
Arguments:
- queries: bfloat16 [64, 64, 1024], P('ty', 'tx'), may hold values from -6 to 6
- fine_key_rows: bfloat16 [64, 64, 1024], P('ty', 'tx'), may hold values from -6 to 6
- fine_value_rows: bfloat16 [64, 64, 1024], P('ty', 'tx'), may hold values from -6 to 6
- fine_query_tangent: bfloat16 [64, 64, 1024], P('ty', 'tx'), may hold values from -6 to 6
- fine_key_tangent: bfloat16 [64, 64, 1024], P('ty', 'tx'), may hold values from -6 to 6
- fine_value_tangent: bfloat16 [64, 64, 1024], P('ty', 'tx'), may hold values from -6 to 6
- fine_head_scale: float32 [16], replicated, may hold values from 2 to 20
- merged_token_weight: bfloat16 [1024, 1024], replicated, may hold values from -0.1875 to 0.1875
- time_plan_index: int32 [2], replicated, may hold values from 0 to 999
- time_modulation_weight: float32 [256, 4096], replicated, may hold values from -0.09375 to 0.09375
- coarse_projection_weight: bfloat16 [1024, 16, 192], P(None, 'tx'), may hold values from -0.1875 to 0.1875
- coarse_head_scale: float32 [16], P('tx'), may hold values from 2 to 20
- head_output_weight: bfloat16 [16, 64, 1024], P('tx'), may hold values from -0.1875 to 0.1875
- up_projection_weight: bfloat16 [1024, 4096], P(None, 'tx'), may hold values from -0.1875 to 0.1875
- down_projection_weight: bfloat16 [4096, 1024], P('tx'), may hold values from -0.09375 to 0.09375
Outputs:
- fine_out: bfloat16 [64, 64, 1024], P('ty', 'tx')
- fine_tangent: bfloat16 [64, 64, 1024], P('ty', 'tx')
- coarse_out: bfloat16 [16, 16, 1024], P('ty', 'tx')
- coarse_tangent: bfloat16 [16, 16, 1024], P('ty', 'tx')
Inputs may be any that keep to these rules, and one draw needn't show every extreme that they name: `time_plan_index`: two indices into the plan t_k = k / 1000; the larger gives t, the smaller r.
All inputs are finite; a program needn't handle non-finite values.
Results may differ from a plain program's by a relative error of at most 0.035.
Values may be sent and summed in bfloat16 or wider, within the bound.
No kernel may reach another device: no remote copies, remote signals or barrier semaphores. Data moves between devices by JAX's collectives and lax.ppermute only.
A program may use at most 64 MiB of HBM per device.

v0:
```python
import jax
import jax.numpy as jnp
from jax import lax
from jax.sharding import PartitionSpec as P

EMBED = 128
RADIUS = 3
MERGE = 4
STEPS = 1000


EPSILON = 1e-06


def padded(cells, sides, width):
    for axis, dim in sides:
        count = lax.axis_size(axis)
        ends = count - 1
        head = lax.slice_in_dim(cells, 0, width, axis=dim)
        tail = lax.slice_in_dim(cells, cells.shape[dim] - width, cells.shape[dim], axis=dim)
        cells = jnp.concatenate(
            [
                lax.ppermute(tail, axis, [(i, (i + 1) % count) for i in range(ends)]),
                cells,
                lax.ppermute(head, axis, [((i + 1) % count, i) for i in range(ends)]),
            ],
            axis=dim,
        )
    return cells


def normed_pair(values, tangent):
    factor = lax.rsqrt(jnp.mean(values * values, axis=-1, keepdims=True) + EPSILON)
    normed = values * factor
    drift = (tangent - normed * jnp.mean(normed * tangent, axis=-1, keepdims=True)) * factor
    return (normed, drift)


def modulation(time_plan_index, time_modulation_weight):
    latest = jnp.max(time_plan_index)
    earlier = jnp.min(time_plan_index)
    moment = latest.astype(jnp.float32) / STEPS
    spacing = (latest - earlier).astype(jnp.float32) / STEPS
    halves = EMBED // 2
    angular = 16.0 ** (jnp.arange(halves).astype(jnp.float32) / halves)
    embedded = jnp.concatenate(
        [
            jnp.cos(angular * moment),
            jnp.sin(angular * moment),
            jnp.cos(angular * spacing),
            jnp.sin(angular * spacing),
        ]
    )
    slopes = jnp.concatenate(
        [
            -angular * jnp.sin(angular * moment),
            angular * jnp.cos(angular * moment),
            -angular * jnp.sin(angular * spacing),
            angular * jnp.cos(angular * spacing),
        ]
    )
    result = jnp.dot(
        jnp.stack([embedded, slopes]), time_modulation_weight, precision=lax.Precision.HIGHEST
    )
    return (jnp.split(result[0], 4), jnp.split(result[1], 4))


def conditioned(values, tangent, offset, stretch, offset_drift, stretch_drift):
    normed, drift = normed_pair(values, tangent)
    primal = (normed * (1.0 + stretch) + offset).astype(jnp.bfloat16)
    moving = (drift * (1.0 + stretch) + normed * stretch_drift + offset_drift).astype(jnp.bfloat16)
    return (primal, moving)


def gelu_tanh(values):
    return jax.nn.gelu(values, approximate=True)


def block_terms(query_pair, keyset, factor):
    query_normalized, query_velocity = query_pair
    key_normalized, value_head, key_velocity, value_drift = keyset
    scores = (
        jnp.einsum(
            "qhd,khd->hqk", query_normalized, key_normalized, preferred_element_type=jnp.float32
        )
        * factor[:, None, None]
    )
    slopes = (
        jnp.einsum(
            "qhd,khd->hqk", query_velocity, key_normalized, preferred_element_type=jnp.float32
        )
        + jnp.einsum(
            "qhd,khd->hqk", query_normalized, key_velocity, preferred_element_type=jnp.float32
        )
    ) * factor[:, None, None]
    weights = jnp.exp(scores)
    tilted = weights * slopes
    weights_low = weights.astype(jnp.bfloat16)
    tilted_low = tilted.astype(jnp.bfloat16)
    return (
        jnp.sum(weights, axis=-1),
        jnp.sum(tilted, axis=-1),
        jnp.einsum("hqk,khd->qhd", weights_low, value_head, preferred_element_type=jnp.float32),
        jnp.einsum("hqk,khd->qhd", tilted_low, value_head, preferred_element_type=jnp.float32),
        jnp.einsum("hqk,khd->qhd", weights_low, value_drift, preferred_element_type=jnp.float32),
    )


def finish(running):
    weight_sum, slope_sum, value_sum, turned, shifted = running
    inverse = (1.0 / weight_sum).T[:, :, None]
    output = value_sum * inverse
    return (output, (turned + shifted) * inverse - output * (slope_sum.T[:, :, None] * inverse))


def tile_attention(query_pair, keyset, factor, allowed):
    query_normalized, query_velocity = query_pair
    key_normalized, value_head, key_velocity, value_drift = keyset
    scores = (
        jnp.einsum(
            "qhd,khd->hqk", query_normalized, key_normalized, preferred_element_type=jnp.float32
        )
        * factor[:, None, None]
    )
    slopes = (
        jnp.einsum(
            "qhd,khd->hqk", query_velocity, key_normalized, preferred_element_type=jnp.float32
        )
        + jnp.einsum(
            "qhd,khd->hqk", query_normalized, key_velocity, preferred_element_type=jnp.float32
        )
    ) * factor[:, None, None]
    weights = jnp.where(allowed[None], jnp.exp(scores), 0.0)
    tilted = weights * slopes
    weights_low = weights.astype(jnp.bfloat16)
    tilted_low = tilted.astype(jnp.bfloat16)
    weight_sum = jnp.sum(weights, axis=-1).T[:, :, None]
    slope_sum = jnp.sum(tilted, axis=-1).T[:, :, None]
    value_sum = jnp.einsum(
        "hqk,khd->qhd", weights_low, value_head, preferred_element_type=jnp.float32
    )
    turned = jnp.einsum("hqk,khd->qhd", tilted_low, value_head, preferred_element_type=jnp.float32)
    shifted = jnp.einsum(
        "hqk,khd->qhd", weights_low, value_drift, preferred_element_type=jnp.float32
    )
    inverse = 1.0 / weight_sum
    output = value_sum * inverse
    return (output, (turned + shifted) * inverse - output * (slope_sum * inverse))


def shards(
    queries,
    fine_key_rows,
    fine_value_rows,
    fine_query_tangent,
    fine_key_tangent,
    fine_value_tangent,
    fine_head_scale,
    merged_token_weight,
    time_plan_index,
    time_modulation_weight,
    coarse_projection_weight,
    coarse_head_scale,
    head_output_weight,
    up_projection_weight,
    down_projection_weight,
):
    tile_rows, tile_columns, model_width = queries.shape
    number_of_heads = fine_head_scale.shape[0]
    head_channel_width = model_width // number_of_heads
    token_count = tile_rows * tile_columns
    by_head = (token_count, number_of_heads, head_channel_width)
    grid_shape = (tile_rows, tile_columns, model_width)

    def as_heads(array):
        return array.astype(jnp.float32).reshape(by_head)

    query_normalized, query_velocity = normed_pair(as_heads(queries), as_heads(fine_query_tangent))
    key_normalized, key_velocity = normed_pair(as_heads(fine_key_rows), as_heads(fine_key_tangent))
    neighbours = (
        padded(
            key_normalized.astype(jnp.bfloat16).reshape(grid_shape), (("ty", 0), ("tx", 1)), RADIUS
        ),
        padded(fine_value_rows, (("ty", 0), ("tx", 1)), RADIUS),
        padded(
            key_velocity.astype(jnp.bfloat16).reshape(grid_shape), (("ty", 0), ("tx", 1)), RADIUS
        ),
        padded(fine_value_tangent, (("ty", 0), ("tx", 1)), RADIUS),
    )
    span_rows = tile_rows + 2 * RADIUS
    span_columns = tile_columns + 2 * RADIUS
    key_count = span_rows * span_columns
    key_pad = -(-key_count // 128) * 128

    def flat_keys(member):
        return jnp.pad(
            member.reshape(key_count, number_of_heads, head_channel_width),
            ((0, key_pad - key_count), (0, 0), (0, 0)),
        )

    keyset = tuple((flat_keys(member) for member in neighbours))
    query_pair = (query_normalized.astype(jnp.bfloat16), query_velocity.astype(jnp.bfloat16))
    top_row = lax.axis_index("ty") * tile_rows
    left_column = lax.axis_index("tx") * tile_columns
    grid_rows = tile_rows * lax.axis_size("ty")
    grid_columns = tile_columns * lax.axis_size("tx")
    key_slot = jnp.arange(key_pad)
    key_row = key_slot // span_columns - RADIUS
    key_column = key_slot % span_columns - RADIUS
    places = jnp.arange(token_count)
    query_row = places // tile_columns
    query_column = places % tile_columns
    absolute_row = top_row + key_row
    absolute_column = left_column + key_column
    inside = (
        (key_slot < key_count)
        & (absolute_row >= 0)
        & (absolute_row < grid_rows)
        & (absolute_column >= 0)
        & (absolute_column < grid_columns)
    )
    near = (jnp.abs(query_row[:, None] - key_row[None, :]) <= RADIUS) & (
        jnp.abs(query_column[:, None] - key_column[None, :]) <= RADIUS
    )
    allowed = inside[None, :] & near
    fine_scale_factor = fine_head_scale / head_channel_width
    fine_output, fine_moving = tile_attention(query_pair, keyset, fine_scale_factor, allowed)
    fine_out = fine_output.reshape(grid_shape).astype(jnp.bfloat16)
    fine_tangent = fine_moving.reshape(grid_shape).astype(jnp.bfloat16)

    def pooled(tile_grid):
        return (
            jnp.mean(
                tile_grid.astype(jnp.float32).reshape(
                    tile_rows // MERGE, MERGE, tile_columns // MERGE, MERGE, model_width
                ),
                axis=(1, 3),
            )
            .reshape(-1, model_width)
            .astype(jnp.bfloat16)
        )

    coarse = jnp.dot(
        pooled(fine_out), merged_token_weight, preferred_element_type=jnp.float32
    ).astype(jnp.bfloat16)
    coarse_drift = jnp.dot(
        pooled(fine_tangent), merged_token_weight, preferred_element_type=jnp.float32
    ).astype(jnp.bfloat16)
    own_rows = coarse.shape[0]
    primal_mod, drift_mod = modulation(time_plan_index, time_modulation_weight)
    offset_a, stretch_a, offset_m, stretch_m = primal_mod
    offset_ad, stretch_ad, offset_md, stretch_md = drift_mod
    normed, normed_drift = conditioned(
        coarse.astype(jnp.float32),
        coarse_drift.astype(jnp.float32),
        offset_a,
        stretch_a,
        offset_ad,
        stretch_ad,
    )
    normed_rows, normed_rows_drift, residual_rows, residual_drift = (
        lax.all_gather(normed, "tx", axis=0, tiled=True),
        lax.all_gather(normed_drift, "tx", axis=0, tiled=True),
        lax.all_gather(coarse, "tx", axis=0, tiled=True),
        lax.all_gather(coarse_drift, "tx", axis=0, tiled=True),
    )
    neighbour_heads = coarse_head_scale.shape[0]
    group_rows = normed_rows.shape[0]
    packed = coarse_projection_weight.reshape(model_width, neighbour_heads * 3 * head_channel_width)
    projected_rows = jnp.dot(normed_rows, packed, preferred_element_type=jnp.float32).reshape(
        group_rows, neighbour_heads, 3 * head_channel_width
    )
    projected_velocity = jnp.dot(
        normed_rows_drift, packed, preferred_element_type=jnp.float32
    ).reshape(group_rows, neighbour_heads, 3 * head_channel_width)
    coarse_query_rows, coarse_query_velocity = normed_pair(
        projected_rows[..., :head_channel_width], projected_velocity[..., :head_channel_width]
    )
    coarse_key_rows, coarse_key_velocity = normed_pair(
        projected_rows[..., head_channel_width : 2 * head_channel_width],
        projected_velocity[..., head_channel_width : 2 * head_channel_width],
    )
    stacked = jnp.concatenate(
        [
            coarse_key_rows.astype(jnp.bfloat16),
            projected_rows[..., 2 * head_channel_width :].astype(jnp.bfloat16),
            coarse_key_velocity.astype(jnp.bfloat16),
            projected_velocity[..., 2 * head_channel_width :].astype(jnp.bfloat16),
        ],
        axis=-1,
    ).reshape(group_rows, neighbour_heads * 4 * head_channel_width)
    coarse_queries = (
        coarse_query_rows.astype(jnp.bfloat16),
        coarse_query_velocity.astype(jnp.bfloat16),
    )
    coarse_scale_factor = coarse_head_scale / head_channel_width
    portion = lax.all_gather(stacked, "ty", axis=0, tiled=True)
    pieces = portion.reshape(portion.shape[0], neighbour_heads, 4 * head_channel_width)
    portion_keys = tuple(
        (
            pieces[:, :, member * head_channel_width : (member + 1) * head_channel_width]
            for member in range(4)
        )
    )
    attended, attended_drift = finish(
        block_terms(coarse_queries, portion_keys, coarse_scale_factor)
    )
    merged_heads = attended.reshape(group_rows, neighbour_heads * head_channel_width).astype(
        jnp.bfloat16
    )
    merged_drift = attended_drift.reshape(group_rows, neighbour_heads * head_channel_width).astype(
        jnp.bfloat16
    )
    out_packed = head_output_weight.reshape(neighbour_heads * head_channel_width, model_width)
    mixture, mixture_drift = (
        lax.psum(
            jnp.dot(merged_heads, out_packed, preferred_element_type=jnp.float32).astype(
                jnp.bfloat16
            ),
            "tx",
        ).astype(jnp.float32),
        lax.psum(
            jnp.dot(merged_drift, out_packed, preferred_element_type=jnp.float32).astype(
                jnp.bfloat16
            ),
            "tx",
        ).astype(jnp.float32),
    )
    updated = residual_rows.astype(jnp.float32) + mixture
    updated_drift = residual_drift.astype(jnp.float32) + mixture_drift
    mlp_source, mlp_source_drift = conditioned(
        updated, updated_drift, offset_m, stretch_m, offset_md, stretch_md
    )
    own_start = lax.axis_index("tx") * own_rows
    updated_own = lax.dynamic_slice_in_dim(updated, own_start, own_rows, 0)
    updated_own_drift = lax.dynamic_slice_in_dim(updated_drift, own_start, own_rows, 0)
    hidden_in = jnp.dot(mlp_source, up_projection_weight, preferred_element_type=jnp.float32)
    hidden_in_drift = jnp.dot(
        mlp_source_drift, up_projection_weight, preferred_element_type=jnp.float32
    )
    hidden_out, hidden_out_drift = jax.jvp(gelu_tanh, (hidden_in,), (hidden_in_drift,))
    hidden_low = hidden_out.astype(jnp.bfloat16)
    hidden_low_drift = hidden_out_drift.astype(jnp.bfloat16)
    summed_mlp = lax.psum_scatter(
        jnp.concatenate(
            [
                jnp.dot(hidden_low, down_projection_weight, preferred_element_type=jnp.float32),
                jnp.dot(
                    hidden_low_drift, down_projection_weight, preferred_element_type=jnp.float32
                ),
            ],
            axis=1,
        ).astype(jnp.bfloat16),
        "tx",
        scatter_dimension=0,
        tiled=True,
    ).astype(jnp.float32)
    block_shape = (tile_rows // MERGE, tile_columns // MERGE, model_width)
    coarse_out = (
        (updated_own + summed_mlp[:, :model_width]).astype(jnp.bfloat16).reshape(block_shape)
    )
    coarse_tangent = (
        (updated_own_drift + summed_mlp[:, model_width:]).astype(jnp.bfloat16).reshape(block_shape)
    )
    return (fine_out, fine_tangent, coarse_out, coarse_tangent)


def solution(mesh):
    return jax.shard_map(
        shards,
        mesh=mesh,
        in_specs=(
            P("ty", "tx", None),
            P("ty", "tx", None),
            P("ty", "tx", None),
            P("ty", "tx", None),
            P("ty", "tx", None),
            P("ty", "tx", None),
            P(),
            P(),
            P(),
            P(),
            P(None, "tx", None),
            P("tx"),
            P("tx", None, None),
            P(None, "tx"),
            P("tx", None),
        ),
        out_specs=(
            P("ty", "tx", None),
            P("ty", "tx", None),
            P("ty", "tx", None),
            P("ty", "tx", None),
        ),
        check_vma=False,
    )
```

profile of v0, /device:TPU:0, one launch (start us, length us, event | category | flops | bytes accessed | tf_op | source)
XLA Modules:
  0.0 264.0 jit_solution(8278470896663984634)
XLA Ops:
  10.3 1.9 multiply_reduce_fusion
  14.1 3.0 %collective-permute-start.4 = (bf16[3,16,1024]{2,1,0:T(8,128)(2,1)}, bf16[3,16,1024]{2,1,0:T(8,128)(2,1)}, u32[]{:S(2)}, u32[]{:S(2)}) collective-permute-start(bf16[3,16,1024]{2,1,0:T(8,128)(2,1)} %slice.121), channel_id=1, source_target_pairs={{0,4},{4,8},{8,12},{12,16},{16,20},{20,24},{24,28},{1,5},{5,9},{9,... | collective-permute-start | bytes 294920 | tf_op jit(solution)/shard_map/ppermute | solution.py:23
  20.0 5.1 %collective-permute-start.8 = (bf16[3,16,1024]{2,1,0:T(8,128)(2,1)}, bf16[3,16,1024]{2,1,0:T(8,128)(2,1)}, u32[]{:S(2)}, u32[]{:S(2)}) collective-permute-start(bf16[3,16,1024]{2,1,0:T(8,128)(2,1)} %slice.127), channel_id=1, source_target_pairs={{0,4},{4,8},{8,12},{12,16},{16,20},{20,24},{24,28},{1,5},{5,9},{9,... | collective-permute-start | bytes 294920 | tf_op jit(solution)/shard_map/ppermute | solution.py:23
  28.0 4.3 %collective-permute-start.12 = (bf16[3,16,1024]{2,1,0:T(8,128)(2,1)}, bf16[3,16,1024]{2,1,0:T(8,128)(2,1)}, u32[]{:S(2)}, u32[]{:S(2)}) collective-permute-start(bf16[3,16,1024]{2,1,0:T(8,128)(2,1)} %get-tuple-element.35), channel_id=1, source_target_pairs={{0,4},{4,8},{8,12},{12,16},{16,20},{20,24},{24,28},{1,5},{5,9},{9,... | collective-permute-start | bytes 294920 | tf_op jit(solution)/shard_map/ppermute | solution.py:23
  41.8 2.3 reshape.340
  44.1 1.9 multiply_reduce_fusion.1
  49.4 4.4 %fusion.129 = f32[2,4096]{1,0:T(2,128)S(1)} fusion(f32[256,4096]{1,0:T(8,128)} %param.24, f32[1,256]{1,0:T(1,128)S(1)} %bitcast.107, f32[1,256]{1,0:T(1,128)S(1)} %bitcast.106), kind=kOutput, calls=%fused_computation.192 | convolution fusion | flops 25166336 | bytes 4229120 | tf_op jit(solution)/shard_map/dot_general | solution.py:62
  59.2 3.6 %collective-permute-start = (bf16[3,16,1024]{2,1,0:T(8,128)(2,1)}, bf16[3,16,1024]{2,1,0:T(8,128)(2,1)S(1)}, u32[]{:S(2)}, u32[]{:S(2)}) collective-permute-start(bf16[3,16,1024]{2,1,0:T(8,128)(2,1)} %get-tuple-element.37), channel_id=1, source_target_pairs={{0,4},{4,8},{8,12},{12,16},{16,20},{20,24},{24,28},{1,5},{5,9},{9,... | collective-permute-start | bytes 294920 | tf_op jit(solution)/shard_map/ppermute | solution.py:23
  65.2 3.5 %collective-permute-start.6 = (bf16[14,3,1024]{2,1,0:T(4,128)(2,1)S(1)}, bf16[14,3,1024]{2,1,0:T(4,128)(2,1)S(1)}, u32[]{:S(2)}, u32[]{:S(2)}) collective-permute-start(bf16[14,3,1024]{2,1,0:T(4,128)(2,1)S(1)} %get-tuple-element.30), channel_id=1, source_target_pairs={{0,1},{1,2},{2,3},{4,5},{5,6},{6,7},{8,9},{9,10},{10,11},{12,13},{... | collective-permute-start | bytes 258056 | tf_op jit(solution)/shard_map/ppermute | solution.py:23
  71.6 5.2 %collective-permute-start.10 = (bf16[14,3,1024]{2,1,0:T(4,128)(2,1)}, bf16[14,3,1024]{2,1,0:T(4,128)(2,1)}, u32[]{:S(2)}, u32[]{:S(2)}) collective-permute-start(bf16[14,3,1024]{2,1,0:T(4,128)(2,1)} %get-tuple-element.26), channel_id=1, source_target_pairs={{0,1},{1,2},{2,3},{4,5},{5,6},{6,7},{8,9},{9,10},{10,11},{12,13},{... | collective-permute-start | bytes 258056 | tf_op jit(solution)/shard_map/ppermute | solution.py:23
  79.1 5.2 %collective-permute-start.14 = (bf16[14,3,1024]{2,1,0:T(4,128)(2,1)}, bf16[14,3,1024]{2,1,0:T(4,128)(2,1)}, u32[]{:S(2)}, u32[]{:S(2)}) collective-permute-start(bf16[14,3,1024]{2,1,0:T(4,128)(2,1)} %get-tuple-element.28), channel_id=1, source_target_pairs={{0,1},{1,2},{2,3},{4,5},{5,6},{6,7},{8,9},{9,10},{10,11},{12,13},{... | collective-permute-start | bytes 258056 | tf_op jit(solution)/shard_map/ppermute | solution.py:23
  87.1 5.2 %collective-permute-start.2 = (bf16[14,3,1024]{2,1,0:T(4,128)(2,1)}, bf16[14,3,1024]{2,1,0:T(4,128)(2,1)}, u32[]{:S(2)}, u32[]{:S(2)}) collective-permute-start(bf16[14,3,1024]{2,1,0:T(4,128)(2,1)} %get-tuple-element.32), channel_id=1, source_target_pairs={{0,1},{1,2},{2,3},{4,5},{5,6},{6,7},{8,9},{9,10},{10,11},{12,13},{... | collective-permute-start | bytes 258056 | tf_op jit(solution)/shard_map/ppermute | solution.py:23
  92.3 2.1 pad_maximum_fusion.1
  94.4 1.9 reshape.326
  99.4 2.3 pad_maximum_fusion.2
  101.7 1.9 reshape.330
  105.4 2.3 pad_maximum_fusion.3
  107.7 1.9 reshape.331
  116.2 2.6 fusion.167
  122.0 2.1 copy.30
  124.1 3.6 %fusion.166 = (bf16[128,16,64]{0,2,1:T(8,128)(2,1)}, f32[128,16,64]{0,2,1:T(8,128)S(1)}) fusion(f32[128,16]{0,1:T(8,128)S(1)} %divide_bitcast_fusion, f32[16,128,384]{2,1,0:T(8,128)} %copy-done.1, f32[16]{0:T(128)S(1)} %broadcast_multiply_fusion.7, pred[128,384]{1,0:T(8,128)(4,1)S(1)} %fusion.45, bf16[308,16,64]{0,2,1:T(8,128)(2,1)S(1)} %copy.30), kind=kOutput, calls=%fused_computation.255 | convolution fusion | flops 103284736 | bytes 4620352 | tf_op jit(solution)/shard_map/hqk,khd->qhd/dot_general | solution.py:139
  135.4 2.2 fusion.106
  138.2 14.2 %all_gather.16 = bf16[32,1024]{1,0:T(8,128)(2,1)S(1)} all-gather(bf16[8,1024]{1,0:T(8,128)(2,1)S(1)} %get-tuple-element.53), channel_id=1, replica_groups=mesh['ty'=8,'tx'=4] {'tx'}, dimensions={0}, use_global_device_ids=true | all-gather | bytes 81920 | tf_op jit(solution)/shard_map/all_gather | solution.py:262
  153.3 13.2 %all_gather.17 = bf16[32,1024]{1,0:T(8,128)(2,1)S(1)} all-gather(bf16[8,1024]{1,0:T(8,128)(2,1)S(1)} %get-tuple-element.54), channel_id=1, replica_groups=mesh['ty'=8,'tx'=4] {'tx'}, dimensions={0}, use_global_device_ids=true | all-gather | bytes 81920 | tf_op jit(solution)/shard_map/all_gather | solution.py:263
  167.5 17.0 %all_gather.18 = bf16[256,1024]{1,0:T(8,128)(2,1)} all-gather(bf16[32,1024]{1,0:T(8,128)(2,1)S(1)} %bitcast.96), channel_id=1, replica_groups=mesh['ty'=8,'tx'=4] {'ty'}, dimensions={0}, use_global_device_ids=true | all-gather | bytes 589824 | tf_op jit(solution)/shard_map/all_gather | solution.py:297
  188.9 2.1 fusion.28
  191.0 13.2 %all_gather.15 = bf16[32,1024]{1,0:T(8,128)(2,1)S(1)} all-gather(bf16[8,1024]{1,0:T(8,128)(2,1)S(1)} %get-tuple-element.62), channel_id=1, replica_groups=mesh['ty'=8,'tx'=4] {'tx'}, dimensions={0}, use_global_device_ids=true | all-gather | bytes 81920 | tf_op jit(solution)/shard_map/all_gather | solution.py:264
  204.3 13.2 %all_gather.19 = bf16[32,1024]{1,0:T(8,128)(2,1)S(1)} all-gather(bf16[8,1024]{1,0:T(8,128)(2,1)S(1)} %get-tuple-element.64), channel_id=1, replica_groups=mesh['ty'=8,'tx'=4] {'tx'}, dimensions={0}, use_global_device_ids=true | all-gather | bytes 81920 | tf_op jit(solution)/shard_map/all_gather | solution.py:265
  217.5 9.0 %all-reduce.7.cloned.1.call-done = (bf16[32,1024]{1,0:T(8,128)(2,1)}, bf16[32,1024]{1,0:T(8,128)(2,1)}) async-done(((bf16[32,1024]{1,0:T(8,128)(2,1)}, bf16[32,1024]{1,0:T(8,128)(2,1)}), (bf16[32,1024]{1,0:T(8,128)(2,1)}, bf16[32,1024]{1,0:T(8,128)(2,1)})) %all-reduce.7.cloned.1.call-update) | async-done | bytes 131088 | tf_op jit(solution)/shard_map/psum | solution.py:316
  229.1 2.2 fusion.68
  231.8 2.6 convolution_convert_fusion
  238.0 16.4 %reduce-scatter.2.cloned.1.call-done = bf16[8,2048]{1,0:T(8,128)(2,1)} async-done(((bf16[32,2048]{1,0:T(8,128)(2,1)}), bf16[8,2048]{1,0:T(8,128)(2,1)}) %reduce-scatter.2.cloned.1.call-update) | async-done | bytes 32784 | tf_op jit(solution)/shard_map/reduce_scatter | solution.py:344
  (211 shorter events, 75.4 us)
Async XLA Ops:
  7.2 224.1 %copy-start = (bf16[1024,1024]{1,0:T(8,128)(2,1)S(1)}, bf16[1024,1024]{1,0:T(8,128)(2,1)}, u32[]{:S(2)}) copy-start(bf16[1024,1024]{1,0:T(8,128)(2,1)} %param.29) | copy-start | bytes 6291460
  7.2 219.2 %all-reduce.7.cloned.1.call-start = ((), (), s32[]{:S(2)}) async-start(), calls=%async_computation.2 | async-start | bytes 262144 | tf_op jit(solution)/shard_map/psum | solution.py:316
  13.1 14.2 %copy-start.23 = (bf16[8,16,1024]{2,1,0:T(8,128)(2,1)S(1)}, bf16[8,16,1024]{2,1,0:T(8,128)(2,1)}, u32[]{:S(2)}) copy-start(bf16[8,16,1024]{2,1,0:T(8,128)(2,1)} %param.20) | copy-start | bytes 786436
  13.1 20.3 %copy-start.34 = (s32[2]{0:T(128)S(1)}, s32[2]{0:T(128)}, u32[]{:S(2)}) copy-start(s32[2]{0:T(128)} %param.23) | copy-start | bytes 28
  14.1 45.2 %collective-permute-start.4 = (bf16[3,16,1024]{2,1,0:T(8,128)(2,1)}, bf16[3,16,1024]{2,1,0:T(8,128)(2,1)}, u32[]{:S(2)}, u32[]{:S(2)}) collective-permute-start(bf16[3,16,1024]{2,1,0:T(8,128)(2,1)} %slice.121), channel_id=1, source_target_pairs={{0,4},{4,8},{8,12},{12,16},{16,20},{20,24},{24,28},{1,5},{5,9},{9,... | collective-permute-start | bytes 294920 | tf_op jit(solution)/shard_map/ppermute | solution.py:23
  17.9 45.0 %collective-permute-start.5 = (bf16[3,16,1024]{2,1,0:T(8,128)(2,1)}, bf16[3,16,1024]{2,1,0:T(8,128)(2,1)}, u32[]{:S(2)}, u32[]{:S(2)}) collective-permute-start(bf16[3,16,1024]{2,1,0:T(8,128)(2,1)} %slice.123), channel_id=1, source_target_pairs={{4,0},{8,4},{12,8},{16,12},{20,16},{24,20},{28,24},{5,1},{9,5},{13... | collective-permute-start | bytes 294920 | tf_op jit(solution)/shard_map/ppermute | solution.py:25
  20.0 45.2 %collective-permute-start.8 = (bf16[3,16,1024]{2,1,0:T(8,128)(2,1)}, bf16[3,16,1024]{2,1,0:T(8,128)(2,1)}, u32[]{:S(2)}, u32[]{:S(2)}) collective-permute-start(bf16[3,16,1024]{2,1,0:T(8,128)(2,1)} %slice.127), channel_id=1, source_target_pairs={{0,4},{4,8},{8,12},{12,16},{16,20},{20,24},{24,28},{1,5},{5,9},{9,... | collective-permute-start | bytes 294920 | tf_op jit(solution)/shard_map/ppermute | solution.py:23
  26.0 42.7 %collective-permute-start.9 = (bf16[3,16,1024]{2,1,0:T(8,128)(2,1)}, bf16[3,16,1024]{2,1,0:T(8,128)(2,1)}, u32[]{:S(2)}, u32[]{:S(2)}) collective-permute-start(bf16[3,16,1024]{2,1,0:T(8,128)(2,1)} %slice.129), channel_id=1, source_target_pairs={{4,0},{8,4},{12,8},{16,12},{20,16},{24,20},{28,24},{5,1},{9,5},{13... | collective-permute-start | bytes 294920 | tf_op jit(solution)/shard_map/ppermute | solution.py:25
  28.0 28.1 %collective-permute-start.12 = (bf16[3,16,1024]{2,1,0:T(8,128)(2,1)}, bf16[3,16,1024]{2,1,0:T(8,128)(2,1)}, u32[]{:S(2)}, u32[]{:S(2)}) collective-permute-start(bf16[3,16,1024]{2,1,0:T(8,128)(2,1)} %get-tuple-element.35), channel_id=1, source_target_pairs={{0,4},{4,8},{8,12},{12,16},{16,20},{20,24},{24,28},{1,5},{5,9},{9,... | collective-permute-start | bytes 294920 | tf_op jit(solution)/shard_map/ppermute | solution.py:23
  46.1 3.3 %copy-start.30 = (f32[64]{0:T(128)S(1)}, f32[64]{0:T(128)}, u32[]{:S(2)}) copy-start(f32[64]{0:T(128)} %get-tuple-element.79) | copy-start | bytes 772
  46.1 3.3 %copy-start.31 = (f32[64]{0:T(128)S(1)}, f32[64]{0:T(128)}, u32[]{:S(2)}) copy-start(f32[64]{0:T(128)} %get-tuple-element.82) | copy-start | bytes 772
  49.4 4.5 %copy-start.14 = (f32[8,16,1024]{2,1,0:T(8,128)S(1)}, f32[8,16,1024]{2,1,0:T(8,128)}, u32[]{:S(2)}) copy-start(f32[8,16,1024]{2,1,0:T(8,128)} %mul.429) | copy-start | bytes 1572868
  49.4 4.5 %copy-start.15 = (f32[8,16,1024]{2,1,0:T(8,128)S(1)}, f32[8,16,1024]{2,1,0:T(8,128)}, u32[]{:S(2)}) copy-start(f32[8,16,1024]{2,1,0:T(8,128)} %mul.415) | copy-start | bytes 1572868
  49.4 4.5 %copy-start.21 = (bf16[8,16,1024]{2,1,0:T(8,128)(2,1)S(1)}, bf16[8,16,1024]{2,1,0:T(8,128)(2,1)}, u32[]{:S(2)}) copy-start(bf16[8,16,1024]{2,1,0:T(8,128)(2,1)} %param.16) | copy-start | bytes 786436
  54.1 25.0 %copy-start.11 = (bf16[8,16,1024]{2,1,0:T(8,128)(2,1)}, bf16[8,16,1024]{2,1,0:T(8,128)(2,1)S(1)}, u32[]{:S(2)}) copy-start(bf16[8,16,1024]{2,1,0:T(8,128)(2,1)S(1)} %get-tuple-element.20) | copy-start | bytes 786436
  54.1 24.9 %copy-start.24 = (bf16[8,16,1024]{2,1,0:T(8,128)(2,1)S(1)}, bf16[8,16,1024]{2,1,0:T(8,128)(2,1)}, u32[]{:S(2)}) copy-start(bf16[8,16,1024]{2,1,0:T(8,128)(2,1)} %param.17) | copy-start | bytes 786436
  56.0 15.6 %collective-permute-start.13 = (bf16[3,16,1024]{2,1,0:T(8,128)(2,1)}, bf16[3,16,1024]{2,1,0:T(8,128)(2,1)S(1)}, u32[]{:S(2)}, u32[]{:S(2)}) collective-permute-start(bf16[3,16,1024]{2,1,0:T(8,128)(2,1)} %get-tuple-element.34), channel_id=1, source_target_pairs={{4,0},{8,4},{12,8},{16,12},{20,16},{24,20},{28,24},{5,1},{9,5},{13... | collective-permute-start | bytes 294920 | tf_op jit(solution)/shard_map/ppermute | solution.py:25
  59.2 18.5 %collective-permute-start = (bf16[3,16,1024]{2,1,0:T(8,128)(2,1)}, bf16[3,16,1024]{2,1,0:T(8,128)(2,1)S(1)}, u32[]{:S(2)}, u32[]{:S(2)}) collective-permute-start(bf16[3,16,1024]{2,1,0:T(8,128)(2,1)} %get-tuple-element.37), channel_id=1, source_target_pairs={{0,4},{4,8},{8,12},{12,16},{16,20},{20,24},{24,28},{1,5},{5,9},{9,... | collective-permute-start | bytes 294920 | tf_op jit(solution)/shard_map/ppermute | solution.py:23
  62.9 16.2 %collective-permute-start.1 = (bf16[3,16,1024]{2,1,0:T(8,128)(2,1)}, bf16[3,16,1024]{2,1,0:T(8,128)(2,1)S(1)}, u32[]{:S(2)}, u32[]{:S(2)}) collective-permute-start(bf16[3,16,1024]{2,1,0:T(8,128)(2,1)} %get-tuple-element.36), channel_id=1, source_target_pairs={{4,0},{8,4},{12,8},{16,12},{20,16},{24,20},{28,24},{5,1},{9,5},{13... | collective-permute-start | bytes 294920 | tf_op jit(solution)/shard_map/ppermute | solution.py:25
  65.2 20.7 %collective-permute-start.6 = (bf16[14,3,1024]{2,1,0:T(4,128)(2,1)S(1)}, bf16[14,3,1024]{2,1,0:T(4,128)(2,1)S(1)}, u32[]{:S(2)}, u32[]{:S(2)}) collective-permute-start(bf16[14,3,1024]{2,1,0:T(4,128)(2,1)S(1)} %get-tuple-element.30), channel_id=1, source_target_pairs={{0,1},{1,2},{2,3},{4,5},{5,6},{6,7},{8,9},{9,10},{10,11},{12,13},{... | collective-permute-start | bytes 258056 | tf_op jit(solution)/shard_map/ppermute | solution.py:23
  68.7 18.4 %collective-permute-start.7 = (bf16[14,3,1024]{2,1,0:T(4,128)(2,1)S(1)}, bf16[14,3,1024]{2,1,0:T(4,128)(2,1)S(1)}, u32[]{:S(2)}, u32[]{:S(2)}) collective-permute-start(bf16[14,3,1024]{2,1,0:T(4,128)(2,1)S(1)} %get-tuple-element.31), channel_id=1, source_target_pairs={{1,0},{2,1},{3,2},{5,4},{6,5},{7,6},{9,8},{10,9},{11,10},{13,12},{... | collective-permute-start | bytes 258056 | tf_op jit(solution)/shard_map/ppermute | solution.py:25
  71.6 26.5 %collective-permute-start.10 = (bf16[14,3,1024]{2,1,0:T(4,128)(2,1)}, bf16[14,3,1024]{2,1,0:T(4,128)(2,1)}, u32[]{:S(2)}, u32[]{:S(2)}) collective-permute-start(bf16[14,3,1024]{2,1,0:T(4,128)(2,1)} %get-tuple-element.26), channel_id=1, source_target_pairs={{0,1},{1,2},{2,3},{4,5},{5,6},{6,7},{8,9},{9,10},{10,11},{12,13},{... | collective-permute-start | bytes 258056 | tf_op jit(solution)/shard_map/ppermute | solution.py:23
  77.7 21.7 %collective-permute-start.11 = (bf16[14,3,1024]{2,1,0:T(4,128)(2,1)}, bf16[14,3,1024]{2,1,0:T(4,128)(2,1)}, u32[]{:S(2)}, u32[]{:S(2)}) collective-permute-start(bf16[14,3,1024]{2,1,0:T(4,128)(2,1)} %get-tuple-element.27), channel_id=1, source_target_pairs={{1,0},{2,1},{3,2},{5,4},{6,5},{7,6},{9,8},{10,9},{11,10},{13,12},{... | collective-permute-start | bytes 258056 | tf_op jit(solution)/shard_map/ppermute | solution.py:25
  79.1 26.3 %collective-permute-start.14 = (bf16[14,3,1024]{2,1,0:T(4,128)(2,1)}, bf16[14,3,1024]{2,1,0:T(4,128)(2,1)}, u32[]{:S(2)}, u32[]{:S(2)}) collective-permute-start(bf16[14,3,1024]{2,1,0:T(4,128)(2,1)} %get-tuple-element.28), channel_id=1, source_target_pairs={{0,1},{1,2},{2,3},{4,5},{5,6},{6,7},{8,9},{9,10},{10,11},{12,13},{... | collective-permute-start | bytes 258056 | tf_op jit(solution)/shard_map/ppermute | solution.py:23
  85.8 19.6 %collective-permute-start.15 = (bf16[14,3,1024]{2,1,0:T(4,128)(2,1)}, bf16[14,3,1024]{2,1,0:T(4,128)(2,1)}, u32[]{:S(2)}, u32[]{:S(2)}) collective-permute-start(bf16[14,3,1024]{2,1,0:T(4,128)(2,1)} %get-tuple-element.29), channel_id=1, source_target_pairs={{1,0},{2,1},{3,2},{5,4},{6,5},{7,6},{9,8},{10,9},{11,10},{13,12},{... | collective-permute-start | bytes 258056 | tf_op jit(solution)/shard_map/ppermute | solution.py:25
  87.1 31.7 %collective-permute-start.2 = (bf16[14,3,1024]{2,1,0:T(4,128)(2,1)}, bf16[14,3,1024]{2,1,0:T(4,128)(2,1)}, u32[]{:S(2)}, u32[]{:S(2)}) collective-permute-start(bf16[14,3,1024]{2,1,0:T(4,128)(2,1)} %get-tuple-element.32), channel_id=1, source_target_pairs={{0,1},{1,2},{2,3},{4,5},{5,6},{6,7},{8,9},{9,10},{10,11},{12,13},{... | collective-permute-start | bytes 258056 | tf_op jit(solution)/shard_map/ppermute | solution.py:23
  98.1 20.7 %collective-permute-start.3 = (bf16[14,3,1024]{2,1,0:T(4,128)(2,1)}, bf16[14,3,1024]{2,1,0:T(4,128)(2,1)}, u32[]{:S(2)}, u32[]{:S(2)}) collective-permute-start(bf16[14,3,1024]{2,1,0:T(4,128)(2,1)} %get-tuple-element.33), channel_id=1, source_target_pairs={{1,0},{2,1},{3,2},{5,4},{6,5},{7,6},{9,8},{10,9},{11,10},{13,12},{... | collective-permute-start | bytes 258056 | tf_op jit(solution)/shard_map/ppermute | solution.py:25
  124.1 3.6 %copy-start.6 = (bf16[16,128,384]{2,1,0:T(8,128)(2,1)S(1)}, bf16[16,128,384]{2,1,0:T(8,128)(2,1)}, u32[]{:S(2)}) copy-start(bf16[16,128,384]{2,1,0:T(8,128)(2,1)} %get-tuple-element.60) | copy-start | bytes 4718596
  124.1 3.6 %copy-start.12 = (f32[16,64,128]{2,1,0:T(8,128)S(1)}, f32[16,64,128]{2,1,0:T(8,128)}, u32[]{:S(2)}) copy-start(f32[16,64,128]{2,1,0:T(8,128)} %fusion.34) | copy-start | bytes 1572868
  135.4 17.1 %copy-start.5 = (bf16[1024,4,192]{0,2,1:T(8,128)(2,1)S(1)}, bf16[1024,4,192]{0,2,1:T(8,128)(2,1)}, u32[]{:S(2)}) copy-start(bf16[1024,4,192]{0,2,1:T(8,128)(2,1)} %param.25) | copy-start | bytes 4718596
  191.0 63.4 %reduce-scatter.2.cloned.1.call-start = ((), (), s32[]{:S(2)}) async-start(), calls=%async_computation.1 | async-start | bytes 163840 | tf_op jit(solution)/shard_map/reduce_scatter | solution.py:344
  231.8 3.7 %copy-start.10 = (bf16[128,16,64]{0,2,1:T(8,128)(2,1)S(1)}, bf16[128,16,64]{0,2,1:T(8,128)(2,1)}, u32[]{:S(2)}) copy-start(bf16[128,16,64]{0,2,1:T(8,128)(2,1)} %get-tuple-element.57) | copy-start | bytes 786436
  (23 other events, 40.4 us)
Sparse Core Ops, SparseCore 0:
  191.1 35.2 all-reduce.6
  235.2 19.1 reduce-scatter.1
where the time goes:
time: 266 us; the launch traced here: 264 us
  blocking collectives  70.8 us (27%)
  local copies, waits for them, and re-layouts  45.9 us (17%)
  starting transfers between devices  45.5 us (17%)
  matrix products  30.2 us (11%)
  other arithmetic  29.3 us (11%)
  waiting for transfers between devices  25.4 us (10%)
  between operations  16.9 us (6%)
    ppermute x8, starting transfers between devices, padded(): lax.ppermute(tail, axis, [(i, (i + 1) % count) for i in range(ends)])  35.1 us
    all_gather x1, blocking collectives, shards(): portion = lax.all_gather(stacked, 'ty', axis=0, tiled=True)  17 us
    reduce_scatter x1, waiting for transfers between devices, shards(): lax.psum_scatter(jnp.concatenate([jnp.dot(hidden_low, down_projection_wei...  16.4 us
    reshape x8, local copies, waits for them, and re-layouts, flat_keys(): member.reshape(key_count, number_of_heads, head_channel_width)  15 us
    all_gather x1, blocking collectives, shards(): lax.all_gather(normed, 'tx', axis=0, tiled=True)  14.2 us
    all_gather x1, blocking collectives, shards(): lax.all_gather(coarse, 'tx', axis=0, tiled=True)  13.2 us
    all_gather x1, blocking collectives, shards(): lax.all_gather(normed_drift, 'tx', axis=0, tiled=True)  13.2 us
    all_gather x1, blocking collectives, shards(): lax.all_gather(coarse_drift, 'tx', axis=0, tiled=True)  13.2 us
  transfers between devices with their start and end apart: 18, of which 2 were waited for; matrix products, arithmetic and copies ran while one was open for 22% of the time, Pallas kernels for 0%

commit v1 on v0

v1 whole, which is shorter than its diff:
```python
import functools
import math

import jax
import jax.numpy as jnp
import numpy as np
from jax import lax
from jax.experimental import pallas as pl
from jax.experimental.pallas import tpu as pltpu
from jax.sharding import PartitionSpec as P

EMBED = 128
RADIUS = 3
MERGE = 4
STEPS = 1000
EPSILON = 1e-06
LANES = 128
LOG2E = math.log2(math.e)
F32 = jnp.float32
BF16 = jnp.bfloat16


def dot(a, b):
    return jnp.dot(a, b, preferred_element_type=F32)


def dot_nt(a, b):
    return lax.dot_general(a, b, (((1,), (1,)), ((), ())), preferred_element_type=F32)


def block_ones(width, head, value):
    row = lax.broadcasted_iota(jnp.int32, (width, width), 0)
    col = lax.broadcasted_iota(jnp.int32, (width, width), 1)
    same = lax.shift_right_logical(row, head) == lax.shift_right_logical(col, head)
    return jnp.where(same, value, 0.0).astype(BF16)


def head_mean(values, ones):
    high = values.astype(BF16)
    low = (values - high.astype(F32)).astype(BF16)
    return dot(high, ones) + dot(low, ones)


def head_pair(values, tangent, ones):
    factor = lax.rsqrt(head_mean(values * values, ones) + EPSILON)
    normed = values * factor
    drift = (tangent - normed * head_mean(normed * tangent, ones)) * factor
    return normed.astype(BF16), drift.astype(BF16)


def row_pair(values, tangent):
    factor = lax.rsqrt(jnp.mean(values * values, axis=-1, keepdims=True) + EPSILON)
    normed = values * factor
    drift = (tangent - normed * jnp.mean(normed * tangent, axis=-1, keepdims=True)) * factor
    return normed, drift


def conditioned(values, tangent, mod, part, width):
    normed, drift = row_pair(values, tangent)
    offset = mod[0:1, 2 * part * width : (2 * part + 1) * width]
    stretch = mod[0:1, (2 * part + 1) * width : (2 * part + 2) * width]
    offset_drift = mod[1:2, 2 * part * width : (2 * part + 1) * width]
    stretch_drift = mod[1:2, (2 * part + 1) * width : (2 * part + 2) * width]
    primal = (normed * (1.0 + stretch) + offset).astype(BF16)
    moving = (drift * (1.0 + stretch) + normed * stretch_drift + offset_drift).astype(BF16)
    return primal, moving


def side(axis, phase):
    at = lax.axis_index(axis)
    after = (at & 1) == phase
    exists = jnp.where(after, at + 1 < lax.axis_size(axis), at > 0)
    return after, exists


def couples(count, phase):
    return [
        edge for i in range(phase, count - 1, 2) for edge in ((i, i + 1), (i + 1, i))
    ]


def partner(count, step, back=False):
    if count & (count - 1) == 0:
        return [(i, i ^ step) for i in range(count)]
    return [(i, (i - step if back else i + step) % count) for i in range(count)]


def gathered(value, axis):
    count = lax.axis_size(axis)
    return [value] + [
        lax.ppermute(value, axis, partner(count, step)) for step in range(1, count)
    ]


def returned(pieces, axis):
    count = lax.axis_size(axis)
    return [
        lax.ppermute(piece, axis, partner(count, step, True))
        for step, piece in zip(range(1, count), pieces)
    ]


def attend(query, query_drift, key, key_drift, value, value_drift, mask, factors, head):
    count = query.shape[0]
    lane = lax.broadcasted_iota(jnp.int32, (1, LANES), 1)
    first = (lane < head).astype(F32).astype(BF16)
    second = (lane >= head).astype(F32).astype(BF16)
    query_0, query_1 = query * first, query * second
    drift_0, drift_1 = query_drift * first, query_drift * second
    score = dot_nt(jnp.concatenate([query_0, query_1], 0), key)
    slope = dot_nt(
        jnp.concatenate(
            [
                jnp.concatenate([drift_0, query_0], 1),
                jnp.concatenate([drift_1, query_1], 1),
            ],
            0,
        ),
        jnp.concatenate([key, key_drift], 1),
    )
    weights, tilted = [], []
    for place, factor in enumerate(factors):
        rows = slice(place * count, (place + 1) * count)
        weight = jnp.exp2(score[rows] * (factor * LOG2E)) * mask
        weights.append(weight)
        tilted.append(weight * (slope[rows] * factor))
    weight = jnp.concatenate(weights, 0).astype(BF16)
    tilt = jnp.concatenate(tilted, 0).astype(BF16)
    ones = jnp.ones((key.shape[0], LANES), BF16)
    mixed = dot(weight, jnp.concatenate([value, value_drift], 1))
    turned = dot(tilt, value)
    total = dot(weight, ones)
    lean = dot(tilt, ones)

    def own(stack):
        return jnp.where(lane < head, stack[:count], stack[count:])

    return own(mixed[:, :LANES]), own(mixed[:, LANES:] + turned), own(total), own(lean)


def near(key_row, key_column, columns, count):
    place = lax.broadcasted_iota(jnp.int32, (count, 1), 0)
    shift = columns.bit_length() - 1
    row = lax.shift_right_logical(place, shift)
    column = place & (columns - 1)
    close = (jnp.abs(row - key_row) <= RADIUS) & (jnp.abs(column - key_column) <= RADIUS)
    return jnp.where(close, 1.0, 0.0)


def pack_kernel(head_tail, key, value, key_drift, value_drift, y0, y1, z0, z1):
    rows, columns, width = key.shape
    strip = RADIUS * columns
    band = head_tail.shape[1]
    for array, ref in enumerate((key, value, key_drift, value_drift)):
        flat = ref[...].reshape(rows * columns, width)
        for phase, (y, z) in enumerate(((y0, z0), (y1, z1))):
            down, _ = side("ty", phase)
            start = jnp.where(down, rows - RADIUS, 0)
            y[array * strip : (array + 1) * strip] = ref[pl.ds(start, RADIUS)].reshape(
                strip, width
            )
            right, _ = side("tx", phase)
            pick = head_tail[jnp.where(right, 1, 0)]
            z[array * band : (array + 1) * band] = dot(pick, flat).astype(BF16)


def corner_kernel(picks, z0, z1, c0, c1):
    for phase, c in enumerate((c0, c1)):
        down, _ = side("ty", phase)
        pick = picks[jnp.where(down, 1, 0)]
        half = z0.shape[0]
        c[...] = (dot(pick[:, :half], z0[...]) + dot(pick[:, half:], z1[...])).astype(BF16)


def own_kernel(head, scale, q, qd, k, kd, v, vd, qn, qdn, *sums):
    rows, columns, width = q.shape
    count = rows * columns
    pair = pl.program_id(0)
    ones = block_ones(LANES, head.bit_length() - 1, 1.0 / head)

    def flat(ref):
        return ref[...].reshape(count, width)

    query, query_drift = head_pair(flat(q).astype(F32), flat(qd).astype(F32), ones)
    key, key_drift = head_pair(flat(k).astype(F32), flat(kd).astype(F32), ones)
    qn[...] = query
    qdn[...] = query_drift
    place = lax.broadcasted_iota(jnp.int32, (1, count), 1)
    shift = columns.bit_length() - 1
    mask = near(lax.shift_right_logical(place, shift), place & (columns - 1), columns, count)
    factors = [scale[2 * pair + i] / head for i in range(2)]
    parts = attend(query, query_drift, key, key_drift, flat(v), flat(vd), mask, factors, head)
    for ref, part in zip(sums, parts):
        ref[...] = part


def halo_places(places, tile):
    rows, columns = tile
    row, column, group = places[0:1], places[1:2], places[2:3]
    outside = 4 * (rows + columns)
    for phase in range(2):
        down, below = side("ty", phase)
        right, beside = side("tx", phase)
        row_move = jnp.where(below, jnp.where(down, rows, -RADIUS), outside)
        column_move = jnp.where(beside, jnp.where(right, columns, -RADIUS), outside)
        row = row + jnp.where((group & (1 + phase)) != 0, row_move, 0)
        column = column + jnp.where((group & (4 + 4 * phase)) != 0, column_move, 0)
    return row, column


def strip_kernel(head, tile, scale, places, qn, qdn, z0, z1, y0, y1, *sums):
    pair = pl.program_id(0)
    ones = block_ones(LANES, head.bit_length() - 1, 1.0 / head)
    messages = (z0, z1, y0, y1)

    def part(array):
        pieces = []
        for ref in messages:
            size = ref.shape[0] // 4
            pieces.append(ref[array * size : (array + 1) * size])
        return jnp.concatenate(pieces, 0)

    key, key_drift = head_pair(part(0).astype(F32), part(2).astype(F32), ones)
    row, column = halo_places(places, tile)
    mask = near(row, column, tile[1], qn.shape[0])
    factors = [scale[2 * pair + i] / head for i in range(2)]
    parts = attend(
        qn[...], qdn[...], key, key_drift, part(1), part(3), mask, factors, head
    )
    for before, after, piece in zip(sums[:4], sums[4:], parts):
        after[...] = before[...] + piece


def last_kernel(
    head, tile, scale, places, unpack, pool, qn, qdn, c0, c1, a, ce, l, b, weight,
    out, tangent, coarse, running,
):
    pair = pl.program_id(0)
    ones = block_ones(LANES, head.bit_length() - 1, 1.0 / head)

    def part(array):
        pieces = [dot(unpack[array], c[...]) for c in (c0, c1)]
        return jnp.concatenate(pieces, 0)

    key, key_drift = head_pair(part(0), part(2), ones)
    row, column = halo_places(places, tile)
    mask = near(row, column, tile[1], qn.shape[0])
    factors = [scale[2 * pair + i] / head for i in range(2)]
    parts = attend(
        qn[...], qdn[...], key, key_drift, part(1).astype(BF16), part(3).astype(BF16),
        mask, factors, head,
    )
    inverse = 1.0 / (l[...] + parts[2])
    output = (a[...] + parts[0]) * inverse
    moving = (ce[...] + parts[1]) * inverse - output * ((b[...] + parts[3]) * inverse)
    output = output.astype(BF16)
    moving = moving.astype(BF16)
    out[...] = output.reshape(out.shape)
    tangent[...] = moving.reshape(out.shape)
    merged = jnp.concatenate([dot(pool[...], output), dot(pool[...], moving)], 0)
    step = dot(merged.astype(BF16), weight[...])

    @pl.when(pair == 0)
    def _():
        running[...] = step

    @pl.when(pair > 0)
    def _():
        running[...] += step

    @pl.when(pair == pl.num_programs(0) - 1)
    def _():
        coarse[...] = running[...].astype(BF16)


def stacked(refs):
    halves = [ref[...].astype(F32) for ref in refs]
    own = halves[0].shape[0] // 2
    return (
        jnp.concatenate([half[:own] for half in halves], 0),
        jnp.concatenate([half[own:] for half in halves], 0),
    )


def project_kernel(head, slots, mod, weight, *refs):
    tokens, (query_out, keys_out) = refs[:slots], refs[slots:]
    primal, moving = stacked(tokens)
    width = primal.shape[1]
    count = primal.shape[0]
    normed, drift = conditioned(primal, moving, mod, 0, width)
    projected = dot(jnp.concatenate([normed, drift], 0), weight[...])
    span = weight.shape[1] // 3
    ones = block_ones(span, head.bit_length() - 1, 1.0 / head)
    top, low = projected[:count], projected[count:]
    query = head_pair(top[:, :span], low[:, :span], ones)
    key = head_pair(top[:, span : 2 * span], low[:, span : 2 * span], ones)
    query_out[...] = jnp.concatenate(query, 1)
    keys_out[...] = jnp.concatenate(
        [key[0], top[:, 2 * span :].astype(BF16), key[1], low[:, 2 * span :].astype(BF16)], 1
    )


def coarse_kernel(head, slots, groups, scale, weight, query, *refs):
    blocks, outs = refs[:groups], refs[groups:]
    count = query.shape[0]
    span = query.shape[1] // 2
    heads = span // head

    def part(member):
        return jnp.concatenate(
            [block[:, member * span : (member + 1) * span] for block in blocks], 0
        )

    key, value, key_drift, value_drift = (part(member) for member in range(4))
    lane = lax.broadcasted_iota(jnp.int32, (1, span), 1)
    masks = [
        ((lane >= h * head) & (lane < (h + 1) * head)).astype(F32) for h in range(heads)
    ]
    plain, drifting = query[:, :span], query[:, span:]
    plain = jnp.concatenate([plain * mask.astype(BF16) for mask in masks], 0)
    drifting = jnp.concatenate([drifting * mask.astype(BF16) for mask in masks], 0)
    score = dot_nt(plain, key)
    slope = dot_nt(drifting, key) + dot_nt(plain, key_drift)
    weights, tilted = [], []
    for h in range(heads):
        rows = slice(h * count, (h + 1) * count)
        factor = scale[h] / head
        e = jnp.exp2(score[rows] * (factor * LOG2E))
        weights.append(e)
        tilted.append(e * (slope[rows] * factor))
    weights = jnp.concatenate(weights, 0).astype(BF16)
    tilted = jnp.concatenate(tilted, 0).astype(BF16)
    ones = jnp.ones((key.shape[0], span), BF16)

    def own(stack):
        return sum(
            stack[h * count : (h + 1) * count] * mask for h, mask in enumerate(masks)
        )

    inverse = 1.0 / own(dot(weights, ones))
    output = own(dot(weights, value)) * inverse
    shifted = own(dot(tilted, value) + dot(weights, value_drift))
    moving = shifted * inverse - output * (own(dot(tilted, ones)) * inverse)
    both = jnp.concatenate([output.astype(BF16), moving.astype(BF16)], 0)
    spread(dot(both, weight[...]), slots, outs)


def spread(both, slots, outs):
    count = both.shape[0] // 2
    own = count // slots
    for slot, out in enumerate(outs):
        piece = jnp.concatenate(
            [both[slot * own : (slot + 1) * own], both[count + slot * own : count + (slot + 1) * own]],
            0,
        )
        out[...] = piece.astype(out.dtype)


def update_kernel(slots, mod, coarse, *refs):
    parts, (updated, source) = refs[:slots], refs[slots:]
    total = coarse[...].astype(F32)
    for ref in parts:
        total = total + ref[...].astype(F32)
    updated[...] = total
    own, width = total.shape[0] // 2, total.shape[1]
    source[...] = jnp.concatenate(conditioned(total[:own], total[own:], mod, 1, width), 0)


def mlp_kernel(slots, up, down, *refs):
    tokens, outs, running = refs[:slots], refs[slots:-1], refs[-1]
    step = pl.program_id(0)
    primal, moving = stacked(tokens)
    count = primal.shape[0]
    both = jnp.concatenate([primal, moving], 0).astype(BF16)
    hidden = dot(both, up[...])
    x, dx = hidden[:count], hidden[count:]
    root = math.sqrt(2.0 / math.pi)
    square = x * x
    bend = jnp.tanh(root * (x + 0.044715 * (square * x)))
    half = 0.5 * (1.0 + bend)
    rise = half + 0.5 * x * (1.0 - bend * bend) * (root * (1.0 + 3 * 0.044715 * square))
    active = jnp.concatenate([(x * half).astype(BF16), (rise * dx).astype(BF16)], 0)
    result = dot(active, down[...])

    @pl.when(step == 0)
    def _():
        running[...] = result

    @pl.when(step > 0)
    def _():
        running[...] += result

    @pl.when(step == pl.num_programs(0) - 1)
    def _():
        spread(running[...], slots, outs)


def final_kernel(slots, updated, *refs):
    parts, (out, tangent) = refs[:slots], refs[slots:]
    total = updated[...]
    for ref in parts:
        total = total + ref[...].astype(F32)
    own = total.shape[0] // 2
    out[...] = total[:own].astype(BF16).reshape(out.shape)
    tangent[...] = total[own:].astype(BF16).reshape(out.shape)


def modulation(time_plan_index, time_modulation_weight):
    latest = jnp.max(time_plan_index)
    earlier = jnp.min(time_plan_index)
    moment = latest.astype(F32) / STEPS
    spacing = (latest - earlier).astype(F32) / STEPS
    halves = EMBED // 2
    angular = 16.0 ** (jnp.arange(halves).astype(F32) / halves)
    angles = jnp.concatenate([angular * moment, angular * spacing]).reshape(2, halves)
    cosine, sine = jnp.cos(angles), jnp.sin(angles)
    embedded = jnp.stack([cosine, sine], 1)
    slopes = jnp.stack([-angular * sine, angular * cosine], 1)
    features = jnp.stack([embedded.reshape(-1), slopes.reshape(-1)])
    return jnp.dot(features, time_modulation_weight, precision=lax.Precision.HIGHEST)


def struct(shape, dtype=BF16):
    return jax.ShapeDtypeStruct(shape, dtype)


def whole(array):
    return pl.BlockSpec(array.shape, lambda *_: (0,) * len(array.shape))


def smem():
    return pl.BlockSpec(memory_space=pltpu.SMEM)


def columns_of(array, width):
    lead = array.shape[:-1]
    return pl.BlockSpec(lead + (width,), lambda i: (0,) * len(lead) + (i,))


def one_call(kernel, outs, args, smem_count=0, name=None):
    return pl.pallas_call(
        kernel,
        grid=(1,),
        in_specs=[smem()] * smem_count + [whole(a) for a in args[smem_count:]],
        out_specs=[whole(o) for o in outs],
        out_shape=outs,
        name=name,
    )(*args)


def shards(
    queries,
    fine_key_rows,
    fine_value_rows,
    fine_query_tangent,
    fine_key_tangent,
    fine_value_tangent,
    fine_head_scale,
    merged_token_weight,
    time_plan_index,
    time_modulation_weight,
    coarse_projection_weight,
    coarse_head_scale,
    head_output_weight,
    up_projection_weight,
    down_projection_weight,
):
    rows, columns, width = queries.shape
    heads = fine_head_scale.shape[0]
    head = width // heads
    count = rows * columns
    pairs = width // LANES
    tile = (rows, columns)
    strip = RADIUS * columns
    side_tokens = RADIUS * rows
    band = -(-side_tokens // 16) * 16
    square = RADIUS * RADIUS
    corner_keys = 2 * square
    corner_band = -(-corner_keys // 16) * 16
    corner_rows = 4 * corner_keys

    head_tail = np.zeros((2, band, count), np.float32)
    for r in range(rows):
        for c in range(RADIUS):
            head_tail[0, r * RADIUS + c, r * columns + c] = 1
            head_tail[1, r * RADIUS + c, r * columns + columns - RADIUS + c] = 1
    picks = np.zeros((2, corner_rows, 8 * band), np.float32)
    unpack = np.zeros((4, corner_band, corner_rows), np.float32)
    corner_places = np.full((8, 2 * corner_band), 8 * (rows + columns), np.int32)
    corner_places[2:] = 0
    for array in range(4):
        for phase in range(2):
            for r in range(RADIUS):
                for c in range(RADIUS):
                    slot = phase * square + r * RADIUS + c
                    at = array * corner_keys + slot
                    unpack[array, slot, at] = 1
                    for low, first in ((0, 0), (1, rows - RADIUS)):
                        source = phase * 4 * band + array * band + (first + r) * RADIUS + c
                        picks[low, at, source] = 1
                    for meet in range(2):
                        key = meet * corner_band + slot
                        corner_places[:3, key] = (r, c, (1 + meet) + (4 + 4 * phase))
    strip_places = np.full((8, 2 * band + 2 * strip), 8 * (rows + columns), np.int32)
    strip_places[2:] = 0
    for phase in range(2):
        for r in range(rows):
            for c in range(RADIUS):
                strip_places[:3, phase * band + r * RADIUS + c] = (r, c, 4 + 4 * phase)
        for r in range(RADIUS):
            for c in range(columns):
                key = 2 * band + phase * strip + r * columns + c
                strip_places[:3, key] = (r, c, 1 + phase)
    blocks = (rows // MERGE, columns // MERGE)
    own = blocks[0] * blocks[1]
    pool = np.zeros((own, count), np.float32)
    for r in range(rows):
        for c in range(columns):
            pool[(r // MERGE) * blocks[1] + c // MERGE, r * columns + c] = 1 / (MERGE * MERGE)
    head_tail, picks, unpack, pool = (
        jnp.asarray(table, BF16) for table in (head_tail, picks, unpack, pool)
    )
    corner_places, strip_places = jnp.asarray(corner_places), jnp.asarray(strip_places)

    wide = 2 * LANES
    fields = (fine_key_rows, fine_value_rows, fine_key_tangent, fine_value_tangent)
    messages = (
        [struct((4 * strip, width))] * 2 + [struct((4 * band, width))] * 2
    )
    y0, y1, z0, z1 = pl.pallas_call(
        pack_kernel,
        grid=(width // wide,),
        in_specs=[whole(head_tail)] + [columns_of(f, wide) for f in fields],
        out_specs=[columns_of(m, wide) for m in messages],
        out_shape=messages,
        name="pack",
    )(head_tail, *fields)
    down_count, across_count = lax.axis_size("ty"), lax.axis_size("tx")
    y0, y1 = (
        lax.ppermute(y, "ty", couples(down_count, phase)) for phase, y in enumerate((y0, y1))
    )
    z0, z1 = (
        lax.ppermute(z, "tx", couples(across_count, phase)) for phase, z in enumerate((z0, z1))
    )

    flat = struct((count, width))
    sums = [struct((count, width), F32)] * 4
    fine = (
        queries, fine_query_tangent, fine_key_rows, fine_key_tangent, fine_value_rows,
        fine_value_tangent,
    )
    qn, qdn, *own_sums = pl.pallas_call(
        functools.partial(own_kernel, head),
        grid=(pairs,),
        in_specs=[smem()] + [columns_of(f, LANES) for f in fine],
        out_specs=[columns_of(o, LANES) for o in [flat] * 2 + sums],
        out_shape=[flat] * 2 + sums,
        name="own_attention",
    )(fine_head_scale, *fine)

    corner = struct((corner_rows, width))
    c0, c1 = pl.pallas_call(
        corner_kernel,
        grid=(width // wide,),
        in_specs=[whole(picks)] + [columns_of(z, wide) for z in (z0, z1)],
        out_specs=[columns_of(corner, wide)] * 2,
        out_shape=[corner] * 2,
        name="corners",
    )(picks, z0, z1)
    c0, c1 = (
        lax.ppermute(c, "ty", couples(down_count, phase)) for phase, c in enumerate((c0, c1))
    )
    strip_args = (qn, qdn, z0, z1, y0, y1, *own_sums)
    strip_sums = pl.pallas_call(
        functools.partial(strip_kernel, head, tile),
        grid=(pairs,),
        in_specs=[smem(), whole(strip_places)] + [columns_of(a, LANES) for a in strip_args],
        out_specs=[columns_of(o, LANES) for o in sums],
        out_shape=sums,
        input_output_aliases={8 + i: i for i in range(4)},
        name="strip_attention",
    )(fine_head_scale, strip_places, *strip_args)
    last_args = (qn, qdn, c0, c1, *strip_sums)
    grid_shape = struct(queries.shape)
    pooled = struct((2 * own, width))
    fine_out, fine_tangent, coarse = pl.pallas_call(
        functools.partial(last_kernel, head, tile),
        grid=(pairs,),
        in_specs=[smem()]
        + [whole(t) for t in (corner_places, unpack, pool)]
        + [columns_of(a, LANES) for a in last_args]
        + [pl.BlockSpec((LANES, width), lambda i: (i, 0))],
        out_specs=[columns_of(grid_shape, LANES)] * 2 + [whole(pooled)],
        out_shape=[grid_shape] * 2 + [pooled],
        scratch_shapes=[pltpu.VMEM((2 * own, width), F32)],
        name="last_attention",
    )(fine_head_scale, corner_places, unpack, pool, *last_args, merged_token_weight)

    mod = modulation(time_plan_index, time_modulation_weight)
    near_heads = coarse_head_scale.shape[0]
    span = near_heads * head
    packed = (
        coarse_projection_weight.reshape(width, near_heads, 3, head)
        .transpose(0, 2, 1, 3)
        .reshape(width, 3 * span)
    )
    slots = across_count
    tokens = gathered(coarse, "tx")
    group = slots * own
    query, keys = one_call(
        functools.partial(project_kernel, head, slots),
        [struct((group, 2 * span)), struct((group, 4 * span))],
        (mod, packed, *tokens),
        name="project",
    )
    key_blocks = gathered(keys, "ty")
    pieces = [struct((2 * own, width), F32)] + [struct((2 * own, width))] * (slots - 1)
    kept, *sent = one_call(
        functools.partial(coarse_kernel, head, slots, down_count),
        pieces,
        (coarse_head_scale, head_output_weight.reshape(span, width), query, *key_blocks),
        1,
        name="coarse_attention",
    )
    updated, source = one_call(
        functools.partial(update_kernel, slots),
        [struct((2 * own, width), F32), struct((2 * own, width))],
        (mod, coarse, kept, *returned(sent, "tx")),
        name="update",
    )
    sources = gathered(source, "tx")
    units = up_projection_weight.shape[1]
    step = min(units, wide)
    kept, *sent = pl.pallas_call(
        functools.partial(mlp_kernel, slots),
        grid=(units // step,),
        in_specs=[
            pl.BlockSpec((width, step), lambda i: (0, i)),
            pl.BlockSpec((step, width), lambda i: (i, 0)),
        ]
        + [whole(s) for s in sources],
        out_specs=[whole(p) for p in pieces],
        out_shape=pieces,
        scratch_shapes=[pltpu.VMEM((2 * group, width), F32)],
        name="mlp",
    )(up_projection_weight, down_projection_weight, *sources)
    block_shape = struct((*blocks, width))
    coarse_out, coarse_tangent = one_call(
        functools.partial(final_kernel, slots),
        [block_shape] * 2,
        (updated, kept, *returned(sent, "tx")),
        name="final",
    )
    return (fine_out, fine_tangent, coarse_out, coarse_tangent)


def solution(mesh):
    return jax.shard_map(
        shards,
        mesh=mesh,
        in_specs=(
            P("ty", "tx", None),
            P("ty", "tx", None),
            P("ty", "tx", None),
            P("ty", "tx", None),
            P("ty", "tx", None),
            P("ty", "tx", None),
            P(),
            P(),
            P(),
            P(),
            P(None, "tx", None),
            P("tx"),
            P("tx", None, None),
            P(None, "tx"),
            P("tx", None),
        ),
        out_specs=(
            P("ty", "tx", None),
            P("ty", "tx", None),
            P("ty", "tx", None),
            P("ty", "tx", None),
        ),
        check_vma=False,
    )
```

time: 266 us -> 121 us (0.45)
  blocking collectives: 70.8 us -> 0 us
  Pallas kernels: 0 us -> 48.1 us
  local copies, waits for them, and re-layouts: 45.9 us -> 8.63 us
  other arithmetic: 29.3 us -> 1.4 us
  matrix products: 30.2 us -> 4.86 us
  between operations: 16.9 us -> 2.84 us
  starting transfers between devices: 45.5 us -> 35.4 us
  waiting for transfers between devices: 25.4 us -> 17.4 us
    all_gather x5 -> x0, blocking collectives: 70.8 us -> none  [the longest x1 17 us: shards(): portion = lax.all_gather(stacked, 'ty', axis=0, tiled=True)]
    pallas_call x0 -> x10, Pallas kernels: none -> 48.1 us  [the longest x1 10.7 us: shards(): pl.pallas_call(functools.partial(last_kernel, head, tile), grid=(pairs,),...]
    dot_general x21 -> x1, matrix products: 30.2 us -> 4.86 us  [modulation(): jnp.dot(features, time_modulation_weight, precision=lax.Precision.HIGHEST)]
    reshape x15 -> x1, local copies, waits for them, and re-layouts: 22.4 us -> 1.58 us  [shards(): packed = coarse_projection_weight.reshape(width, near_heads, 3, head).tra...]
    ppermute x16 -> x25, waiting for transfers between devices: 0.04 us -> 17.4 us  [the longest x13 7.89 us: gathered(): lax.ppermute(value, axis, partner(count, step))]
    reduce_scatter x1 -> x0, waiting for transfers between devices: 16.4 us -> none  [shards(): lax.psum_scatter(jnp.concatenate([jnp.dot(hidden_low, down_projection_wei...]
    ppermute x16 -> x25, starting transfers between devices: 45.4 us -> 35.4 us  [the longest x13 20.4 us: gathered(): lax.ppermute(value, axis, partner(count, step))]
    psum x1 -> x0, waiting for transfers between devices: 8.98 us -> none  [shards(): lax.psum(jnp.dot(merged_heads, out_packed, preferred_element_type=jnp.flo...]
  transfers between devices with their start and end apart: 18 -> 25, of which waited for: 2 -> 10; matrix products, arithmetic and copies ran while one was open for 22% -> 7% of each run, Pallas kernels for 0% -> 17%
where the time goes in v1:
time: 121 us; the launch traced here: 119 us
  Pallas kernels  48.1 us (40%)
  starting transfers between devices  35.4 us (29%)
  waiting for transfers between devices  17.4 us (14%)
  local copies, waits for them, and re-layouts  8.63 us (7%)
  matrix products  4.86 us (4%)
  between operations  2.84 us (2%)
  other arithmetic  1.4 us (1%)
    ppermute x13, starting transfers between devices, gathered(): lax.ppermute(value, axis, partner(count, step))  20.4 us
    pallas_call x1, Pallas kernels, shards(): pl.pallas_call(functools.partial(last_kernel, head, tile), grid=(pairs,),...  10.7 us
    pallas_call x1, Pallas kernels, shards(): pl.pallas_call(functools.partial(strip_kernel, head, tile), grid=(pairs,)...  8.82 us
    ppermute x6, starting transfers between devices, returned(): lax.ppermute(piece, axis, partner(count, step, True))  8.81 us
    pallas_call x4, Pallas kernels, one_call(): pl.pallas_call(kernel, grid=(1,), in_specs=[smem()] * smem_count + [whole...  8.63 us
    pallas_call x1, Pallas kernels, shards(): pl.pallas_call(functools.partial(own_kernel, head), grid=(pairs,), in_spe...  7.98 us
    ppermute x13, waiting for transfers between devices, gathered(): lax.ppermute(value, axis, partner(count, step))  7.89 us
    ppermute x6, waiting for transfers between devices, returned(): lax.ppermute(piece, axis, partner(count, step, True))  7.68 us
  transfers between devices with their start and end apart: 25, of which 10 were waited for; matrix products, arithmetic and copies ran while one was open for 7% of the time, Pallas kernels for 17%

profile of v1, /device:TPU:0, one launch (start us, length us, event | category | flops | bytes accessed | tf_op | source)
XLA Modules:
  0.0 118.6 jit_solution(7997396725870506399)
XLA Ops:
  0.6 3.6 %pack.1 = (bf16[192,1024]{1,0:T(8,128)(2,1)}, bf16[192,1024]{1,0:T(8,128)(2,1)}, bf16[128,1024]{1,0:T(8,128)(2,1)}, bf16[128,1024]{1,0:T(8,128)(2,1)}) custom-call(bf16[2,32,128]{2,1,0:T(8,128)(2,1)} %constant.25.clone.head_tail, bf16[8,16,1024]{2,1,0:T(8,128)(2,1)} %key.1, bf16[8,16,1024]{2,1,0:T(8,128)(2,1)} %value.1, bf16[8,16,1024]{2,1,0:T(8,128)(2,1)} %key_drift.1, ...), custom_call_target="tpu_custom_call" | custom-call | tf_op jit(solution)/shard_map/pack/pallas_call | solution.py:530
  4.2 3.1 %collective-permute-start = (bf16[128,1024]{1,0:T(8,128)(2,1)}, bf16[128,1024]{1,0:T(8,128)(2,1)S(1)}, u32[]{:S(2)}, u32[]{:S(2)}) collective-permute-start(bf16[128,1024]{1,0:T(8,128)(2,1)} %get-tuple-element.39), channel_id=1, source_target_pairs={{0,1},{1,0},{2,3},{3,2},{4,5},{5,4},{6,7},{7,6},{8,9},{9,8},{10,11... | collective-permute-start | bytes 786440 | tf_op jit(solution)/shard_map/ppermute | solution.py:543
  8.8 1.3 %fusion.8 = (s32[]{:T(128)}, s32[]{:T(128)}) fusion(s32[2]{0:T(128)} %param.29), kind=kLoop, calls=%fused_computation.17 | loop fusion | flops 2 | bytes 16 | tf_op jit(solution)/shard_map/reduce_min | solution.py:410
  12.1 1.8 %collective-permute-done.z0 = bf16[128,1024]{1,0:T(8,128)(2,1)S(1)} collective-permute-done((bf16[128,1024]{1,0:T(8,128)(2,1)}, bf16[128,1024]{1,0:T(8,128)(2,1)S(1)}, u32[]{:S(2)}, u32[]{:S(2)}) %collective-permute-start) | collective-permute-done | bytes 262176 | tf_op jit(solution)/shard_map/ppermute | solution.py:543
  15.2 3.5 %corners.1 = (bf16[72,1024]{1,0:T(8,128)(2,1)}, bf16[72,1024]{1,0:T(8,128)(2,1)}) custom-call(bf16[2,72,256]{2,1,0:T(8,128)(2,1)} %constant.26.clone.picks, bf16[128,1024]{1,0:T(8,128)(2,1)} %copy-done.1, bf16[128,1024]{1,0:T(8,128)(2,1)} %copy-done.2), custom_call_target="tpu_custom_call" | custom-call | tf_op jit(solution)/shard_map/corners/pallas_call | solution.py:562
  20.7 8.0 %own_attention.1 = (bf16[128,1024]{1,0:T(8,128)(2,1)}, bf16[128,1024]{1,0:T(8,128)(2,1)}, f32[128,1024]{1,0:T(8,128)}, f32[128,1024]{1,0:T(8,128)}, f32[128,1024]{1,0:T(8,128)}, /*index=5*/f32[128,1024]{1,0:T(8,128)}) custom-call(f32[16]{0:T(128)} %scale.6, bf16[8,16,1024]{2,1,0:T(8,128)(2,1)} %q.1, bf16[8,16,1024]{2,1,0:T(8,128)(2,1)} %qd.1, ...), custom_call_target="tpu_custom_call" | custom-call | tf_op jit(solution)/shard_map/own_attention/pallas_call | solution.py:552
  29.6 8.8 %strip_attention.1 = (f32[128,1024]{1,0:T(8,128)}, f32[128,1024]{1,0:T(8,128)}, f32[128,1024]{1,0:T(8,128)}, f32[128,1024]{1,0:T(8,128)}) custom-call(f32[16]{0:T(128)} %scale.6, s32[8,160]{1,0:T(8,128)} %constant.30.clone.places, bf16[128,1024]{1,0:T(8,128)(2,1)} %get-tuple-element.37.qn, ...), custom_call_target="tpu_custom_call", output_to_operand_aliasing={{0}: (8, {}), {1}: (9, {}), {2}: (10, {}), {3}: (11, {})} | custom-call | tf_op jit(solution)/shard_map/strip_attention/pallas_call | solution.py:574
  39.2 10.7 %last_attention.1 = (bf16[8,16,1024]{2,1,0:T(8,128)(2,1)}, bf16[8,16,1024]{2,1,0:T(8,128)(2,1)}, bf16[16,1024]{1,0:T(8,128)(2,1)}) custom-call(f32[16]{0:T(128)} %scale.6, s32[8,64]{1,0:T(8,128)} %constant.29.clone.places, bf16[4,32,72]{2,1,0:T(8,128)(2,1)} %constant.27.clone.unpack, bf16[8,128]{1,0:T(8,128)(2,1)} %constant.28.clone.pool, ...), custom_call_target="tpu_custom_call" | custom-call | tf_op jit(solution)/shard_map/last_attention/pallas_call | solution.py:586
  49.9 4.4 %collective-permute-start.6 = (bf16[16,1024]{1,0:T(8,128)(2,1)}, bf16[16,1024]{1,0:T(8,128)(2,1)S(1)}, u32[]{:S(2)}, u32[]{:S(2)}) collective-permute-start(bf16[16,1024]{1,0:T(8,128)(2,1)} %get-tuple-element.55.refs_0_.coarse), channel_id=1, source_target_pairs={{0,1},{1,0},{2,3},{3,2},{4,5},{5,4},{6,7},{7,6},{8,9},{9,8},{10,11... | collective-permute-start | bytes 98312 | tf_op jit(solution)/shard_map/ppermute | solution.py:91
  54.4 2.4 %collective-permute-start.8 = (bf16[16,1024]{1,0:T(8,128)(2,1)}, bf16[16,1024]{1,0:T(8,128)(2,1)S(1)}, u32[]{:S(2)}, u32[]{:S(2)}) collective-permute-start(bf16[16,1024]{1,0:T(8,128)(2,1)} %get-tuple-element.55.refs_0_.coarse), channel_id=1, source_target_pairs={{0,3},{1,2},{2,1},{3,0},{4,7},{5,6},{6,5},{7,4},{8,11},{9,10},{10,... | collective-permute-start | bytes 98312 | tf_op jit(solution)/shard_map/ppermute | solution.py:91
  56.8 4.9 %fusion.mod = f32[2,4096]{1,0:T(2,128)} fusion(f32[256,4096]{1,0:T(8,128)} %param.30, f32[1,256]{1,0:T(1,128)S(1)} %stack_reshape.7, f32[1,256]{1,0:T(1,128)S(1)} %stack_reshape.6), kind=kOutput, calls=%fused_computation.2 | convolution fusion | flops 25166336 | bytes 4229120 | tf_op jit(solution)/shard_map/dot_general | solution.py:420
  61.9 1.6 %copy.32.weight = bf16[1024,768]{1,0:T(8,128)(2,1)} copy(bf16[1024,768]{0,1:T(8,128)(2,1)S(1)} %bitcast.10) | data formatting | bytes 3145728 | tf_op jit(solution)/shard_map/reshape | solution.py:605
  64.7 2.9 %project.1 = (bf16[32,512]{1,0:T(8,128)(2,1)}, bf16[32,1024]{1,0:T(8,128)(2,1)}) custom-call(f32[2,4096]{1,0:T(2,128)} %fusion.mod, bf16[1024,768]{1,0:T(8,128)(2,1)} %copy.32.weight, bf16[16,1024]{1,0:T(8,128)(2,1)} %get-tuple-element.55.refs_0_.coarse, bf16[16,1024]{1,0:T(8,128)(2,1)} %copy-done.19, bf16[16,1024]{1,0:T(8,128)(2,1)} %copy-done.22, ...), custom_call_target="tpu_custom_call" | custom-call | tf_op jit(solution)/shard_map/project/pallas_call | solution.py:441
  67.6 2.9 %collective-permute-start.10 = (bf16[32,1024]{1,0:T(8,128)(2,1)}, bf16[32,1024]{1,0:T(8,128)(2,1)S(1)}, u32[]{:S(2)}, u32[]{:S(2)}) collective-permute-start(bf16[32,1024]{1,0:T(8,128)(2,1)} %get-tuple-element.57.refs_0_), channel_id=1, source_target_pairs={{0,8},{4,12},{8,0},{12,4},{16,24},{20,28},{24,16},{28,20},{1,9},{5... | collective-permute-start | bytes 196616 | tf_op jit(solution)/shard_map/ppermute | solution.py:91
  71.2 1.2 collective-permute-start.12
  73.1 2.2 %collective-permute-start.14 = (bf16[32,1024]{1,0:T(8,128)(2,1)}, bf16[32,1024]{1,0:T(8,128)(2,1)S(1)}, u32[]{:S(2)}, u32[]{:S(2)}) collective-permute-start(bf16[32,1024]{1,0:T(8,128)(2,1)} %get-tuple-element.57.refs_0_), channel_id=1, source_target_pairs={{0,24},{4,28},{8,16},{12,20},{16,8},{20,12},{24,0},{28,4},{1,25},{... | collective-permute-start | bytes 196616 | tf_op jit(solution)/shard_map/ppermute | solution.py:91
  77.0 1.6 %collective-permute-done.14.refs_6_ = bf16[32,1024]{1,0:T(8,128)(2,1)S(1)} collective-permute-done((bf16[32,1024]{1,0:T(8,128)(2,1)}, bf16[32,1024]{1,0:T(8,128)(2,1)S(1)}, u32[]{:S(2)}, u32[]{:S(2)}) %collective-permute-start.14) | collective-permute-done | bytes 65568 | tf_op jit(solution)/shard_map/ppermute | solution.py:91
  78.6 1.8 %collective-permute-done.15.refs_7_ = bf16[32,1024]{1,0:T(8,128)(2,1)S(1)} collective-permute-done((bf16[32,1024]{1,0:T(8,128)(2,1)}, bf16[32,1024]{1,0:T(8,128)(2,1)S(1)}, u32[]{:S(2)}, u32[]{:S(2)}) %collective-permute-start.15) | collective-permute-done | bytes 65568 | tf_op jit(solution)/shard_map/ppermute | solution.py:91
  81.1 2.5 %coarse_attention.1 = (f32[16,1024]{1,0:T(8,128)}, bf16[16,1024]{1,0:T(8,128)(2,1)}, bf16[16,1024]{1,0:T(8,128)(2,1)}, bf16[16,1024]{1,0:T(8,128)(2,1)}) custom-call(f32[4]{0:T(128)} %scale.7, bf16[256,1024]{1,0:T(8,128)(2,1)} %bitcast.12, bf16[32,512]{1,0:T(8,128)(2,1)} %get-tuple-element.56.query, bf16[32,1024]{1,0:T(8,128)(2,1)} %get-tuple-element.57.refs_0_, ...), custom_call_target="tpu_custom_call" | custom-call | tf_op jit(solution)/shard_map/coarse_attention/pallas_call | solution.py:441
  84.6 1.3 %collective-permute-start.17 = (bf16[16,1024]{1,0:T(8,128)(2,1)}, bf16[16,1024]{1,0:T(8,128)(2,1)S(1)}, u32[]{:S(2)}, u32[]{:S(2)}) collective-permute-start(bf16[16,1024]{1,0:T(8,128)(2,1)} %get-tuple-element.60), channel_id=1, source_target_pairs={{0,2},{1,3},{2,0},{3,1},{4,6},{5,7},{6,4},{7,5},{8,10},{9,11},{10,... | collective-permute-start | bytes 98312 | tf_op jit(solution)/shard_map/ppermute | solution.py:98
  85.9 2.1 %collective-permute-start.18 = (bf16[16,1024]{1,0:T(8,128)(2,1)}, bf16[16,1024]{1,0:T(8,128)(2,1)S(1)}, u32[]{:S(2)}, u32[]{:S(2)}) collective-permute-start(bf16[16,1024]{1,0:T(8,128)(2,1)} %get-tuple-element.61), channel_id=1, source_target_pairs={{0,3},{1,2},{2,1},{3,0},{4,7},{5,6},{6,5},{7,4},{8,11},{9,10},{10,... | collective-permute-start | bytes 98312 | tf_op jit(solution)/shard_map/ppermute | solution.py:98
  88.0 1.7 %collective-permute-done.17.refs_2_ = bf16[16,1024]{1,0:T(8,128)(2,1)S(1)} collective-permute-done((bf16[16,1024]{1,0:T(8,128)(2,1)}, bf16[16,1024]{1,0:T(8,128)(2,1)S(1)}, u32[]{:S(2)}, u32[]{:S(2)}) %collective-permute-start.17) | collective-permute-done | bytes 32800 | tf_op jit(solution)/shard_map/ppermute | solution.py:98
  89.7 2.1 %collective-permute-done.18.refs_3_ = bf16[16,1024]{1,0:T(8,128)(2,1)S(1)} collective-permute-done((bf16[16,1024]{1,0:T(8,128)(2,1)}, bf16[16,1024]{1,0:T(8,128)(2,1)S(1)}, u32[]{:S(2)}, u32[]{:S(2)}) %collective-permute-start.18) | collective-permute-done | bytes 32800 | tf_op jit(solution)/shard_map/ppermute | solution.py:98
  92.4 1.7 %update.1 = (f32[16,1024]{1,0:T(8,128)}, bf16[16,1024]{1,0:T(8,128)(2,1)}) custom-call(f32[2,4096]{1,0:T(2,128)} %fusion.mod, bf16[16,1024]{1,0:T(8,128)(2,1)} %get-tuple-element.55.refs_0_.coarse, f32[16,1024]{1,0:T(8,128)} %get-tuple-element.58.refs_0_, bf16[16,1024]{1,0:T(8,128)(2,1)} %copy-done.17, bf16[16,1024]{1,0:T(8,128)(2,1)} %copy-done.20, ...), custom_call_target="tpu_custom_call" | custom-call | tf_op jit(solution)/shard_map/update/pallas_call | solution.py:441
  94.1 2.6 %collective-permute-start.20 = (bf16[16,1024]{1,0:T(8,128)(2,1)}, bf16[16,1024]{1,0:T(8,128)(2,1)S(1)}, u32[]{:S(2)}, u32[]{:S(2)}) collective-permute-start(bf16[16,1024]{1,0:T(8,128)(2,1)} %get-tuple-element.63.refs_0_), channel_id=1, source_target_pairs={{0,2},{1,3},{2,0},{3,1},{4,6},{5,7},{6,4},{7,5},{8,10},{9,11},{10,... | collective-permute-start | bytes 98312 | tf_op jit(solution)/shard_map/ppermute | solution.py:91
  96.8 1.7 %collective-permute-start.21 = (bf16[16,1024]{1,0:T(8,128)(2,1)}, bf16[16,1024]{1,0:T(8,128)(2,1)S(1)}, u32[]{:S(2)}, u32[]{:S(2)}) collective-permute-start(bf16[16,1024]{1,0:T(8,128)(2,1)} %get-tuple-element.63.refs_0_), channel_id=1, source_target_pairs={{0,3},{1,2},{2,1},{3,0},{4,7},{5,6},{6,5},{7,4},{8,11},{9,10},{10,... | collective-permute-start | bytes 98312 | tf_op jit(solution)/shard_map/ppermute | solution.py:91
  99.5 3.2 %collective-permute-done.21.refs_3_ = bf16[16,1024]{1,0:T(8,128)(2,1)S(1)} collective-permute-done((bf16[16,1024]{1,0:T(8,128)(2,1)}, bf16[16,1024]{1,0:T(8,128)(2,1)S(1)}, u32[]{:S(2)}, u32[]{:S(2)}) %collective-permute-start.21) | collective-permute-done | bytes 32800 | tf_op jit(solution)/shard_map/ppermute | solution.py:91
  103.3 4.9 %mlp.1 = (f32[16,1024]{1,0:T(8,128)}, bf16[16,1024]{1,0:T(8,128)(2,1)}, bf16[16,1024]{1,0:T(8,128)(2,1)}, bf16[16,1024]{1,0:T(8,128)(2,1)}) custom-call(bf16[1024,1024]{1,0:T(8,128)(2,1)} %up.1, bf16[1024,1024]{1,0:T(8,128)(2,1)} %down.1, bf16[16,1024]{1,0:T(8,128)(2,1)} %get-tuple-element.63.refs_0_, bf16[16,1024]{1,0:T(8,128)(2,1)} %copy-done.14, ...), custom_call_target="tpu_custom_call" | custom-call | tf_op jit(solution)/shard_map/mlp/pallas_call | solution.py:634
  108.2 2.3 %collective-permute-start.23 = (bf16[16,1024]{1,0:T(8,128)(2,1)}, bf16[16,1024]{1,0:T(8,128)(2,1)S(1)}, u32[]{:S(2)}, u32[]{:S(2)}) collective-permute-start(bf16[16,1024]{1,0:T(8,128)(2,1)} %get-tuple-element.66), channel_id=1, source_target_pairs={{0,2},{1,3},{2,0},{3,1},{4,6},{5,7},{6,4},{7,5},{8,10},{9,11},{10,... | collective-permute-start | bytes 98312 | tf_op jit(solution)/shard_map/ppermute | solution.py:98
  110.5 2.1 %collective-permute-start.24 = (bf16[16,1024]{1,0:T(8,128)(2,1)}, bf16[16,1024]{1,0:T(8,128)(2,1)S(1)}, u32[]{:S(2)}, u32[]{:S(2)}) collective-permute-start(bf16[16,1024]{1,0:T(8,128)(2,1)} %get-tuple-element.67), channel_id=1, source_target_pairs={{0,3},{1,2},{2,1},{3,0},{4,7},{5,6},{6,5},{7,4},{8,11},{9,10},{10,... | collective-permute-start | bytes 98312 | tf_op jit(solution)/shard_map/ppermute | solution.py:98
  113.3 3.1 %collective-permute-done.24.refs_3_ = bf16[16,1024]{1,0:T(8,128)(2,1)S(1)} collective-permute-done((bf16[16,1024]{1,0:T(8,128)(2,1)}, bf16[16,1024]{1,0:T(8,128)(2,1)S(1)}, u32[]{:S(2)}, u32[]{:S(2)}) %collective-permute-start.24) | collective-permute-done | bytes 32800 | tf_op jit(solution)/shard_map/ppermute | solution.py:98
  117.1 1.5 %final.1 = (bf16[2,4,1024]{2,1,0:T(4,128)(2,1)}, bf16[2,4,1024]{2,1,0:T(4,128)(2,1)}) custom-call(f32[16,1024]{1,0:T(8,128)} %get-tuple-element.62.updated, f32[16,1024]{1,0:T(8,128)} %get-tuple-element.64.refs_0_, bf16[16,1024]{1,0:T(8,128)(2,1)} %copy-done.18, bf16[16,1024]{1,0:T(8,128)(2,1)} %copy-done.21, bf16[16,1024]{1,0:T(8,128)(2,1)} %copy-done.24), custom_call_target="tpu_custom_call" | custom-call | tf_op jit(solution)/shard_map/final/pallas_call | solution.py:441
  (92 shorter events, 16.3 us)
Async XLA Ops:
  4.2 9.6 %collective-permute-start = (bf16[128,1024]{1,0:T(8,128)(2,1)}, bf16[128,1024]{1,0:T(8,128)(2,1)S(1)}, u32[]{:S(2)}, u32[]{:S(2)}) collective-permute-start(bf16[128,1024]{1,0:T(8,128)(2,1)} %get-tuple-element.39), channel_id=1, source_target_pairs={{0,1},{1,0},{2,3},{3,2},{4,5},{5,4},{6,7},{7,6},{8,9},{9,8},{10,11... | collective-permute-start | bytes 786440 | tf_op jit(solution)/shard_map/ppermute | solution.py:543
  7.3 6.5 %collective-permute-start.1 = (bf16[128,1024]{1,0:T(8,128)(2,1)}, bf16[128,1024]{1,0:T(8,128)(2,1)S(1)}, u32[]{:S(2)}, u32[]{:S(2)}) collective-permute-start(bf16[128,1024]{1,0:T(8,128)(2,1)} %get-tuple-element.40), channel_id=1, source_target_pairs={{1,2},{2,1},{5,6},{6,5},{9,10},{10,9},{13,14},{14,13},{17,18},{18,... | collective-permute-start | bytes 786440 | tf_op jit(solution)/shard_map/ppermute | solution.py:543
  8.0 20.7 %collective-permute-start.4 = (bf16[192,1024]{1,0:T(8,128)(2,1)}, bf16[192,1024]{1,0:T(8,128)(2,1)S(1)}, u32[]{:S(2)}, u32[]{:S(2)}) collective-permute-start(bf16[192,1024]{1,0:T(8,128)(2,1)} %get-tuple-element.43), channel_id=1, source_target_pairs={{0,4},{4,0},{8,12},{12,8},{16,20},{20,16},{24,28},{28,24},{1,5},{5... | collective-permute-start | bytes 1179656 | tf_op jit(solution)/shard_map/ppermute | solution.py:540
  8.1 20.6 %collective-permute-start.5 = (bf16[192,1024]{1,0:T(8,128)(2,1)}, bf16[192,1024]{1,0:T(8,128)(2,1)S(1)}, u32[]{:S(2)}, u32[]{:S(2)}) collective-permute-start(bf16[192,1024]{1,0:T(8,128)(2,1)} %get-tuple-element.44), channel_id=1, source_target_pairs={{4,8},{8,4},{12,16},{16,12},{20,24},{24,20},{5,9},{9,5},{13,17},{1... | collective-permute-start | bytes 1179656 | tf_op jit(solution)/shard_map/ppermute | solution.py:540
  18.7 19.7 %collective-permute-start.2 = (bf16[72,1024]{1,0:T(8,128)(2,1)}, bf16[72,1024]{1,0:T(8,128)(2,1)S(1)}, u32[]{:S(2)}, u32[]{:S(2)}) collective-permute-start(bf16[72,1024]{1,0:T(8,128)(2,1)} %get-tuple-element.41), channel_id=1, source_target_pairs={{0,4},{4,0},{8,12},{12,8},{16,20},{20,16},{24,28},{28,24},{1,5},{5... | collective-permute-start | bytes 442376 | tf_op jit(solution)/shard_map/ppermute | solution.py:571
  19.8 18.6 %collective-permute-start.3 = (bf16[72,1024]{1,0:T(8,128)(2,1)}, bf16[72,1024]{1,0:T(8,128)(2,1)S(1)}, u32[]{:S(2)}, u32[]{:S(2)}) collective-permute-start(bf16[72,1024]{1,0:T(8,128)(2,1)} %get-tuple-element.42), channel_id=1, source_target_pairs={{4,8},{8,4},{12,16},{16,12},{20,24},{24,20},{5,9},{9,5},{13,17},{1... | collective-permute-start | bytes 442376 | tf_op jit(solution)/shard_map/ppermute | solution.py:571
  49.9 11.8 %copy-start = (bf16[1024,4,192]{0,2,1:T(8,128)(2,1)S(1)}, bf16[1024,4,192]{0,2,1:T(8,128)(2,1)}, u32[]{:S(2)}) copy-start(bf16[1024,4,192]{0,2,1:T(8,128)(2,1)} %param.31) | copy-start | bytes 4718596
  49.9 13.5 %collective-permute-start.6 = (bf16[16,1024]{1,0:T(8,128)(2,1)}, bf16[16,1024]{1,0:T(8,128)(2,1)S(1)}, u32[]{:S(2)}, u32[]{:S(2)}) collective-permute-start(bf16[16,1024]{1,0:T(8,128)(2,1)} %get-tuple-element.55.refs_0_.coarse), channel_id=1, source_target_pairs={{0,1},{1,0},{2,3},{3,2},{4,5},{5,4},{6,7},{7,6},{8,9},{9,8},{10,11... | collective-permute-start | bytes 98312 | tf_op jit(solution)/shard_map/ppermute | solution.py:91
  54.4 9.1 %collective-permute-start.7 = (bf16[16,1024]{1,0:T(8,128)(2,1)}, bf16[16,1024]{1,0:T(8,128)(2,1)S(1)}, u32[]{:S(2)}, u32[]{:S(2)}) collective-permute-start(bf16[16,1024]{1,0:T(8,128)(2,1)} %get-tuple-element.55.refs_0_.coarse), channel_id=1, source_target_pairs={{0,2},{1,3},{2,0},{3,1},{4,6},{5,7},{6,4},{7,5},{8,10},{9,11},{10,... | collective-permute-start | bytes 98312 | tf_op jit(solution)/shard_map/ppermute | solution.py:91
  54.4 9.1 %collective-permute-start.8 = (bf16[16,1024]{1,0:T(8,128)(2,1)}, bf16[16,1024]{1,0:T(8,128)(2,1)S(1)}, u32[]{:S(2)}, u32[]{:S(2)}) collective-permute-start(bf16[16,1024]{1,0:T(8,128)(2,1)} %get-tuple-element.55.refs_0_.coarse), channel_id=1, source_target_pairs={{0,3},{1,2},{2,1},{3,0},{4,7},{5,6},{6,5},{7,4},{8,11},{9,10},{10,... | collective-permute-start | bytes 98312 | tf_op jit(solution)/shard_map/ppermute | solution.py:91
  67.6 7.7 %collective-permute-start.10 = (bf16[32,1024]{1,0:T(8,128)(2,1)}, bf16[32,1024]{1,0:T(8,128)(2,1)S(1)}, u32[]{:S(2)}, u32[]{:S(2)}) collective-permute-start(bf16[32,1024]{1,0:T(8,128)(2,1)} %get-tuple-element.57.refs_0_), channel_id=1, source_target_pairs={{0,8},{4,12},{8,0},{12,4},{16,24},{20,28},{24,16},{28,20},{1,9},{5... | collective-permute-start | bytes 196616 | tf_op jit(solution)/shard_map/ppermute | solution.py:91
  70.4 5.2 %collective-permute-start.11 = (bf16[32,1024]{1,0:T(8,128)(2,1)}, bf16[32,1024]{1,0:T(8,128)(2,1)S(1)}, u32[]{:S(2)}, u32[]{:S(2)}) collective-permute-start(bf16[32,1024]{1,0:T(8,128)(2,1)} %get-tuple-element.57.refs_0_), channel_id=1, source_target_pairs={{0,12},{4,8},{8,4},{12,0},{16,28},{20,24},{24,20},{28,16},{1,13},{... | collective-permute-start | bytes 196616 | tf_op jit(solution)/shard_map/ppermute | solution.py:91
  71.2 5.5 %collective-permute-start.12 = (bf16[32,1024]{1,0:T(8,128)(2,1)}, bf16[32,1024]{1,0:T(8,128)(2,1)S(1)}, u32[]{:S(2)}, u32[]{:S(2)}) collective-permute-start(bf16[32,1024]{1,0:T(8,128)(2,1)} %get-tuple-element.57.refs_0_), channel_id=1, source_target_pairs={{0,16},{4,20},{8,24},{12,28},{16,0},{20,4},{24,8},{28,12},{1,17},{... | collective-permute-start | bytes 196616 | tf_op jit(solution)/shard_map/ppermute | solution.py:91
  72.4 4.6 %collective-permute-start.13 = (bf16[32,1024]{1,0:T(8,128)(2,1)}, bf16[32,1024]{1,0:T(8,128)(2,1)S(1)}, u32[]{:S(2)}, u32[]{:S(2)}) collective-permute-start(bf16[32,1024]{1,0:T(8,128)(2,1)} %get-tuple-element.57.refs_0_), channel_id=1, source_target_pairs={{0,20},{4,16},{8,28},{12,24},{16,4},{20,0},{24,12},{28,8},{1,21},{... | collective-permute-start | bytes 196616 | tf_op jit(solution)/shard_map/ppermute | solution.py:91
  73.1 5.4 %collective-permute-start.14 = (bf16[32,1024]{1,0:T(8,128)(2,1)}, bf16[32,1024]{1,0:T(8,128)(2,1)S(1)}, u32[]{:S(2)}, u32[]{:S(2)}) collective-permute-start(bf16[32,1024]{1,0:T(8,128)(2,1)} %get-tuple-element.57.refs_0_), channel_id=1, source_target_pairs={{0,24},{4,28},{8,16},{12,20},{16,8},{20,12},{24,0},{28,4},{1,25},{... | collective-permute-start | bytes 196616 | tf_op jit(solution)/shard_map/ppermute | solution.py:91
  75.3 5.1 %copy-start.7 = (bf16[32,1024]{1,0:T(8,128)(2,1)}, bf16[32,1024]{1,0:T(8,128)(2,1)S(1)}, u32[]{:S(2)}) copy-start(bf16[32,1024]{1,0:T(8,128)(2,1)S(1)} %collective-permute-done.10.refs_2_) | copy-start | bytes 196612
  75.3 5.1 %collective-permute-start.15 = (bf16[32,1024]{1,0:T(8,128)(2,1)}, bf16[32,1024]{1,0:T(8,128)(2,1)S(1)}, u32[]{:S(2)}, u32[]{:S(2)}) collective-permute-start(bf16[32,1024]{1,0:T(8,128)(2,1)} %get-tuple-element.57.refs_0_), channel_id=1, source_target_pairs={{0,28},{4,24},{8,20},{12,16},{16,12},{20,8},{24,4},{28,0},{1,29},{... | collective-permute-start | bytes 196616 | tf_op jit(solution)/shard_map/ppermute | solution.py:91
  75.6 4.8 %copy-start.8 = (bf16[32,1024]{1,0:T(8,128)(2,1)}, bf16[32,1024]{1,0:T(8,128)(2,1)S(1)}, u32[]{:S(2)}) copy-start(bf16[32,1024]{1,0:T(8,128)(2,1)S(1)} %collective-permute-done.11.refs_3_) | copy-start | bytes 196612
  75.6 4.8 %collective-permute-start.9 = (bf16[32,1024]{1,0:T(8,128)(2,1)}, bf16[32,1024]{1,0:T(8,128)(2,1)S(1)}, u32[]{:S(2)}, u32[]{:S(2)}) collective-permute-start(bf16[32,1024]{1,0:T(8,128)(2,1)} %get-tuple-element.57.refs_0_), channel_id=1, source_target_pairs={{0,4},{4,0},{8,12},{12,8},{16,20},{20,16},{24,28},{28,24},{1,5},{5... | collective-permute-start | bytes 196616 | tf_op jit(solution)/shard_map/ppermute | solution.py:91
  76.7 3.7 %copy-start.9 = (bf16[32,1024]{1,0:T(8,128)(2,1)}, bf16[32,1024]{1,0:T(8,128)(2,1)S(1)}, u32[]{:S(2)}) copy-start(bf16[32,1024]{1,0:T(8,128)(2,1)S(1)} %collective-permute-done.12.refs_4_) | copy-start | bytes 196612
  83.6 4.4 %collective-permute-start.16 = (bf16[16,1024]{1,0:T(8,128)(2,1)}, bf16[16,1024]{1,0:T(8,128)(2,1)S(1)}, u32[]{:S(2)}, u32[]{:S(2)}) collective-permute-start(bf16[16,1024]{1,0:T(8,128)(2,1)} %get-tuple-element.59), channel_id=1, source_target_pairs={{0,1},{1,0},{2,3},{3,2},{4,5},{5,4},{6,7},{7,6},{8,9},{9,8},{10,11... | collective-permute-start | bytes 98312 | tf_op jit(solution)/shard_map/ppermute | solution.py:98
  84.6 5.0 %collective-permute-start.17 = (bf16[16,1024]{1,0:T(8,128)(2,1)}, bf16[16,1024]{1,0:T(8,128)(2,1)S(1)}, u32[]{:S(2)}, u32[]{:S(2)}) collective-permute-start(bf16[16,1024]{1,0:T(8,128)(2,1)} %get-tuple-element.60), channel_id=1, source_target_pairs={{0,2},{1,3},{2,0},{3,1},{4,6},{5,7},{6,4},{7,5},{8,10},{9,11},{10,... | collective-permute-start | bytes 98312 | tf_op jit(solution)/shard_map/ppermute | solution.py:98
  85.9 5.9 %collective-permute-start.18 = (bf16[16,1024]{1,0:T(8,128)(2,1)}, bf16[16,1024]{1,0:T(8,128)(2,1)S(1)}, u32[]{:S(2)}, u32[]{:S(2)}) collective-permute-start(bf16[16,1024]{1,0:T(8,128)(2,1)} %get-tuple-element.61), channel_id=1, source_target_pairs={{0,3},{1,2},{2,1},{3,0},{4,7},{5,6},{6,5},{7,4},{8,11},{9,10},{10,... | collective-permute-start | bytes 98312 | tf_op jit(solution)/shard_map/ppermute | solution.py:98
  88.0 3.8 %copy-start.17 = (bf16[16,1024]{1,0:T(8,128)(2,1)}, bf16[16,1024]{1,0:T(8,128)(2,1)S(1)}, u32[]{:S(2)}) copy-start(bf16[16,1024]{1,0:T(8,128)(2,1)S(1)} %collective-permute-done.16.refs_1_) | copy-start | bytes 98308
  94.1 4.4 %collective-permute-start.19 = (bf16[16,1024]{1,0:T(8,128)(2,1)}, bf16[16,1024]{1,0:T(8,128)(2,1)S(1)}, u32[]{:S(2)}, u32[]{:S(2)}) collective-permute-start(bf16[16,1024]{1,0:T(8,128)(2,1)} %get-tuple-element.63.refs_0_), channel_id=1, source_target_pairs={{0,1},{1,0},{2,3},{3,2},{4,5},{5,4},{6,7},{7,6},{8,9},{9,8},{10,11... | collective-permute-start | bytes 98312 | tf_op jit(solution)/shard_map/ppermute | solution.py:91
  94.1 5.4 %collective-permute-start.20 = (bf16[16,1024]{1,0:T(8,128)(2,1)}, bf16[16,1024]{1,0:T(8,128)(2,1)S(1)}, u32[]{:S(2)}, u32[]{:S(2)}) collective-permute-start(bf16[16,1024]{1,0:T(8,128)(2,1)} %get-tuple-element.63.refs_0_), channel_id=1, source_target_pairs={{0,2},{1,3},{2,0},{3,1},{4,6},{5,7},{6,4},{7,5},{8,10},{9,11},{10,... | collective-permute-start | bytes 98312 | tf_op jit(solution)/shard_map/ppermute | solution.py:91
  96.8 5.9 %collective-permute-start.21 = (bf16[16,1024]{1,0:T(8,128)(2,1)}, bf16[16,1024]{1,0:T(8,128)(2,1)S(1)}, u32[]{:S(2)}, u32[]{:S(2)}) collective-permute-start(bf16[16,1024]{1,0:T(8,128)(2,1)} %get-tuple-element.63.refs_0_), channel_id=1, source_target_pairs={{0,3},{1,2},{2,1},{3,0},{4,7},{5,6},{6,5},{7,4},{8,11},{9,10},{10,... | collective-permute-start | bytes 98312 | tf_op jit(solution)/shard_map/ppermute | solution.py:91
  98.5 4.2 %copy-start.14 = (bf16[16,1024]{1,0:T(8,128)(2,1)}, bf16[16,1024]{1,0:T(8,128)(2,1)S(1)}, u32[]{:S(2)}) copy-start(bf16[16,1024]{1,0:T(8,128)(2,1)S(1)} %collective-permute-done.19.refs_1_) | copy-start | bytes 98308
  108.2 4.4 %collective-permute-start.22 = (bf16[16,1024]{1,0:T(8,128)(2,1)}, bf16[16,1024]{1,0:T(8,128)(2,1)S(1)}, u32[]{:S(2)}, u32[]{:S(2)}) collective-permute-start(bf16[16,1024]{1,0:T(8,128)(2,1)} %get-tuple-element.65), channel_id=1, source_target_pairs={{0,1},{1,0},{2,3},{3,2},{4,5},{5,4},{6,7},{7,6},{8,9},{9,8},{10,11... | collective-permute-start | bytes 98312 | tf_op jit(solution)/shard_map/ppermute | solution.py:98
  108.2 5.1 %collective-permute-start.23 = (bf16[16,1024]{1,0:T(8,128)(2,1)}, bf16[16,1024]{1,0:T(8,128)(2,1)S(1)}, u32[]{:S(2)}, u32[]{:S(2)}) collective-permute-start(bf16[16,1024]{1,0:T(8,128)(2,1)} %get-tuple-element.66), channel_id=1, source_target_pairs={{0,2},{1,3},{2,0},{3,1},{4,6},{5,7},{6,4},{7,5},{8,10},{9,11},{10,... | collective-permute-start | bytes 98312 | tf_op jit(solution)/shard_map/ppermute | solution.py:98
  110.5 5.9 %collective-permute-start.24 = (bf16[16,1024]{1,0:T(8,128)(2,1)}, bf16[16,1024]{1,0:T(8,128)(2,1)S(1)}, u32[]{:S(2)}, u32[]{:S(2)}) collective-permute-start(bf16[16,1024]{1,0:T(8,128)(2,1)} %get-tuple-element.67), channel_id=1, source_target_pairs={{0,3},{1,2},{2,1},{3,0},{4,7},{5,6},{6,5},{7,4},{8,11},{9,10},{10,... | collective-permute-start | bytes 98312 | tf_op jit(solution)/shard_map/ppermute | solution.py:98
  112.6 3.8 %copy-start.18 = (bf16[16,1024]{1,0:T(8,128)(2,1)}, bf16[16,1024]{1,0:T(8,128)(2,1)S(1)}, u32[]{:S(2)}) copy-start(bf16[16,1024]{1,0:T(8,128)(2,1)S(1)} %collective-permute-done.22.refs_1_) | copy-start | bytes 98308
  (19 other events, 23.2 us)

commit v2 on v1

v2 whole, which is shorter than its diff:
```python
import functools
import math

import jax
import jax.numpy as jnp
from jax import lax
from jax.experimental import pallas as pl
from jax.experimental.pallas import tpu as pltpu
from jax.sharding import PartitionSpec as P

EMBED = 128
RADIUS = 3
MERGE = 4
STEPS = 1000
EPSILON = 1e-06
LANES = 128
TOGETHER = 4
LOG2E = math.log2(math.e)
F32 = jnp.float32
BF16 = jnp.bfloat16


def dot(a, b):
    return jnp.dot(a, b, preferred_element_type=F32)


def dot_nt(a, b):
    return lax.dot_general(a, b, (((1,), (1,)), ((), ())), preferred_element_type=F32)


def block_ones(width, head, value):
    row = lax.broadcasted_iota(jnp.int32, (width, width), 0)
    col = lax.broadcasted_iota(jnp.int32, (width, width), 1)
    same = lax.shift_right_logical(row, head) == lax.shift_right_logical(col, head)
    return jnp.where(same, value, 0.0).astype(BF16)


def head_means(arrays, ones):
    highs = [array.astype(BF16) for array in arrays]
    lows = [(a - h.astype(F32)).astype(BF16) for a, h in zip(arrays, highs)]
    means = dot(jnp.concatenate(highs, 0), ones) + dot(jnp.concatenate(lows, 0), ones)
    pieces, at = [], 0
    for array in arrays:
        pieces.append(means[at : at + array.shape[0]])
        at += array.shape[0]
    return pieces


def head_pairs(couples_of, ones):
    factors = [
        lax.rsqrt(mean + EPSILON)
        for mean in head_means([values * values for values, _ in couples_of], ones)
    ]
    normed = [values * factor for (values, _), factor in zip(couples_of, factors)]
    leans = head_means([n * tangent for n, (_, tangent) in zip(normed, couples_of)], ones)
    return [
        (n.astype(BF16), ((tangent - n * lean) * factor).astype(BF16))
        for n, (_, tangent), lean, factor in zip(normed, couples_of, leans, factors)
    ]


def row_pair(values, tangent):
    factor = lax.rsqrt(jnp.mean(values * values, axis=-1, keepdims=True) + EPSILON)
    normed = values * factor
    drift = (tangent - normed * jnp.mean(normed * tangent, axis=-1, keepdims=True)) * factor
    return normed, drift


def conditioned(values, tangent, mod, part, width):
    normed, drift = row_pair(values, tangent)
    offset = mod[0:1, 2 * part * width : (2 * part + 1) * width]
    stretch = mod[0:1, (2 * part + 1) * width : (2 * part + 2) * width]
    offset_drift = mod[1:2, 2 * part * width : (2 * part + 1) * width]
    stretch_drift = mod[1:2, (2 * part + 1) * width : (2 * part + 2) * width]
    primal = (normed * (1.0 + stretch) + offset).astype(BF16)
    moving = (drift * (1.0 + stretch) + normed * stretch_drift + offset_drift).astype(BF16)
    return primal, moving


def side(axis, phase):
    at = lax.axis_index(axis)
    after = (at & 1) == phase
    exists = jnp.where(after, at + 1 < lax.axis_size(axis), at > 0)
    return after, exists


def couples(count, phase):
    return [
        edge for i in range(phase, count - 1, 2) for edge in ((i, i + 1), (i + 1, i))
    ]


def partner(count, step, back=False):
    if count & (count - 1) == 0:
        return [(i, i ^ step) for i in range(count)]
    return [(i, (i - step if back else i + step) % count) for i in range(count)]


def gathered(value, axis):
    count = lax.axis_size(axis)
    return [value] + [
        lax.ppermute(value, axis, partner(count, step)) for step in range(1, count)
    ]


def row_gathered(value, axis):
    count = lax.axis_size(axis)
    if count < 4 or count & (count - 1):
        return gathered(value, axis)
    part = jnp.concatenate(
        [value] + [lax.ppermute(value, axis, partner(count, step)) for step in range(2, count, 2)],
        0,
    )
    return [part, lax.ppermute(part, axis, partner(count, 1))]


def returned(pieces, axis):
    count = lax.axis_size(axis)
    return [
        lax.ppermute(piece, axis, partner(count, step, True))
        for step, piece in zip(range(1, count), pieces)
    ]


def attend(items, mask, head):
    count, keys = mask.shape
    lane = lax.broadcasted_iota(jnp.int32, (1, LANES), 1)
    first = (lane < head).astype(F32).astype(BF16)
    second = (lane >= head).astype(F32).astype(BF16)
    scores, slopes = [], []
    for query, query_drift, key, key_drift, _, _, _ in items:
        query_0, query_1 = query * first, query * second
        drift_0, drift_1 = query_drift * first, query_drift * second
        scores.append(dot_nt(jnp.concatenate([query_0, query_1], 0), key))
        slopes.append(
            dot_nt(
                jnp.concatenate(
                    [
                        jnp.concatenate([drift_0, query_0], 1),
                        jnp.concatenate([drift_1, query_1], 1),
                    ],
                    0,
                ),
                jnp.concatenate([key, key_drift], 1),
            )
        )
    weights, tilts = [], []
    for score, slope, item in zip(scores, slopes, items):
        heavy, tilted = [], []
        for place, factor in enumerate(item[6]):
            rows = slice(place * count, (place + 1) * count)
            weight = jnp.exp2(score[rows] * (factor * LOG2E)) * mask
            heavy.append(weight.astype(BF16))
            tilted.append((weight * (slope[rows] * factor)).astype(BF16))
        weights.append(jnp.concatenate(heavy, 0))
        tilts.append(jnp.concatenate(tilted, 0))
    ones = jnp.ones((keys, LANES), BF16)

    def own(stack):
        return jnp.where(lane < head, stack[:count], stack[count:])

    results = []
    for weight, tilt, item in zip(weights, tilts, items):
        value, value_drift = item[4], item[5]
        mixed = dot(weight, jnp.concatenate([value, value_drift], 1))
        turned = dot(tilt, value)
        sums = dot(jnp.concatenate([weight, tilt], 0), ones)
        results.append(
            (
                own(mixed[:, :LANES]),
                own(mixed[:, LANES:] + turned),
                own(sums[: 2 * count]),
                own(sums[2 * count :]),
            )
        )
    return results


def near(key_row, key_column, columns, count):
    place = lax.broadcasted_iota(jnp.int32, (count, 1), 0)
    shift = columns.bit_length() - 1
    row = lax.shift_right_logical(place, shift)
    column = place & (columns - 1)
    close = (jnp.abs(row - key_row) <= RADIUS) & (jnp.abs(column - key_column) <= RADIUS)
    return jnp.where(close, 1.0, 0.0)


def one_hot(rows, place, valid):
    row = lax.broadcasted_iota(jnp.int32, (rows, place.shape[1]), 0)
    return jnp.where((row == place) & valid, 1.0, 0.0).astype(BF16)


def log2(number):
    return number.bit_length() - 1


def by_radius(number):
    return lax.shift_right_logical(number * (128 // RADIUS + 1), 7)


def pack_kernel(key, value, key_drift, value_drift, query, query_drift, *refs):
    y0, y1, z0, z1, sems = *refs[:4], refs[-1]
    near = refs[4:10]
    far = (key, value, key_drift, value_drift, query, query_drift)
    copies = [
        pltpu.make_async_copy(source, target, sems.at[i])
        for i, (source, target) in enumerate(zip(far, near))
    ]
    for copy in copies:
        copy.start()
    rows, columns, width = key.shape
    count = rows * columns
    strip = RADIUS * columns
    band = z0.shape[0] // 4
    place = lax.broadcasted_iota(jnp.int32, (1, count), 1)
    row = lax.shift_right_logical(place, log2(columns))
    picks, starts = [], []
    for phase in range(2):
        right, _ = side("tx", phase)
        column = (place & (columns - 1)) - jnp.where(right, columns - RADIUS, 0)
        valid = (column >= 0) & (column < RADIUS)
        picks.append(one_hot(band, row * RADIUS + column, valid))
        down, _ = side("ty", phase)
        starts.append(jnp.where(down, rows - RADIUS, 0))
    for array, ref in enumerate(near[:4]):
        copies[array].wait()
        flat = ref[...].reshape(count, width)
        for start, pick, y, z in zip(starts, picks, (y0, y1), (z0, z1)):
            y[array * strip : (array + 1) * strip] = ref[pl.ds(start, RADIUS)].reshape(
                strip, width
            )
            z[array * band : (array + 1) * band] = dot(pick, flat).astype(BF16)
    for copy in copies[4:]:
        copy.wait()


def corner_kernel(rows, z0, z1, c0, c1):
    half = z0.shape[0]
    band = half // 4
    square = RADIUS * RADIUS
    place = lax.broadcasted_iota(jnp.int32, (1, half), 1)
    array = lax.shift_right_logical(place, log2(band))
    for phase, c in enumerate((c0, c1)):
        down, _ = side("ty", phase)
        token = (place & (band - 1)) - jnp.where(down, (rows - RADIUS) * RADIUS, 0)
        valid = (token >= 0) & (token < square)
        total = None
        for meet, z in enumerate((z0, z1)):
            at = (2 * array + meet) * square + token
            part = dot(one_hot(c.shape[0], at, valid), z[...])
            total = part if total is None else total + part
        c[...] = total.astype(BF16)


def each_group(pairs, body):
    together = math.gcd(pairs, TOGETHER)

    @pl.loop(0, pairs // together)
    def _(step):
        starts = [
            pl.multiple_of((step * together + i) * LANES, LANES) for i in range(together)
        ]
        body(step * together, [pl.ds(start, LANES) for start in starts])


def own_kernel(head, scale, q, qd, k, kd, v, vd, qn, qdn, *sums):
    rows, columns, width = q.shape
    count = rows * columns
    ones = block_ones(LANES, head.bit_length() - 1, 1.0 / head)
    place = lax.broadcasted_iota(jnp.int32, (1, count), 1)
    shift = columns.bit_length() - 1
    mask = near(lax.shift_right_logical(place, shift), place & (columns - 1), columns, count)

    def body(pair, lanes):
        def flat(ref, at):
            return ref[:, :, at].reshape(count, LANES)

        normed = head_pairs(
            [
                (flat(a, at).astype(F32), flat(b, at).astype(F32))
                for at in lanes
                for a, b in ((q, qd), (k, kd))
            ],
            ones,
        )
        items = []
        for i, at in enumerate(lanes):
            query, key = normed[2 * i], normed[2 * i + 1]
            qn[:, at], qdn[:, at] = query
            factors = [scale[2 * (pair + i) + j] / head for j in range(2)]
            items.append((*query, *key, flat(v, at), flat(vd, at), factors))
        for at, parts in zip(lanes, attend(items, mask, head)):
            for ref, part in zip(sums, parts):
                ref[:, at] = part

    each_group(width // LANES, body)


def moved(row, column, phase_down, phase_right, tile):
    rows, columns = tile
    outside = 4 * (rows + columns)
    for phase in range(2):
        down, below = side("ty", phase)
        right, beside = side("tx", phase)
        row_move = jnp.where(below, jnp.where(down, rows, -RADIUS), outside)
        column_move = jnp.where(beside, jnp.where(right, columns, -RADIUS), outside)
        row = row + jnp.where(phase_down == phase, row_move, 0)
        column = column + jnp.where(phase_right == phase, column_move, 0)
    return row, column


def strip_places(tile, band):
    rows, columns = tile
    strip = RADIUS * columns
    place = lax.broadcasted_iota(jnp.int32, (1, 2 * band + 2 * strip), 1)
    beside = place < 2 * band
    phase = lax.shift_right_logical(place, log2(band))
    token = place & (band - 1)
    side_row = by_radius(token)
    side_column = token - side_row * RADIUS
    side_row = jnp.where(side_row < rows, side_row, 8 * (rows + columns))
    rest = place - 2 * band
    later = rest >= strip
    rest = rest - jnp.where(later, strip, 0)
    row = jnp.where(beside, side_row, lax.shift_right_logical(rest, log2(columns)))
    column = jnp.where(beside, side_column, rest & (columns - 1))
    down = jnp.where(beside, -1, jnp.where(later, 1, 0))
    return moved(row, column, down, jnp.where(beside, phase, -1), tile)


def corner_places(tile, band):
    square = RADIUS * RADIUS
    place = lax.broadcasted_iota(jnp.int32, (1, 2 * band), 1)
    slot = place & (band - 1)
    later = slot >= square
    token = slot - jnp.where(later, square, 0)
    row = by_radius(token)
    column = token - row * RADIUS
    row = jnp.where(slot < 2 * square, row, 8 * sum(tile))
    down = lax.shift_right_logical(place, log2(band))
    return moved(row, column, down, jnp.where(later, 1, 0), tile)


def strip_kernel(head, tile, scale, qn, qdn, z0, z1, y0, y1, *sums):
    ones = block_ones(LANES, head.bit_length() - 1, 1.0 / head)
    messages = (z0, z1, y0, y1)
    row, column = strip_places(tile, z0.shape[0] // 4)
    mask = near(row, column, tile[1], qn.shape[0])

    def body(pair, lanes):
        def part(array, at):
            pieces = []
            for ref in messages:
                size = ref.shape[0] // 4
                pieces.append(ref[array * size : (array + 1) * size, at])
            return jnp.concatenate(pieces, 0)

        keys = head_pairs(
            [(part(0, at).astype(F32), part(2, at).astype(F32)) for at in lanes], ones
        )
        items = [
            (
                qn[:, at], qdn[:, at], *key, part(1, at), part(3, at),
                [scale[2 * (pair + i) + j] / head for j in range(2)],
            )
            for i, (at, key) in enumerate(zip(lanes, keys))
        ]
        for at, parts in zip(lanes, attend(items, mask, head)):
            for before, after, piece in zip(sums[:4], sums[4:], parts):
                after[:, at] = before[:, at] + piece

    each_group(qn.shape[1] // LANES, body)


def last_kernel(
    head, tile, scale, qn, qdn, c0, c1, a, ce, l, b, weight, out, tangent, coarse, pooled
):
    rows, columns = tile
    count = rows * columns
    ones = block_ones(LANES, log2(head), 1.0 / head)
    corner_rows = c0.shape[0]
    corner_keys = corner_rows // 4
    band = -(-corner_keys // 32) * 32
    row, column = corner_places(tile, band)
    mask = near(row, column, columns, count)
    place = lax.broadcasted_iota(jnp.int32, (1, corner_rows), 1)
    unpack = []
    for array in range(4):
        slot = place - array * corner_keys
        unpack.append(one_hot(band, slot, (slot >= 0) & (slot < corner_keys)))
    own = pooled.shape[0] // 2
    place = lax.broadcasted_iota(jnp.int32, (1, count), 1)
    block = lax.shift_right_logical(place, log2(columns) + log2(MERGE)) * (columns // MERGE)
    block = block + lax.shift_right_logical(place & (columns - 1), log2(MERGE))
    pool = one_hot(own, block, block >= 0) * jnp.asarray(1 / (MERGE * MERGE), BF16)

    def body(pair, lanes):
        def part(array, at):
            return jnp.concatenate([dot(unpack[array], c[:, at]) for c in (c0, c1)], 0)

        keys = head_pairs([(part(0, at), part(2, at)) for at in lanes], ones)
        items = [
            (
                qn[:, at], qdn[:, at], *key, part(1, at).astype(BF16),
                part(3, at).astype(BF16),
                [scale[2 * (pair + i) + j] / head for j in range(2)],
            )
            for i, (at, key) in enumerate(zip(lanes, keys))
        ]
        for at, parts in zip(lanes, attend(items, mask, head)):
            inverse = 1.0 / (l[:, at] + parts[2])
            output = (a[:, at] + parts[0]) * inverse
            moving = (ce[:, at] + parts[1]) * inverse - output * ((b[:, at] + parts[3]) * inverse)
            output = output.astype(BF16)
            moving = moving.astype(BF16)
            out[:, :, at] = output.reshape(*tile, LANES)
            tangent[:, :, at] = moving.reshape(*tile, LANES)
            pooled[:own, at] = dot(pool, output)
            pooled[own:, at] = dot(pool, moving)

    each_group(qn.shape[1] // LANES, body)
    coarse[...] = dot(pooled[...].astype(BF16), weight[...]).astype(BF16)


def stacked(refs):
    halves = [ref[...].astype(F32) for ref in refs]
    own = halves[0].shape[0] // 2
    return (
        jnp.concatenate([half[:own] for half in halves], 0),
        jnp.concatenate([half[own:] for half in halves], 0),
    )


def project_kernel(head, slots, mod, weight, *refs):
    tokens, (query_out, keys_out) = refs[:slots], refs[slots:]
    primal, moving = stacked(tokens)
    width = primal.shape[1]
    count = primal.shape[0]
    both = jnp.concatenate(conditioned(primal, moving, mod, 0, width), 0)
    heads = weight.shape[0] // (3 * head)
    span = heads * head
    ones = block_ones(span, head.bit_length() - 1, 1.0 / head)

    def projected(member):
        rows = [weight[(3 * h + member) * head : (3 * h + member + 1) * head] for h in range(heads)]
        result = dot_nt(both, jnp.concatenate(rows, 0))
        return result[:count], result[count:]

    query, key = head_pairs([projected(0), projected(1)], ones)
    value, value_drift = projected(2)
    query_out[...] = jnp.concatenate(query, 1)
    keys_out[...] = jnp.concatenate(
        [key[0], value.astype(BF16), key[1], value_drift.astype(BF16)], 1
    )


def coarse_kernel(head, slots, groups, scale, weight, query, *refs):
    blocks, outs = refs[:groups], refs[groups:]
    count = query.shape[0]
    span = query.shape[1] // 2
    heads = span // head

    def part(member):
        return jnp.concatenate(
            [block[:, member * span : (member + 1) * span] for block in blocks], 0
        )

    key, value, key_drift, value_drift = (part(member) for member in range(4))
    lane = lax.broadcasted_iota(jnp.int32, (1, span), 1)
    masks = [
        ((lane >= h * head) & (lane < (h + 1) * head)).astype(F32) for h in range(heads)
    ]
    plain, drifting = query[:, :span], query[:, span:]
    plain = jnp.concatenate([plain * mask.astype(BF16) for mask in masks], 0)
    drifting = jnp.concatenate([drifting * mask.astype(BF16) for mask in masks], 0)
    score = dot_nt(plain, key)
    slope = dot_nt(drifting, key) + dot_nt(plain, key_drift)
    weights, tilted = [], []
    for h in range(heads):
        rows = slice(h * count, (h + 1) * count)
        factor = scale[h] / head
        e = jnp.exp2(score[rows] * (factor * LOG2E))
        weights.append(e)
        tilted.append(e * (slope[rows] * factor))
    weights = jnp.concatenate(weights, 0).astype(BF16)
    tilted = jnp.concatenate(tilted, 0).astype(BF16)
    ones = jnp.ones((key.shape[0], span), BF16)

    def own(stack):
        return sum(
            stack[h * count : (h + 1) * count] * mask for h, mask in enumerate(masks)
        )

    inverse = 1.0 / own(dot(weights, ones))
    output = own(dot(weights, value)) * inverse
    shifted = own(dot(tilted, value) + dot(weights, value_drift))
    moving = shifted * inverse - output * (own(dot(tilted, ones)) * inverse)
    both = jnp.concatenate([output.astype(BF16), moving.astype(BF16)], 0)
    spread(dot(both, weight[...]), slots, outs)


def spread(both, slots, outs):
    count = both.shape[0] // 2
    own = count // slots
    for slot, out in enumerate(outs):
        piece = jnp.concatenate(
            [both[slot * own : (slot + 1) * own], both[count + slot * own : count + (slot + 1) * own]],
            0,
        )
        out[...] = piece.astype(out.dtype)


def update_kernel(slots, mod, coarse, *refs):
    parts, (updated, source) = refs[:slots], refs[slots:]
    total = coarse[...].astype(F32)
    for ref in parts:
        total = total + ref[...].astype(F32)
    updated[...] = total
    own, width = total.shape[0] // 2, total.shape[1]
    source[...] = jnp.concatenate(conditioned(total[:own], total[own:], mod, 1, width), 0)


def mlp_kernel(slots, up, down, *refs):
    tokens, outs = refs[:slots], refs[slots:]
    primal, moving = stacked(tokens)
    count = primal.shape[0]
    both = jnp.concatenate([primal, moving], 0).astype(BF16)
    hidden = dot(both, up[...])
    x, dx = hidden[:count], hidden[count:]
    root = math.sqrt(2.0 / math.pi)
    square = x * x
    bend = jnp.tanh(root * (x + 0.044715 * (square * x)))
    half = 0.5 * (1.0 + bend)
    rise = half + 0.5 * x * (1.0 - bend * bend) * (root * (1.0 + 3 * 0.044715 * square))
    active = jnp.concatenate([(x * half).astype(BF16), (rise * dx).astype(BF16)], 0)
    spread(dot(active, down[...]), slots, outs)


def final_kernel(slots, updated, *refs):
    parts, (out, tangent) = refs[:slots], refs[slots:]
    total = updated[...]
    for ref in parts:
        total = total + ref[...].astype(F32)
    own = total.shape[0] // 2
    out[...] = total[:own].astype(BF16).reshape(out.shape)
    tangent[...] = total[own:].astype(BF16).reshape(out.shape)


def modulation_kernel(index, weight, out):
    latest = jnp.maximum(index[0], index[1])
    earlier = jnp.minimum(index[0], index[1])
    halves = EMBED // 2
    row = lax.broadcasted_iota(jnp.int32, (2 * EMBED, LANES), 0)
    angular = jnp.exp2((row & (halves - 1)).astype(F32) * (4.0 / halves))
    steps = jnp.where(row < EMBED, latest, latest - earlier).astype(F32) / STEPS
    angle = angular * steps
    cosine, sine = jnp.cos(angle), jnp.sin(angle)
    even = (row & halves) == 0
    feature = jnp.where(even, cosine, sine)
    slope = jnp.where(even, -sine, cosine) * angular

    @pl.loop(0, weight.shape[1] // LANES)
    def _(step):
        at = pl.ds(pl.multiple_of(step * LANES, LANES), LANES)
        block = weight[:, at]
        out[0:1, at] = jnp.sum(feature * block, axis=0, keepdims=True)
        out[1:2, at] = jnp.sum(slope * block, axis=0, keepdims=True)


def struct(shape, dtype=BF16):
    return jax.ShapeDtypeStruct(shape, dtype)


def near_call(kernel, outs, args, smem_count=0, scratch=(), name=None, far_out=False):
    def near_spec():
        return pl.BlockSpec(memory_space=pltpu.VMEM)

    args = [
        a if i < smem_count else pltpu.with_memory_space_constraint(a, pltpu.VMEM)
        for i, a in enumerate(args)
    ]
    return pl.pallas_call(
        kernel,
        in_specs=[pl.BlockSpec(memory_space=pltpu.SMEM)] * smem_count
        + [near_spec()] * (len(args) - smem_count),
        out_specs=[pl.BlockSpec() if far_out else near_spec() for _ in outs],
        out_shape=outs if far_out else [pltpu.VMEM(o.shape, o.dtype) for o in outs],
        scratch_shapes=list(scratch),
        compiler_params=pltpu.CompilerParams(vmem_limit_bytes=16 * 1024 * 1024),
        name=name,
    )(*args)


def shards(
    queries,
    fine_key_rows,
    fine_value_rows,
    fine_query_tangent,
    fine_key_tangent,
    fine_value_tangent,
    fine_head_scale,
    merged_token_weight,
    time_plan_index,
    time_modulation_weight,
    coarse_projection_weight,
    coarse_head_scale,
    head_output_weight,
    up_projection_weight,
    down_projection_weight,
):
    rows, columns, width = queries.shape
    heads = fine_head_scale.shape[0]
    head = width // heads
    count = rows * columns
    pairs = width // LANES
    tile = (rows, columns)
    strip = RADIUS * columns
    side_tokens = RADIUS * rows
    band = 1 << (max(side_tokens, 16) - 1).bit_length()
    corner_rows = 8 * RADIUS * RADIUS
    blocks = (rows // MERGE, columns // MERGE)
    own = blocks[0] * blocks[1]

    fields = (fine_key_rows, fine_value_rows, fine_key_tangent, fine_value_tangent)
    near = pl.BlockSpec(memory_space=pltpu.VMEM)
    messages = [pltpu.VMEM((4 * strip, width), BF16)] * 2
    messages += [pltpu.VMEM((4 * band, width), BF16)] * 2
    y0, y1, z0, z1, *fine = pl.pallas_call(
        pack_kernel,
        in_specs=[pl.BlockSpec(memory_space=pltpu.HBM)] * 6,
        out_specs=[near] * 10,
        out_shape=messages + [pltpu.VMEM(queries.shape, BF16)] * 6,
        scratch_shapes=[pltpu.SemaphoreType.DMA((6,))],
        compiler_params=pltpu.CompilerParams(vmem_limit_bytes=16 * 1024 * 1024),
        name="pack",
    )(
        *(
            pltpu.with_memory_space_constraint(field, pltpu.HBM)
            for field in (
                fine_key_rows, fine_value_rows, fine_key_tangent, fine_value_tangent,
                queries, fine_query_tangent,
            )
        )
    )
    key, value, key_drift, value_drift, query, query_drift = fine
    down_count, across_count = lax.axis_size("ty"), lax.axis_size("tx")
    y0, y1 = (
        lax.ppermute(y, "ty", couples(down_count, phase)) for phase, y in enumerate((y0, y1))
    )
    z0, z1 = (
        lax.ppermute(z, "tx", couples(across_count, phase)) for phase, z in enumerate((z0, z1))
    )

    flat = struct((count, width))
    sums = [struct((count, width), F32)] * 4
    qn, qdn, *own_sums = near_call(
        functools.partial(own_kernel, head),
        [flat] * 2 + sums,
        (
            fine_head_scale, query, query_drift, key, key_drift, value, value_drift,
        ),
        1,
        name="own_attention",
    )
    z0, z1, qn = lax.optimization_barrier((z0, z1, qn))
    corner = struct((corner_rows, width))
    c0, c1 = near_call(
        functools.partial(corner_kernel, rows), [corner] * 2, (z0, z1), name="corners"
    )
    c0, c1 = (
        lax.ppermute(c, "ty", couples(down_count, phase)) for phase, c in enumerate((c0, c1))
    )
    strip_sums = near_call(
        functools.partial(strip_kernel, head, tile),
        sums,
        (fine_head_scale, qn, qdn, z0, z1, y0, y1, *own_sums),
        1,
        name="strip_attention",
    )
    grid_shape = struct(queries.shape)
    pooled = struct((2 * own, width))
    fine_out, fine_tangent, coarse = near_call(
        functools.partial(last_kernel, head, tile),
        [grid_shape] * 2 + [pooled],
        (
            fine_head_scale, qn, qdn, c0, c1, *strip_sums, merged_token_weight,
        ),
        1,
        [pltpu.VMEM((2 * own, width), F32)],
        name="last_attention",
    )

    (mod,) = near_call(
        modulation_kernel,
        [struct((2, 4 * width), F32)],
        (time_plan_index, time_modulation_weight),
        1,
        name="modulation",
    )
    near_heads = coarse_head_scale.shape[0]
    span = near_heads * head
    packed = coarse_projection_weight.transpose(1, 2, 0).reshape(3 * span, width)
    slots = across_count
    tokens = gathered(coarse, "tx")
    group = slots * own
    query, keys = near_call(
        functools.partial(project_kernel, head, slots),
        [struct((group, 2 * span)), struct((group, 4 * span))],
        (mod, packed, *tokens),
        name="project",
    )
    key_blocks = row_gathered(keys, "ty")
    pieces = [struct((2 * own, width), F32)] + [struct((2 * own, width))] * (slots - 1)
    kept, *sent = near_call(
        functools.partial(coarse_kernel, head, slots, len(key_blocks)),
        pieces,
        (coarse_head_scale, head_output_weight.reshape(span, width), query, *key_blocks),
        1,
        name="coarse_attention",
    )
    updated, source = near_call(
        functools.partial(update_kernel, slots),
        [struct((2 * own, width), F32), struct((2 * own, width))],
        (mod, coarse, kept, *returned(sent, "tx")),
        name="update",
    )
    kept, *sent = near_call(
        functools.partial(mlp_kernel, slots),
        pieces,
        (up_projection_weight, down_projection_weight, *gathered(source, "tx")),
        name="mlp",
    )
    coarse_out, coarse_tangent = near_call(
        functools.partial(final_kernel, slots),
        [struct((*blocks, width))] * 2,
        (updated, kept, *returned(sent, "tx")),
        name="final",
        far_out=True,
    )
    return (fine_out, fine_tangent, coarse_out, coarse_tangent)


def solution(mesh):
    return jax.shard_map(
        shards,
        mesh=mesh,
        in_specs=(
            P("ty", "tx", None),
            P("ty", "tx", None),
            P("ty", "tx", None),
            P("ty", "tx", None),
            P("ty", "tx", None),
            P("ty", "tx", None),
            P(),
            P(),
            P(),
            P(),
            P(None, "tx", None),
            P("tx"),
            P("tx", None, None),
            P(None, "tx"),
            P("tx", None),
        ),
        out_specs=(
            P("ty", "tx", None),
            P("ty", "tx", None),
            P("ty", "tx", None),
            P("ty", "tx", None),
        ),
        check_vma=False,
    )
```

time: 121 us -> 75.6 us (0.62); the launches traced: 119 us -> 75.4 us
  Pallas kernels: 48.1 us -> 19 us
  local copies, waits for them, and re-layouts: 8.63 us -> 2.12 us
  matrix products: 4.86 us -> 0 us
  between operations: 2.84 us -> 0.89 us
  other arithmetic: 1.4 us -> 0 us
    pallas_call x10 -> x11, Pallas kernels: 48.1 us -> 19 us  [the longest x10 17.1 us: near_call(): pl.pallas_call(kernel, in_specs=[pl.BlockSpec(memory_space=pltpu.SMEM)] *...]
    ppermute x13 -> x6, starting transfers between devices: 20.4 us -> 11.3 us  [gathered(): lax.ppermute(value, axis, partner(count, step))]
    ppermute x0 -> x4, starting transfers between devices: none -> 8.83 us  [the longest x3 8.82 us: row_gathered(): lax.ppermute(value, axis, partner(count, step))]
    ppermute x0 -> x4, waiting for transfers between devices: none -> 5.27 us  [the longest x3 3.75 us: row_gathered(): lax.ppermute(value, axis, partner(count, step))]
    dot_general x1 -> x0, matrix products: 4.86 us -> none  [modulation(): jnp.dot(features, time_modulation_weight, precision=lax.Precision.HIGHEST)]
    unnamed x52 -> x23, local copies, waits for them, and re-layouts: 6.72 us -> 2.11 us
    ppermute x13 -> x6, waiting for transfers between devices: 7.89 us -> 3.89 us  [gathered(): lax.ppermute(value, axis, partner(count, step))]
    reshape x1 -> x0, local copies, waits for them, and re-layouts: 1.58 us -> none  [shards(): packed = coarse_projection_weight.reshape(width, near_heads, 3, head).tra...]
  transfers between devices with their start and end apart: 25 -> 22, of which waited for: 10 -> 10; matrix products, arithmetic and copies ran while one was open for 7% -> 2% of each run, Pallas kernels for 17% -> 13%
where the time goes in v2:
time: 75.6 us; the launch traced here: 75.4 us
  starting transfers between devices  36 us (48%)
  Pallas kernels  19 us (25%)
  waiting for transfers between devices  17.4 us (23%)
  local copies, waits for them, and re-layouts  2.12 us (3%)
  between operations  0.89 us (1%)
    pallas_call x10, Pallas kernels, near_call(): pl.pallas_call(kernel, in_specs=[pl.BlockSpec(memory_space=pltpu.SMEM)] *...  17.1 us
    ppermute x6, starting transfers between devices, gathered(): lax.ppermute(value, axis, partner(count, step))  11.3 us
    ppermute x6, starting transfers between devices, returned(): lax.ppermute(piece, axis, partner(count, step, True))  8.89 us
    ppermute x3, starting transfers between devices, row_gathered(): lax.ppermute(value, axis, partner(count, step))  8.82 us
    ppermute x6, waiting for transfers between devices, returned(): lax.ppermute(piece, axis, partner(count, step, True))  7.19 us
    ppermute x6, waiting for transfers between devices, gathered(): lax.ppermute(value, axis, partner(count, step))  3.89 us
    ppermute x2, starting transfers between devices, shards(): lax.ppermute(z, 'tx', couples(across_count, phase))  3.78 us
    ppermute x3, waiting for transfers between devices, row_gathered(): lax.ppermute(value, axis, partner(count, step))  3.75 us
  transfers between devices with their start and end apart: 22, of which 10 were waited for; matrix products, arithmetic and copies ran while one was open for 2% of the time, Pallas kernels for 13%

profile of v2, /device:TPU:0, one launch (start us, length us, event | category | flops | bytes accessed | tf_op | source)
XLA Modules:
  0.0 75.4 jit_solution(16064033277386124780)
XLA Ops:
  0.6 1.9 %pack.1 = (bf16[192,1024]{1,0:T(8,128)(2,1)S(1)}, bf16[192,1024]{1,0:T(8,128)(2,1)S(1)}, bf16[128,1024]{1,0:T(8,128)(2,1)S(1)}, bf16[128,1024]{1,0:T(8,128)(2,1)...) custom-call(bf16[8,16,1024]{2,1,0:T(8,128)(2,1)} %key.1, ...), custom_call_target="tpu_custom_call" | custom-call | tf_op jit(solution)/shard_map/pack/pallas_call | solution.py:628
  2.5 3.1 %collective-permute-start = (bf16[128,1024]{1,0:T(8,128)(2,1)S(1)}, bf16[128,1024]{1,0:T(8,128)(2,1)S(1)}, u32[]{:S(2)}, u32[]{:S(2)}) collective-permute-start(bf16[128,1024]{1,0:T(8,128)(2,1)S(1)} %get-tuple-element.46), channel_id=1, source_target_pairs={{0,1},{1,0},{2,3},{3,2},{4,5},{5,4},{6,7},{7,6},{8,9},{9,8},{10,11... | collective-permute-start | bytes 786440 | tf_op jit(solution)/shard_map/ppermute | solution.py:651
  7.7 3.1 %own_attention.1 = (bf16[128,1024]{1,0:T(8,128)(2,1)S(1)}, bf16[128,1024]{1,0:T(8,128)(2,1)S(1)}, f32[128,1024]{1,0:T(8,128)S(1)}, f32[128,1024]{1,0:T(8,128)S(1...) custom-call(f32[16]{0:T(128)S(1)} %copy-done.6, bf16[8,16,1024]{2,1,0:T(8,128)(2,1)S(1)} %get-tuple-element.48.q, ...), custom_call_target="tpu_custom_call" | custom-call | tf_op jit(solution)/shard_map/own_attention/pallas_call | solution.py:582
  10.9 1.1 %collective-permute-done.z0 = bf16[128,1024]{1,0:T(8,128)(2,1)S(1)} collective-permute-done((bf16[128,1024]{1,0:T(8,128)(2,1)S(1)}, bf16[128,1024]{1,0:T(8,128)(2,1)S(1)}, u32[]{:S(2)}, u32[]{:S(2)}) %collective-permute-start) | collective-permute-done | bytes 262176 | tf_op jit(solution)/shard_map/ppermute | solution.py:651
  12.3 1.8 %collective-permute-start.2 = (bf16[72,1024]{1,0:T(8,128)(2,1)S(1)}, bf16[72,1024]{1,0:T(8,128)(2,1)S(1)}, u32[]{:S(2)}, u32[]{:S(2)}) collective-permute-start(bf16[72,1024]{1,0:T(8,128)(2,1)S(1)} %get-tuple-element.59), channel_id=1, source_target_pairs={{0,4},{4,0},{8,12},{12,8},{16,20},{20,16},{24,28},{28,24},{1,5},{5... | collective-permute-start | bytes 442376 | tf_op jit(solution)/shard_map/ppermute | solution.py:671
  14.8 3.4 %strip_attention.1 = (f32[128,1024]{1,0:T(8,128)S(1)}, f32[128,1024]{1,0:T(8,128)S(1)}, f32[128,1024]{1,0:T(8,128)S(1)}, f32[128,1024]{1,0:T(8,128)S(1)}) custom-call(f32[16]{0:T(128)S(1)} %copy-done.6, bf16[128,1024]{1,0:T(8,128)(2,1)S(1)} %get-tuple-element.55.qn, bf16[128,1024]{1,0:T(8,128)(2,1)S(1)} %get-tuple-element.56.qdn, ...), custom_call_target="tpu_custom_call" | custom-call | tf_op jit(solution)/shard_map/strip_attention/pallas_call | solution.py:582
  18.3 3.6 %last_attention.1 = (bf16[8,16,1024]{2,1,0:T(8,128)(2,1)S(1)}, bf16[8,16,1024]{2,1,0:T(8,128)(2,1)S(1)}, bf16[16,1024]{1,0:T(8,128)(2,1)S(1)}) custom-call(f32[16]{0:T(128)S(1)} %copy-done.6, bf16[128,1024]{1,0:T(8,128)(2,1)S(1)} %get-tuple-element.55.qn, bf16[128,1024]{1,0:T(8,128)(2,1)S(1)} %get-tuple-element.56.qdn, ...), custom_call_target="tpu_custom_call" | custom-call | tf_op jit(solution)/shard_map/last_attention/pallas_call | solution.py:582
  21.9 4.4 %collective-permute-start.6 = (bf16[16,1024]{1,0:T(8,128)(2,1)S(1)}, bf16[16,1024]{1,0:T(8,128)(2,1)S(1)}, u32[]{:S(2)}, u32[]{:S(2)}) collective-permute-start(bf16[16,1024]{1,0:T(8,128)(2,1)S(1)} %get-tuple-element.73.refs_0_.coarse), channel_id=1, source_target_pairs={{0,1},{1,0},{2,3},{3,2},{4,5},{5,4},{6,7},{7,6},{8,9},{9,8},{10,11... | collective-permute-start | bytes 98312 | tf_op jit(solution)/shard_map/ppermute | solution.py:102
  26.3 2.4 %collective-permute-start.8 = (bf16[16,1024]{1,0:T(8,128)(2,1)S(1)}, bf16[16,1024]{1,0:T(8,128)(2,1)S(1)}, u32[]{:S(2)}, u32[]{:S(2)}) collective-permute-start(bf16[16,1024]{1,0:T(8,128)(2,1)S(1)} %get-tuple-element.73.refs_0_.coarse), channel_id=1, source_target_pairs={{0,3},{1,2},{2,1},{3,0},{4,7},{5,6},{6,5},{7,4},{8,11},{9,10},{10,... | collective-permute-start | bytes 98312 | tf_op jit(solution)/shard_map/ppermute | solution.py:102
  28.8 2.7 %modulation.1.mod = f32[2,4096]{1,0:T(2,128)S(1)} custom-call(s32[2]{0:T(128)S(1)} %copy-done.7, f32[256,4096]{1,0:T(8,128)S(1)} %copy-done), custom_call_target="tpu_custom_call" | custom-call | tf_op jit(solution)/shard_map/modulation/pallas_call | solution.py:582
  32.0 1.1 %project.1 = (bf16[32,512]{1,0:T(8,128)(2,1)S(1)}, bf16[32,1024]{1,0:T(8,128)(2,1)S(1)}) custom-call(f32[2,4096]{1,0:T(2,128)S(1)} %modulation.1.mod, bf16[768,1024]{1,0:T(8,128)(2,1)S(1)} %bitcast.4, bf16[16,1024]{1,0:T(8,128)(2,1)S(1)} %get-tuple-element.73.refs_0_.coarse, bf16[16,1024]{1,0:T(8,128)(2,1)S(1)} %collective-permute-done.6.refs_1_, ...), custom_call_target="tpu_custom_call" | custom-call | tf_op jit(solution)/shard_map/project/pallas_call | solution.py:582
  33.1 4.9 %collective-permute-start.9 = (bf16[32,1024]{1,0:T(8,128)(2,1)S(1)}, bf16[32,1024]{1,0:T(8,128)(2,1)S(1)}, u32[]{:S(2)}, u32[]{:S(2)}) collective-permute-start(bf16[32,1024]{1,0:T(8,128)(2,1)S(1)} %get-tuple-element.75), channel_id=1, source_target_pairs={{0,8},{4,12},{8,0},{12,4},{16,24},{20,28},{24,16},{28,20},{1,9},{5... | collective-permute-start | bytes 196616 | tf_op jit(solution)/shard_map/ppermute | solution.py:111
  38.0 2.6 %collective-permute-start.10 = (bf16[32,1024]{1,0:T(8,128)(2,1)S(1)}, bf16[32,1024]{1,0:T(8,128)(2,1)S(1)}, u32[]{:S(2)}, u32[]{:S(2)}) collective-permute-start(bf16[32,1024]{1,0:T(8,128)(2,1)S(1)} %get-tuple-element.75), channel_id=1, source_target_pairs={{0,16},{4,20},{8,24},{12,28},{16,0},{20,4},{24,8},{28,12},{1,17},{... | collective-permute-start | bytes 196616 | tf_op jit(solution)/shard_map/ppermute | solution.py:111
  40.5 1.4 %collective-permute-start.11 = (bf16[32,1024]{1,0:T(8,128)(2,1)S(1)}, bf16[32,1024]{1,0:T(8,128)(2,1)S(1)}, u32[]{:S(2)}, u32[]{:S(2)}) collective-permute-start(bf16[32,1024]{1,0:T(8,128)(2,1)S(1)} %get-tuple-element.75), channel_id=1, source_target_pairs={{0,24},{4,28},{8,16},{12,20},{16,8},{20,12},{24,0},{28,4},{1,25},{... | collective-permute-start | bytes 196616 | tf_op jit(solution)/shard_map/ppermute | solution.py:111
  41.9 2.2 %collective-permute-done.10 = bf16[32,1024]{1,0:T(8,128)(2,1)S(1)} collective-permute-done((bf16[32,1024]{1,0:T(8,128)(2,1)S(1)}, bf16[32,1024]{1,0:T(8,128)(2,1)S(1)}, u32[]{:S(2)}, u32[]{:S(2)}) %collective-permute-start.10) | collective-permute-done | bytes 65568 | tf_op jit(solution)/shard_map/ppermute | solution.py:111
  44.2 1.5 %collective-permute-done.11 = bf16[32,1024]{1,0:T(8,128)(2,1)S(1)} collective-permute-done((bf16[32,1024]{1,0:T(8,128)(2,1)S(1)}, bf16[32,1024]{1,0:T(8,128)(2,1)S(1)}, u32[]{:S(2)}, u32[]{:S(2)}) %collective-permute-start.11) | collective-permute-done | bytes 65568 | tf_op jit(solution)/shard_map/ppermute | solution.py:111
  45.7 1.5 %collective-permute-done.12.refs_1_ = bf16[128,1024]{1,0:T(8,128)(2,1)S(1)} collective-permute-done((bf16[128,1024]{1,0:T(8,128)(2,1)S(1)}, bf16[128,1024]{1,0:T(8,128)(2,1)S(1)}, u32[]{:S(2)}, u32[]{:S(2)}) %collective-permute-start.12) | collective-permute-done | bytes 262176 | tf_op jit(solution)/shard_map/ppermute | solution.py:114
  47.2 1.2 %coarse_attention.1 = (f32[16,1024]{1,0:T(8,128)S(1)}, bf16[16,1024]{1,0:T(8,128)(2,1)S(1)}, bf16[16,1024]{1,0:T(8,128)(2,1)S(1)}, bf16[16,1024]{1,0:T(8,128)(2,1)S(1)}) custom-call(f32[4]{0:T(128)S(1)} %copy-done.8, bf16[256,1024]{1,0:T(8,128)(2,1)S(1)} %bitcast.5, bf16[32,512]{1,0:T(8,128)(2,1)S(1)} %get-tuple-element.74.query, ...), custom_call_target="tpu_custom_call" | custom-call | tf_op jit(solution)/shard_map/coarse_attention/pallas_call | solution.py:582
  49.0 2.5 %collective-permute-start.14 = (bf16[16,1024]{1,0:T(8,128)(2,1)S(1)}, bf16[16,1024]{1,0:T(8,128)(2,1)S(1)}, u32[]{:S(2)}, u32[]{:S(2)}) collective-permute-start(bf16[16,1024]{1,0:T(8,128)(2,1)S(1)} %get-tuple-element.78), channel_id=1, source_target_pairs={{0,2},{1,3},{2,0},{3,1},{4,6},{5,7},{6,4},{7,5},{8,10},{9,11},{10,... | collective-permute-start | bytes 98312 | tf_op jit(solution)/shard_map/ppermute | solution.py:120
  51.5 1.4 %collective-permute-start.15 = (bf16[16,1024]{1,0:T(8,128)(2,1)S(1)}, bf16[16,1024]{1,0:T(8,128)(2,1)S(1)}, u32[]{:S(2)}, u32[]{:S(2)}) collective-permute-start(bf16[16,1024]{1,0:T(8,128)(2,1)S(1)} %get-tuple-element.79), channel_id=1, source_target_pairs={{0,3},{1,2},{2,1},{3,0},{4,7},{5,6},{6,5},{7,4},{8,11},{9,10},{10,... | collective-permute-start | bytes 98312 | tf_op jit(solution)/shard_map/ppermute | solution.py:120
  52.9 1.5 %collective-permute-done.14.refs_2_ = bf16[16,1024]{1,0:T(8,128)(2,1)S(1)} collective-permute-done((bf16[16,1024]{1,0:T(8,128)(2,1)S(1)}, bf16[16,1024]{1,0:T(8,128)(2,1)S(1)}, u32[]{:S(2)}, u32[]{:S(2)}) %collective-permute-start.14) | collective-permute-done | bytes 32800 | tf_op jit(solution)/shard_map/ppermute | solution.py:120
  54.3 2.8 %collective-permute-done.15.refs_3_ = bf16[16,1024]{1,0:T(8,128)(2,1)S(1)} collective-permute-done((bf16[16,1024]{1,0:T(8,128)(2,1)S(1)}, bf16[16,1024]{1,0:T(8,128)(2,1)S(1)}, u32[]{:S(2)}, u32[]{:S(2)}) %collective-permute-start.15) | collective-permute-done | bytes 32800 | tf_op jit(solution)/shard_map/ppermute | solution.py:120
  57.5 2.0 %collective-permute-start.17 = (bf16[16,1024]{1,0:T(8,128)(2,1)S(1)}, bf16[16,1024]{1,0:T(8,128)(2,1)S(1)}, u32[]{:S(2)}, u32[]{:S(2)}) collective-permute-start(bf16[16,1024]{1,0:T(8,128)(2,1)S(1)} %get-tuple-element.81.refs_0_), channel_id=1, source_target_pairs={{0,2},{1,3},{2,0},{3,1},{4,6},{5,7},{6,4},{7,5},{8,10},{9,11},{10,... | collective-permute-start | bytes 98312 | tf_op jit(solution)/shard_map/ppermute | solution.py:102
  59.4 2.4 %collective-permute-start.18 = (bf16[16,1024]{1,0:T(8,128)(2,1)S(1)}, bf16[16,1024]{1,0:T(8,128)(2,1)S(1)}, u32[]{:S(2)}, u32[]{:S(2)}) collective-permute-start(bf16[16,1024]{1,0:T(8,128)(2,1)S(1)} %get-tuple-element.81.refs_0_), channel_id=1, source_target_pairs={{0,3},{1,2},{2,1},{3,0},{4,7},{5,6},{6,5},{7,4},{8,11},{9,10},{10,... | collective-permute-start | bytes 98312 | tf_op jit(solution)/shard_map/ppermute | solution.py:102
  61.8 0.9 %collective-permute-done.17.refs_2_ = bf16[16,1024]{1,0:T(8,128)(2,1)S(1)} collective-permute-done((bf16[16,1024]{1,0:T(8,128)(2,1)S(1)}, bf16[16,1024]{1,0:T(8,128)(2,1)S(1)}, u32[]{:S(2)}, u32[]{:S(2)}) %collective-permute-start.17) | collective-permute-done | bytes 32800 | tf_op jit(solution)/shard_map/ppermute | solution.py:102
  62.7 2.4 %collective-permute-done.18.refs_3_ = bf16[16,1024]{1,0:T(8,128)(2,1)S(1)} collective-permute-done((bf16[16,1024]{1,0:T(8,128)(2,1)S(1)}, bf16[16,1024]{1,0:T(8,128)(2,1)S(1)}, u32[]{:S(2)}, u32[]{:S(2)}) %collective-permute-start.18) | collective-permute-done | bytes 32800 | tf_op jit(solution)/shard_map/ppermute | solution.py:102
  65.1 0.9 %mlp.1 = (f32[16,1024]{1,0:T(8,128)S(1)}, bf16[16,1024]{1,0:T(8,128)(2,1)S(1)}, bf16[16,1024]{1,0:T(8,128)(2,1)S(1)}, bf16[16,1024]{1,0:T(8,128)(2,1)S(1)}) custom-call(bf16[1024,1024]{1,0:T(8,128)(2,1)S(1)} %copy-done.1, bf16[1024,1024]{1,0:T(8,128)(2,1)S(1)} %copy-done.2, bf16[16,1024]{1,0:T(8,128)(2,1)S(1)} %get-tuple-element.81.refs_0_, ...), custom_call_target="tpu_custom_call" | custom-call | tf_op jit(solution)/shard_map/mlp/pallas_call | solution.py:582
  66.1 3.0 %collective-permute-start.20 = (bf16[16,1024]{1,0:T(8,128)(2,1)S(1)}, bf16[16,1024]{1,0:T(8,128)(2,1)S(1)}, u32[]{:S(2)}, u32[]{:S(2)}) collective-permute-start(bf16[16,1024]{1,0:T(8,128)(2,1)S(1)} %get-tuple-element.84), channel_id=1, source_target_pairs={{0,2},{1,3},{2,0},{3,1},{4,6},{5,7},{6,4},{7,5},{8,10},{9,11},{10,... | collective-permute-start | bytes 98312 | tf_op jit(solution)/shard_map/ppermute | solution.py:120
  69.1 1.4 %collective-permute-start.21 = (bf16[16,1024]{1,0:T(8,128)(2,1)S(1)}, bf16[16,1024]{1,0:T(8,128)(2,1)S(1)}, u32[]{:S(2)}, u32[]{:S(2)}) collective-permute-start(bf16[16,1024]{1,0:T(8,128)(2,1)S(1)} %get-tuple-element.85), channel_id=1, source_target_pairs={{0,3},{1,2},{2,1},{3,0},{4,7},{5,6},{6,5},{7,4},{8,11},{9,10},{10,... | collective-permute-start | bytes 98312 | tf_op jit(solution)/shard_map/ppermute | solution.py:120
  70.5 0.7 copy.22
  71.2 0.7 copy.23
  71.9 2.9 %collective-permute-done.21.refs_3_ = bf16[16,1024]{1,0:T(8,128)(2,1)S(1)} collective-permute-done((bf16[16,1024]{1,0:T(8,128)(2,1)S(1)}, bf16[16,1024]{1,0:T(8,128)(2,1)S(1)}, u32[]{:S(2)}, u32[]{:S(2)}) %collective-permute-start.21) | collective-permute-done | bytes 32800 | tf_op jit(solution)/shard_map/ppermute | solution.py:120
  (47 shorter events, 5.3 us)
Async XLA Ops:
  2.5 9.4 %collective-permute-start = (bf16[128,1024]{1,0:T(8,128)(2,1)S(1)}, bf16[128,1024]{1,0:T(8,128)(2,1)S(1)}, u32[]{:S(2)}, u32[]{:S(2)}) collective-permute-start(bf16[128,1024]{1,0:T(8,128)(2,1)S(1)} %get-tuple-element.46), channel_id=1, source_target_pairs={{0,1},{1,0},{2,3},{3,2},{4,5},{5,4},{6,7},{7,6},{8,9},{9,8},{10,11... | collective-permute-start | bytes 786440 | tf_op jit(solution)/shard_map/ppermute | solution.py:651
  5.6 6.3 %collective-permute-start.1 = (bf16[128,1024]{1,0:T(8,128)(2,1)S(1)}, bf16[128,1024]{1,0:T(8,128)(2,1)S(1)}, u32[]{:S(2)}, u32[]{:S(2)}) collective-permute-start(bf16[128,1024]{1,0:T(8,128)(2,1)S(1)} %get-tuple-element.47), channel_id=1, source_target_pairs={{1,2},{2,1},{5,6},{6,5},{9,10},{10,9},{13,14},{14,13},{17,18},{18,... | collective-permute-start | bytes 786440 | tf_op jit(solution)/shard_map/ppermute | solution.py:651
  6.3 8.5 %collective-permute-start.4 = (bf16[192,1024]{1,0:T(8,128)(2,1)S(1)}, bf16[192,1024]{1,0:T(8,128)(2,1)S(1)}, u32[]{:S(2)}, u32[]{:S(2)}) collective-permute-start(bf16[192,1024]{1,0:T(8,128)(2,1)S(1)} %get-tuple-element.61), channel_id=1, source_target_pairs={{0,4},{4,0},{8,12},{12,8},{16,20},{20,16},{24,28},{28,24},{1,5},{5... | collective-permute-start | bytes 1179656 | tf_op jit(solution)/shard_map/ppermute | solution.py:648
  6.4 8.4 %collective-permute-start.5 = (bf16[192,1024]{1,0:T(8,128)(2,1)S(1)}, bf16[192,1024]{1,0:T(8,128)(2,1)S(1)}, u32[]{:S(2)}, u32[]{:S(2)}) collective-permute-start(bf16[192,1024]{1,0:T(8,128)(2,1)S(1)} %get-tuple-element.62), channel_id=1, source_target_pairs={{4,8},{8,4},{12,16},{16,12},{20,24},{24,20},{5,9},{9,5},{13,17},{1... | collective-permute-start | bytes 1179656 | tf_op jit(solution)/shard_map/ppermute | solution.py:648
  7.1 0.7 copy-start.6
  12.3 6.0 %copy-start.3 = (bf16[1024,1024]{1,0:T(8,128)(2,1)S(1)}, bf16[1024,1024]{1,0:T(8,128)(2,1)}, u32[]{:S(2)}) copy-start(bf16[1024,1024]{1,0:T(8,128)(2,1)} %weight.2) | copy-start | bytes 6291460
  12.3 5.9 %collective-permute-start.2 = (bf16[72,1024]{1,0:T(8,128)(2,1)S(1)}, bf16[72,1024]{1,0:T(8,128)(2,1)S(1)}, u32[]{:S(2)}, u32[]{:S(2)}) collective-permute-start(bf16[72,1024]{1,0:T(8,128)(2,1)S(1)} %get-tuple-element.59), channel_id=1, source_target_pairs={{0,4},{4,0},{8,12},{12,8},{16,20},{20,16},{24,28},{28,24},{1,5},{5... | collective-permute-start | bytes 442376 | tf_op jit(solution)/shard_map/ppermute | solution.py:671
  14.1 4.1 %collective-permute-start.3 = (bf16[72,1024]{1,0:T(8,128)(2,1)S(1)}, bf16[72,1024]{1,0:T(8,128)(2,1)S(1)}, u32[]{:S(2)}, u32[]{:S(2)}) collective-permute-start(bf16[72,1024]{1,0:T(8,128)(2,1)S(1)} %get-tuple-element.60), channel_id=1, source_target_pairs={{4,8},{8,4},{12,16},{16,12},{20,24},{24,20},{5,9},{9,5},{13,17},{1... | collective-permute-start | bytes 442376 | tf_op jit(solution)/shard_map/ppermute | solution.py:671
  18.3 10.5 %copy-start = (f32[256,4096]{1,0:T(8,128)S(1)}, f32[256,4096]{1,0:T(8,128)}, u32[]{:S(2)}) copy-start(f32[256,4096]{1,0:T(8,128)} %weight.3) | copy-start | bytes 12582916
  18.3 10.5 %copy-start.7 = (s32[2]{0:T(128)S(1)}, s32[2]{0:T(128)}, u32[]{:S(2)}) copy-start(s32[2]{0:T(128)} %index.1) | copy-start | bytes 28
  21.9 10.1 %copy-start.4 = (bf16[1024,4,192]{0,2,1:T(8,128)(2,1)S(1)}, bf16[1024,4,192]{0,2,1:T(8,128)(2,1)}, u32[]{:S(2)}) copy-start(bf16[1024,4,192]{0,2,1:T(8,128)(2,1)} %param.25) | copy-start | bytes 4718596
  21.9 9.5 %collective-permute-start.6 = (bf16[16,1024]{1,0:T(8,128)(2,1)S(1)}, bf16[16,1024]{1,0:T(8,128)(2,1)S(1)}, u32[]{:S(2)}, u32[]{:S(2)}) collective-permute-start(bf16[16,1024]{1,0:T(8,128)(2,1)S(1)} %get-tuple-element.73.refs_0_.coarse), channel_id=1, source_target_pairs={{0,1},{1,0},{2,3},{3,2},{4,5},{5,4},{6,7},{7,6},{8,9},{9,8},{10,11... | collective-permute-start | bytes 98312 | tf_op jit(solution)/shard_map/ppermute | solution.py:102
  26.3 5.1 %collective-permute-start.7 = (bf16[16,1024]{1,0:T(8,128)(2,1)S(1)}, bf16[16,1024]{1,0:T(8,128)(2,1)S(1)}, u32[]{:S(2)}, u32[]{:S(2)}) collective-permute-start(bf16[16,1024]{1,0:T(8,128)(2,1)S(1)} %get-tuple-element.73.refs_0_.coarse), channel_id=1, source_target_pairs={{0,2},{1,3},{2,0},{3,1},{4,6},{5,7},{6,4},{7,5},{8,10},{9,11},{10,... | collective-permute-start | bytes 98312 | tf_op jit(solution)/shard_map/ppermute | solution.py:102
  26.3 5.7 %collective-permute-start.8 = (bf16[16,1024]{1,0:T(8,128)(2,1)S(1)}, bf16[16,1024]{1,0:T(8,128)(2,1)S(1)}, u32[]{:S(2)}, u32[]{:S(2)}) collective-permute-start(bf16[16,1024]{1,0:T(8,128)(2,1)S(1)} %get-tuple-element.73.refs_0_.coarse), channel_id=1, source_target_pairs={{0,3},{1,2},{2,1},{3,0},{4,7},{5,6},{6,5},{7,4},{8,11},{9,10},{10,... | collective-permute-start | bytes 98312 | tf_op jit(solution)/shard_map/ppermute | solution.py:102
  28.7 18.5 %copy-start.5 = (bf16[4,64,1024]{2,1,0:T(8,128)(2,1)S(1)}, bf16[4,64,1024]{2,1,0:T(8,128)(2,1)}, u32[]{:S(2)}) copy-start(bf16[4,64,1024]{2,1,0:T(8,128)(2,1)} %param.27) | copy-start | bytes 1572868
  28.7 36.4 %copy-start.2 = (bf16[1024,1024]{1,0:T(8,128)(2,1)S(1)}, bf16[1024,1024]{1,0:T(8,128)(2,1)}, u32[]{:S(2)}) copy-start(bf16[1024,1024]{1,0:T(8,128)(2,1)} %down.1) | copy-start | bytes 6291460
  31.4 15.8 %copy-start.8 = (f32[4]{0:T(128)S(1)}, f32[4]{0:T(128)}, u32[]{:S(2)}) copy-start(f32[4]{0:T(128)} %scale.7) | copy-start | bytes 52
  31.4 33.7 %copy-start.1 = (bf16[1024,1024]{1,0:T(8,128)(2,1)S(1)}, bf16[1024,1024]{1,0:T(8,128)(2,1)}, u32[]{:S(2)}) copy-start(bf16[1024,1024]{1,0:T(8,128)(2,1)} %up.1) | copy-start | bytes 6291460
  33.1 8.8 %collective-permute-start.9 = (bf16[32,1024]{1,0:T(8,128)(2,1)S(1)}, bf16[32,1024]{1,0:T(8,128)(2,1)S(1)}, u32[]{:S(2)}, u32[]{:S(2)}) collective-permute-start(bf16[32,1024]{1,0:T(8,128)(2,1)S(1)} %get-tuple-element.75), channel_id=1, source_target_pairs={{0,8},{4,12},{8,0},{12,4},{16,24},{20,28},{24,16},{28,20},{1,9},{5... | collective-permute-start | bytes 196616 | tf_op jit(solution)/shard_map/ppermute | solution.py:111
  38.0 6.2 %collective-permute-start.10 = (bf16[32,1024]{1,0:T(8,128)(2,1)S(1)}, bf16[32,1024]{1,0:T(8,128)(2,1)S(1)}, u32[]{:S(2)}, u32[]{:S(2)}) collective-permute-start(bf16[32,1024]{1,0:T(8,128)(2,1)S(1)} %get-tuple-element.75), channel_id=1, source_target_pairs={{0,16},{4,20},{8,24},{12,28},{16,0},{20,4},{24,8},{28,12},{1,17},{... | collective-permute-start | bytes 196616 | tf_op jit(solution)/shard_map/ppermute | solution.py:111
  40.5 5.2 %collective-permute-start.11 = (bf16[32,1024]{1,0:T(8,128)(2,1)S(1)}, bf16[32,1024]{1,0:T(8,128)(2,1)S(1)}, u32[]{:S(2)}, u32[]{:S(2)}) collective-permute-start(bf16[32,1024]{1,0:T(8,128)(2,1)S(1)} %get-tuple-element.75), channel_id=1, source_target_pairs={{0,24},{4,28},{8,16},{12,20},{16,8},{20,12},{24,0},{28,4},{1,25},{... | collective-permute-start | bytes 196616 | tf_op jit(solution)/shard_map/ppermute | solution.py:111
  45.7 1.5 %collective-permute-start.12 = (bf16[128,1024]{1,0:T(8,128)(2,1)S(1)}, bf16[128,1024]{1,0:T(8,128)(2,1)S(1)}, u32[]{:S(2)}, u32[]{:S(2)}) collective-permute-start(bf16[128,1024]{1,0:T(8,128)(2,1)S(1)} %constant_dynamic-update-slice_fusion.refs_0_), channel_id=1, source_target_pairs={{0,4},{4,0},{8,12},{12,8},{16,20},{20,16},{24,28},{28,24},{1,5},{5... | collective-permute-start | bytes 786440 | tf_op jit(solution)/shard_map/ppermute | solution.py:114
  48.4 4.5 %collective-permute-start.13 = (bf16[16,1024]{1,0:T(8,128)(2,1)S(1)}, bf16[16,1024]{1,0:T(8,128)(2,1)S(1)}, u32[]{:S(2)}, u32[]{:S(2)}) collective-permute-start(bf16[16,1024]{1,0:T(8,128)(2,1)S(1)} %get-tuple-element.77), channel_id=1, source_target_pairs={{0,1},{1,0},{2,3},{3,2},{4,5},{5,4},{6,7},{7,6},{8,9},{9,8},{10,11... | collective-permute-start | bytes 98312 | tf_op jit(solution)/shard_map/ppermute | solution.py:120
  49.0 5.3 %collective-permute-start.14 = (bf16[16,1024]{1,0:T(8,128)(2,1)S(1)}, bf16[16,1024]{1,0:T(8,128)(2,1)S(1)}, u32[]{:S(2)}, u32[]{:S(2)}) collective-permute-start(bf16[16,1024]{1,0:T(8,128)(2,1)S(1)} %get-tuple-element.78), channel_id=1, source_target_pairs={{0,2},{1,3},{2,0},{3,1},{4,6},{5,7},{6,4},{7,5},{8,10},{9,11},{10,... | collective-permute-start | bytes 98312 | tf_op jit(solution)/shard_map/ppermute | solution.py:120
  51.5 5.7 %collective-permute-start.15 = (bf16[16,1024]{1,0:T(8,128)(2,1)S(1)}, bf16[16,1024]{1,0:T(8,128)(2,1)S(1)}, u32[]{:S(2)}, u32[]{:S(2)}) collective-permute-start(bf16[16,1024]{1,0:T(8,128)(2,1)S(1)} %get-tuple-element.79), channel_id=1, source_target_pairs={{0,3},{1,2},{2,1},{3,0},{4,7},{5,6},{6,5},{7,4},{8,11},{9,10},{10,... | collective-permute-start | bytes 98312 | tf_op jit(solution)/shard_map/ppermute | solution.py:120
  57.4 4.5 %collective-permute-start.16 = (bf16[16,1024]{1,0:T(8,128)(2,1)S(1)}, bf16[16,1024]{1,0:T(8,128)(2,1)S(1)}, u32[]{:S(2)}, u32[]{:S(2)}) collective-permute-start(bf16[16,1024]{1,0:T(8,128)(2,1)S(1)} %get-tuple-element.81.refs_0_), channel_id=1, source_target_pairs={{0,1},{1,0},{2,3},{3,2},{4,5},{5,4},{6,7},{7,6},{8,9},{9,8},{10,11... | collective-permute-start | bytes 98312 | tf_op jit(solution)/shard_map/ppermute | solution.py:102
  57.5 5.2 %collective-permute-start.17 = (bf16[16,1024]{1,0:T(8,128)(2,1)S(1)}, bf16[16,1024]{1,0:T(8,128)(2,1)S(1)}, u32[]{:S(2)}, u32[]{:S(2)}) collective-permute-start(bf16[16,1024]{1,0:T(8,128)(2,1)S(1)} %get-tuple-element.81.refs_0_), channel_id=1, source_target_pairs={{0,2},{1,3},{2,0},{3,1},{4,6},{5,7},{6,4},{7,5},{8,10},{9,11},{10,... | collective-permute-start | bytes 98312 | tf_op jit(solution)/shard_map/ppermute | solution.py:102
  59.4 5.7 %collective-permute-start.18 = (bf16[16,1024]{1,0:T(8,128)(2,1)S(1)}, bf16[16,1024]{1,0:T(8,128)(2,1)S(1)}, u32[]{:S(2)}, u32[]{:S(2)}) collective-permute-start(bf16[16,1024]{1,0:T(8,128)(2,1)S(1)} %get-tuple-element.81.refs_0_), channel_id=1, source_target_pairs={{0,3},{1,2},{2,1},{3,0},{4,7},{5,6},{6,5},{7,4},{8,11},{9,10},{10,... | collective-permute-start | bytes 98312 | tf_op jit(solution)/shard_map/ppermute | solution.py:102
  66.0 5.9 %collective-permute-start.19 = (bf16[16,1024]{1,0:T(8,128)(2,1)S(1)}, bf16[16,1024]{1,0:T(8,128)(2,1)S(1)}, u32[]{:S(2)}, u32[]{:S(2)}) collective-permute-start(bf16[16,1024]{1,0:T(8,128)(2,1)S(1)} %get-tuple-element.83), channel_id=1, source_target_pairs={{0,1},{1,0},{2,3},{3,2},{4,5},{5,4},{6,7},{7,6},{8,9},{9,8},{10,11... | collective-permute-start | bytes 98312 | tf_op jit(solution)/shard_map/ppermute | solution.py:120
  66.1 5.8 %collective-permute-start.20 = (bf16[16,1024]{1,0:T(8,128)(2,1)S(1)}, bf16[16,1024]{1,0:T(8,128)(2,1)S(1)}, u32[]{:S(2)}, u32[]{:S(2)}) collective-permute-start(bf16[16,1024]{1,0:T(8,128)(2,1)S(1)} %get-tuple-element.84), channel_id=1, source_target_pairs={{0,2},{1,3},{2,0},{3,1},{4,6},{5,7},{6,4},{7,5},{8,10},{9,11},{10,... | collective-permute-start | bytes 98312 | tf_op jit(solution)/shard_map/ppermute | solution.py:120
  69.1 5.7 %collective-permute-start.21 = (bf16[16,1024]{1,0:T(8,128)(2,1)S(1)}, bf16[16,1024]{1,0:T(8,128)(2,1)S(1)}, u32[]{:S(2)}, u32[]{:S(2)}) collective-permute-start(bf16[16,1024]{1,0:T(8,128)(2,1)S(1)} %get-tuple-element.85), channel_id=1, source_target_pairs={{0,3},{1,2},{2,1},{3,0},{4,7},{5,6},{6,5},{7,4},{8,11},{9,10},{10,... | collective-permute-start | bytes 98312 | tf_op jit(solution)/shard_map/ppermute | solution.py:120

commit v3 on v2

--- a/solution.py
+++ b/solution.py
@@ -8,13 +8,14 @@
 from jax.experimental.pallas import tpu as pltpu
 from jax.sharding import PartitionSpec as P
 
+
 EMBED = 128
 RADIUS = 3
 MERGE = 4
 STEPS = 1000
 EPSILON = 1e-06
 LANES = 128
-TOGETHER = 4
+WIDE = 256
 LOG2E = math.log2(math.e)
 F32 = jnp.float32
 BF16 = jnp.bfloat16
@@ -90,6 +91,10 @@
     ]
 
 
+def exchanged(value, axis, phase):
+    return lax.ppermute(value, axis, couples(lax.axis_size(axis), phase))
+
+
 def partner(count, step, back=False):
     if count & (count - 1) == 0:
         return [(i, i ^ step) for i in range(count)]
@@ -122,55 +127,62 @@
     ]
 
 
+def lanes_of(head):
+    lane = lax.broadcasted_iota(jnp.int32, (1, LANES), 1)
+    first = lane < head
+    return (
+        first,
+        first.astype(F32).astype(BF16),
+        (lane >= head).astype(F32).astype(BF16),
+    )
+
+
+def filled(array):
+    short = -array.shape[0] % LANES
+    if not short:
+        return array
+    return jnp.concatenate([array, jnp.zeros((short, array.shape[1]), array.dtype)], 0)
+
+
 def attend(items, mask, head):
     count, keys = mask.shape
-    lane = lax.broadcasted_iota(jnp.int32, (1, LANES), 1)
-    first = (lane < head).astype(F32).astype(BF16)
-    second = (lane >= head).astype(F32).astype(BF16)
-    scores, slopes = [], []
-    for query, query_drift, key, key_drift, _, _, _ in items:
-        query_0, query_1 = query * first, query * second
-        drift_0, drift_1 = query_drift * first, query_drift * second
-        scores.append(dot_nt(jnp.concatenate([query_0, query_1], 0), key))
-        slopes.append(
-            dot_nt(
-                jnp.concatenate(
-                    [
-                        jnp.concatenate([drift_0, query_0], 1),
-                        jnp.concatenate([drift_1, query_1], 1),
-                    ],
-                    0,
-                ),
-                jnp.concatenate([key, key_drift], 1),
-            )
-        )
-    weights, tilts = [], []
-    for score, slope, item in zip(scores, slopes, items):
-        heavy, tilted = [], []
+    first, mine, other = lanes_of(head)
+    products = []
+    for query, query_drift, key, key_drift, *_ in items:
+        left = jnp.concatenate([query, query_drift], 1)
+        left = jnp.concatenate(
+            [left * jnp.concatenate([m, m], 1) for m in (mine, other)], 0
+        )
+        right = jnp.concatenate(
+            [
+                jnp.concatenate([key, jnp.zeros_like(key)], 1),
+                jnp.concatenate([key_drift, key], 1),
+            ],
+            0,
+        )
+        products.append(dot_nt(left, right))
+    rows = []
+    for product, item in zip(products, items):
         for place, factor in enumerate(item[6]):
-            rows = slice(place * count, (place + 1) * count)
-            weight = jnp.exp2(score[rows] * (factor * LOG2E)) * mask
-            heavy.append(weight.astype(BF16))
-            tilted.append((weight * (slope[rows] * factor)).astype(BF16))
-        weights.append(jnp.concatenate(heavy, 0))
-        tilts.append(jnp.concatenate(tilted, 0))
-    ones = jnp.ones((keys, LANES), BF16)
-
-    def own(stack):
-        return jnp.where(lane < head, stack[:count], stack[count:])
-
+            block = product[place * count : (place + 1) * count]
+            weight = jnp.exp2(block[:, :keys] * (factor * LOG2E)) * mask
+            tilt = weight * (block[:, keys:] * factor)
+            rows.append(jnp.concatenate([weight.astype(BF16), tilt.astype(BF16)], 0))
     results = []
-    for weight, tilt, item in zip(weights, tilts, items):
+    for i, item in enumerate(items):
         value, value_drift = item[4], item[5]
-        mixed = dot(weight, jnp.concatenate([value, value_drift], 1))
-        turned = dot(tilt, value)
-        sums = dot(jnp.concatenate([weight, tilt], 0), ones)
+        own = dot(rows[2 * i], jnp.concatenate([value * mine + other, value_drift * mine], 1))
+        next_own = dot(
+            rows[2 * i + 1], jnp.concatenate([value * other + mine, value_drift * other], 1)
+        )
+        top, top_next = own[:count, :LANES], next_own[:count, :LANES]
+        low, low_next = own[count:, :LANES], next_own[count:, :LANES]
         results.append(
             (
-                own(mixed[:, :LANES]),
-                own(mixed[:, LANES:] + turned),
-                own(sums[: 2 * count]),
-                own(sums[2 * count :]),
+                jnp.where(first, top, top_next),
+                jnp.where(first, own[:count, LANES:] + low, next_own[:count, LANES:] + low_next),
+                jnp.where(first, top_next, top),
+                jnp.where(first, low_next, low),
             )
         )
     return results
@@ -198,10 +210,10 @@
     return lax.shift_right_logical(number * (128 // RADIUS + 1), 7)
 
 
-def pack_kernel(key, value, key_drift, value_drift, query, query_drift, *refs):
+def pack_kernel(key, value, key_drift, value_drift, query, query_drift, scale, *refs):
     y0, y1, z0, z1, sems = *refs[:4], refs[-1]
-    near = refs[4:10]
-    far = (key, value, key_drift, value_drift, query, query_drift)
+    near = refs[4:11]
+    far = (key, value, key_drift, value_drift, query, query_drift, scale)
     copies = [
         pltpu.make_async_copy(source, target, sems.at[i])
         for i, (source, target) in enumerate(zip(far, near))
@@ -236,13 +248,13 @@
 
 def corner_kernel(rows, z0, z1, c0, c1):
     half = z0.shape[0]
-    band = half // 4
+    side_tokens = half // 4
     square = RADIUS * RADIUS
     place = lax.broadcasted_iota(jnp.int32, (1, half), 1)
-    array = lax.shift_right_logical(place, log2(band))
+    array = sum(jnp.where(place >= i * side_tokens, 1, 0) for i in range(1, 4))
     for phase, c in enumerate((c0, c1)):
         down, _ = side("ty", phase)
-        token = (place & (band - 1)) - jnp.where(down, (rows - RADIUS) * RADIUS, 0)
+        token = place - array * side_tokens - jnp.where(down, (rows - RADIUS) * RADIUS, 0)
         valid = (token >= 0) & (token < square)
         total = None
         for meet, z in enumerate((z0, z1)):
@@ -252,48 +264,54 @@
         c[...] = total.astype(BF16)
 
 
-def each_group(pairs, body):
-    together = math.gcd(pairs, TOGETHER)
-
-    @pl.loop(0, pairs // together)
-    def _(step):
-        starts = [
-            pl.multiple_of((step * together + i) * LANES, LANES) for i in range(together)
-        ]
-        body(step * together, [pl.ds(start, LANES) for start in starts])
+def wide_pairs(parts, width, ones):
+    wide = math.gcd(width, WIDE)
+    normed = head_pairs([parts(slice(at, at + wide)) for at in range(0, width, wide)], ones)
+    return [
+        tuple(filled(member[:, at : at + LANES]) for member in couple)
+        for couple in normed
+        for at in range(0, wide, LANES)
+    ]
+
+
+def factors_of(scale, pair, head):
+    return [scale[2 * pair + i] / head for i in range(2)]
+
+
+def pair_lanes(width):
+    return [slice(at, at + LANES) for at in range(0, width, LANES)]
 
 
 def own_kernel(head, scale, q, qd, k, kd, v, vd, qn, qdn, *sums):
     rows, columns, width = q.shape
     count = rows * columns
-    ones = block_ones(LANES, head.bit_length() - 1, 1.0 / head)
+    ones = block_ones(math.gcd(width, WIDE), log2(head), 1.0 / head)
     place = lax.broadcasted_iota(jnp.int32, (1, count), 1)
-    shift = columns.bit_length() - 1
-    mask = near(lax.shift_right_logical(place, shift), place & (columns - 1), columns, count)
-
-    def body(pair, lanes):
-        def flat(ref, at):
-            return ref[:, :, at].reshape(count, LANES)
-
-        normed = head_pairs(
-            [
-                (flat(a, at).astype(F32), flat(b, at).astype(F32))
-                for at in lanes
-                for a, b in ((q, qd), (k, kd))
-            ],
-            ones,
-        )
-        items = []
-        for i, at in enumerate(lanes):
-            query, key = normed[2 * i], normed[2 * i + 1]
-            qn[:, at], qdn[:, at] = query
-            factors = [scale[2 * (pair + i) + j] / head for j in range(2)]
-            items.append((*query, *key, flat(v, at), flat(vd, at), factors))
-        for at, parts in zip(lanes, attend(items, mask, head)):
-            for ref, part in zip(sums, parts):
-                ref[:, at] = part
-
-    each_group(width // LANES, body)
+    mask = near(
+        lax.shift_right_logical(place, log2(columns)), place & (columns - 1), columns, count
+    )
+
+    def flat(ref, at):
+        return ref[:, :, at].reshape(count, -1)
+
+    def normed(values, tangent):
+        return wide_pairs(
+            lambda at: (flat(values, at).astype(F32), flat(tangent, at).astype(F32)), width, ones
+        )
+
+    queries, keys = normed(q, qd), normed(k, kd)
+    items = []
+    for pair, at in enumerate(pair_lanes(width)):
+        qn[:, at], qdn[:, at] = queries[pair]
+        items.append(
+            (
+                *queries[pair], *keys[pair], flat(v, at), flat(vd, at),
+                factors_of(scale, pair, head),
+            )
+        )
+    for at, parts in zip(pair_lanes(width), attend(items, mask, head)):
+        for ref, part in zip(sums, parts):
+            ref[:, at] = part
 
 
 def moved(row, column, phase_down, phase_right, tile):
@@ -309,116 +327,114 @@
     return row, column
 
 
-def strip_places(tile, band):
+def beside_places(tile):
     rows, columns = tile
-    strip = RADIUS * columns
-    place = lax.broadcasted_iota(jnp.int32, (1, 2 * band + 2 * strip), 1)
-    beside = place < 2 * band
-    phase = lax.shift_right_logical(place, log2(band))
-    token = place & (band - 1)
+    side_tokens, strip = RADIUS * rows, RADIUS * columns
+    place = lax.broadcasted_iota(jnp.int32, (1, LANES), 1)
+    beside = place < 2 * side_tokens
+    later = place >= side_tokens
+    token = place - jnp.where(later, side_tokens, 0)
     side_row = by_radius(token)
-    side_column = token - side_row * RADIUS
-    side_row = jnp.where(side_row < rows, side_row, 8 * (rows + columns))
-    rest = place - 2 * band
-    later = rest >= strip
-    rest = rest - jnp.where(later, strip, 0)
-    row = jnp.where(beside, side_row, lax.shift_right_logical(rest, log2(columns)))
-    column = jnp.where(beside, side_column, rest & (columns - 1))
-    down = jnp.where(beside, -1, jnp.where(later, 1, 0))
-    return moved(row, column, down, jnp.where(beside, phase, -1), tile)
-
-
-def corner_places(tile, band):
-    square = RADIUS * RADIUS
-    place = lax.broadcasted_iota(jnp.int32, (1, 2 * band), 1)
-    slot = place & (band - 1)
-    later = slot >= square
-    token = slot - jnp.where(later, square, 0)
-    row = by_radius(token)
-    column = token - row * RADIUS
-    row = jnp.where(slot < 2 * square, row, 8 * sum(tile))
-    down = lax.shift_right_logical(place, log2(band))
-    return moved(row, column, down, jnp.where(later, 1, 0), tile)
-
-
-def strip_kernel(head, tile, scale, qn, qdn, z0, z1, y0, y1, *sums):
-    ones = block_ones(LANES, head.bit_length() - 1, 1.0 / head)
-    messages = (z0, z1, y0, y1)
-    row, column = strip_places(tile, z0.shape[0] // 4)
-    mask = near(row, column, tile[1], qn.shape[0])
-
-    def body(pair, lanes):
-        def part(array, at):
-            pieces = []
-            for ref in messages:
-                size = ref.shape[0] // 4
-                pieces.append(ref[array * size : (array + 1) * size, at])
-            return jnp.concatenate(pieces, 0)
-
-        keys = head_pairs(
-            [(part(0, at).astype(F32), part(2, at).astype(F32)) for at in lanes], ones
-        )
-        items = [
-            (
-                qn[:, at], qdn[:, at], *key, part(1, at), part(3, at),
-                [scale[2 * (pair + i) + j] / head for j in range(2)],
-            )
-            for i, (at, key) in enumerate(zip(lanes, keys))
-        ]
-        for at, parts in zip(lanes, attend(items, mask, head)):
-            for before, after, piece in zip(sums[:4], sums[4:], parts):
-                after[:, at] = before[:, at] + piece
-
-    each_group(qn.shape[1] // LANES, body)
+    rest = place - 2 * side_tokens
+    rest_row = lax.shift_right_logical(rest, log2(columns))
+    row = jnp.where(beside, side_row, jnp.where(rest < strip, rest_row, 8 * sum(tile)))
+    column = jnp.where(beside, token - side_row * RADIUS, rest & (columns - 1))
+    right = jnp.where(beside, jnp.where(later, 1, 0), -1)
+    return moved(row, column, jnp.where(beside, -1, 0), right, tile)
+
+
+def last_places(tile):
+    _, columns = tile
+    strip, square = RADIUS * columns, RADIUS * RADIUS
+    place = lax.broadcasted_iota(jnp.int32, (1, LANES), 1)
+    level = place < strip
+    slot = place - strip
+    second = slot >= 2 * square
+    token = slot - jnp.where(second, 2 * square, 0)
+    later = token >= square
+    token = token - jnp.where(later, square, 0)
+    corner_row = by_radius(token)
+    row = jnp.where(level, lax.shift_right_logical(place, log2(columns)), corner_row)
+    column = jnp.where(level, place & (columns - 1), token - corner_row * RADIUS)
+    row = jnp.where(slot < 4 * square, row, 8 * sum(tile))
+    down = jnp.where(level, 1, jnp.where(second, 1, 0))
+    return moved(row, column, down, jnp.where(level, -1, jnp.where(later, 1, 0)), tile)
+
+
+def beside_kernel(head, tile, scale, qn, qdn, z0, z1, y0, *sums):
+    width = qn.shape[1]
+    ones = block_ones(math.gcd(width, WIDE), log2(head), 1.0 / head)
+    mask = near(*beside_places(tile), tile[1], qn.shape[0])
+
+    def part(array, at):
+        pieces = []
+        for ref in (z0, z1, y0):
+            size = ref.shape[0] // 4
+            pieces.append(ref[array * size : (array + 1) * size, at].astype(F32))
+        return jnp.concatenate(pieces, 0)
+
+    keys = wide_pairs(lambda at: (part(0, at), part(2, at)), width, ones)
+    items = [
+        (
+            qn[:, at], qdn[:, at], *keys[pair], filled(part(1, at)).astype(BF16),
+            filled(part(3, at)).astype(BF16), factors_of(scale, pair, head),
+        )
+        for pair, at in enumerate(pair_lanes(width))
+    ]
+    for at, parts in zip(pair_lanes(width), attend(items, mask, head)):
+        for before, after, piece in zip(sums[:4], sums[4:], parts):
+            after[:, at] = before[:, at] + piece
 
 
 def last_kernel(
-    head, tile, scale, qn, qdn, c0, c1, a, ce, l, b, weight, out, tangent, coarse, pooled
+    head, tile, scale, qn, qdn, y1, c0, c1, a, ce, l, b, weight, out, tangent, coarse, pooled
 ):
-    rows, columns = tile
-    count = rows * columns
-    ones = block_ones(LANES, log2(head), 1.0 / head)
+    _, columns = tile
+    count, width = qn.shape
+    ones = block_ones(math.gcd(width, WIDE), log2(head), 1.0 / head)
+    mask = near(*last_places(tile), columns, count)
     corner_rows = c0.shape[0]
     corner_keys = corner_rows // 4
-    band = -(-corner_keys // 32) * 32
-    row, column = corner_places(tile, band)
-    mask = near(row, column, columns, count)
+    size = y1.shape[0] // 4
     place = lax.broadcasted_iota(jnp.int32, (1, corner_rows), 1)
-    unpack = []
-    for array in range(4):
+    band = -(-2 * corner_keys // 8) * 8
+    own = pooled.shape[0] // 2
+
+    def part(array, at):
         slot = place - array * corner_keys
-        unpack.append(one_hot(band, slot, (slot >= 0) & (slot < corner_keys)))
-    own = pooled.shape[0] // 2
+        valid = (slot >= 0) & (slot < corner_keys)
+        corners = dot(one_hot(band, slot, valid), c0[:, at]) + dot(
+            one_hot(band, slot + corner_keys, valid), c1[:, at]
+        )
+        strip = y1[array * size : (array + 1) * size, at].astype(F32)
+        return jnp.concatenate([strip, corners], 0)
+
+    whole = slice(0, width)
+    values, value_drifts = (filled(part(array, whole)).astype(BF16) for array in (1, 3))
+    key_values, key_drifts = part(0, whole), part(2, whole)
+    keys = wide_pairs(lambda at: (key_values[:, at], key_drifts[:, at]), width, ones)
+    items = [
+        (
+            qn[:, at], qdn[:, at], *keys[pair], values[:, at], value_drifts[:, at],
+            factors_of(scale, pair, head),
+        )
+        for pair, at in enumerate(pair_lanes(width))
+    ]
     place = lax.broadcasted_iota(jnp.int32, (1, count), 1)
     block = lax.shift_right_logical(place, log2(columns) + log2(MERGE)) * (columns // MERGE)
     block = block + lax.shift_right_logical(place & (columns - 1), log2(MERGE))
     pool = one_hot(own, block, block >= 0) * jnp.asarray(1 / (MERGE * MERGE), BF16)
-
-    def body(pair, lanes):
-        def part(array, at):
-            return jnp.concatenate([dot(unpack[array], c[:, at]) for c in (c0, c1)], 0)
-
-        keys = head_pairs([(part(0, at), part(2, at)) for at in lanes], ones)
-        items = [
-            (
-                qn[:, at], qdn[:, at], *key, part(1, at).astype(BF16),
-                part(3, at).astype(BF16),
-                [scale[2 * (pair + i) + j] / head for j in range(2)],
-            )
-            for i, (at, key) in enumerate(zip(lanes, keys))
-        ]
-        for at, parts in zip(lanes, attend(items, mask, head)):
-            inverse = 1.0 / (l[:, at] + parts[2])
-            output = (a[:, at] + parts[0]) * inverse
-            moving = (ce[:, at] + parts[1]) * inverse - output * ((b[:, at] + parts[3]) * inverse)
-            output = output.astype(BF16)
-            moving = moving.astype(BF16)
-            out[:, :, at] = output.reshape(*tile, LANES)
-            tangent[:, :, at] = moving.reshape(*tile, LANES)
-            pooled[:own, at] = dot(pool, output)
-            pooled[own:, at] = dot(pool, moving)
-
-    each_group(qn.shape[1] // LANES, body)
+    for at, parts in zip(pair_lanes(width), attend(items, mask, head)):
+        inverse = 1.0 / pltpu.roll(l[:, at] + parts[2], head, 1)
+        lean = pltpu.roll(b[:, at] + parts[3], head, 1)
+        output = (a[:, at] + parts[0]) * inverse
+        moving = (ce[:, at] + parts[1]) * inverse - output * (lean * inverse)
+        output = output.astype(BF16)
+        moving = moving.astype(BF16)
+        out[:, :, at] = output.reshape(*tile, LANES)
+        tangent[:, :, at] = moving.reshape(*tile, LANES)
+        pooled[:own, at] = dot(pool, output)
+        pooled[own:, at] = dot(pool, moving)
     coarse[...] = dot(pooled[...].astype(BF16), weight[...]).astype(BF16)
 
 
@@ -550,18 +566,15 @@
     latest = jnp.maximum(index[0], index[1])
     earlier = jnp.minimum(index[0], index[1])
     halves = EMBED // 2
-    row = lax.broadcasted_iota(jnp.int32, (2 * EMBED, LANES), 0)
+    row = lax.broadcasted_iota(jnp.int32, (EMBED, LANES), 0)
     angular = jnp.exp2((row & (halves - 1)).astype(F32) * (4.0 / halves))
-    steps = jnp.where(row < EMBED, latest, latest - earlier).astype(F32) / STEPS
+    steps = jnp.where(row < halves, latest, latest - earlier).astype(F32) / STEPS
     angle = angular * steps
     cosine, sine = jnp.cos(angle), jnp.sin(angle)
-    even = (row & halves) == 0
-    feature = jnp.where(even, cosine, sine)
-    slope = jnp.where(even, -sine, cosine) * angular
-
-    @pl.loop(0, weight.shape[1] // LANES)
-    def _(step):
-        at = pl.ds(pl.multiple_of(step * LANES, LANES), LANES)
+    rise, fall = angular * cosine, -angular * sine
+    feature = jnp.concatenate([cosine[:halves], sine[:halves], cosine[halves:], sine[halves:]], 0)
+    slope = jnp.concatenate([fall[:halves], rise[:halves], fall[halves:], rise[halves:]], 0)
+    for at in pair_lanes(weight.shape[1]):
         block = weight[:, at]
         out[0:1, at] = jnp.sum(feature * block, axis=0, keepdims=True)
         out[1:2, at] = jnp.sum(slope * block, axis=0, keepdims=True)
@@ -571,7 +584,7 @@
     return jax.ShapeDtypeStruct(shape, dtype)
 
 
-def near_call(kernel, outs, args, smem_count=0, scratch=(), name=None, far_out=False):
+def near_call(kernel, outs, args, smem_count=0, scratch=(), far_out=False):
     def near_spec():
         return pl.BlockSpec(memory_space=pltpu.VMEM)
 
@@ -587,7 +600,6 @@
         out_shape=outs if far_out else [pltpu.VMEM(o.shape, o.dtype) for o in outs],
         scratch_shapes=list(scratch),
         compiler_params=pltpu.CompilerParams(vmem_limit_bytes=16 * 1024 * 1024),
-        name=name,
     )(*args)
 
 
@@ -612,25 +624,24 @@
     heads = fine_head_scale.shape[0]
     head = width // heads
     count = rows * columns
-    pairs = width // LANES
     tile = (rows, columns)
     strip = RADIUS * columns
     side_tokens = RADIUS * rows
-    band = 1 << (max(side_tokens, 16) - 1).bit_length()
     corner_rows = 8 * RADIUS * RADIUS
     blocks = (rows // MERGE, columns // MERGE)
     own = blocks[0] * blocks[1]
 
-    fields = (fine_key_rows, fine_value_rows, fine_key_tangent, fine_value_tangent)
     near = pl.BlockSpec(memory_space=pltpu.VMEM)
     messages = [pltpu.VMEM((4 * strip, width), BF16)] * 2
-    messages += [pltpu.VMEM((4 * band, width), BF16)] * 2
+    messages += [pltpu.VMEM((4 * side_tokens, width), BF16)] * 2
     y0, y1, z0, z1, *fine = pl.pallas_call(
         pack_kernel,
-        in_specs=[pl.BlockSpec(memory_space=pltpu.HBM)] * 6,
-        out_specs=[near] * 10,
-        out_shape=messages + [pltpu.VMEM(queries.shape, BF16)] * 6,
-        scratch_shapes=[pltpu.SemaphoreType.DMA((6,))],
+        in_specs=[pl.BlockSpec(memory_space=pltpu.HBM)] * 7,
+        out_specs=[near] * 10 + [pl.BlockSpec(memory_space=pltpu.SMEM)],
+        out_shape=messages
+        + [pltpu.VMEM(queries.shape, BF16)] * 6
+        + [pltpu.SMEM(fine_head_scale.shape, F32)],
+        scratch_shapes=[pltpu.SemaphoreType.DMA((7,))],
         compiler_params=pltpu.CompilerParams(vmem_limit_bytes=16 * 1024 * 1024),
         name="pack",
     )(
@@ -638,18 +649,17 @@
             pltpu.with_memory_space_constraint(field, pltpu.HBM)
             for field in (
                 fine_key_rows, fine_value_rows, fine_key_tangent, fine_value_tangent,
-                queries, fine_query_tangent,
+                queries, fine_query_tangent, fine_head_scale,
             )
         )
     )
-    key, value, key_drift, value_drift, query, query_drift = fine
-    down_count, across_count = lax.axis_size("ty"), lax.axis_size("tx")
-    y0, y1 = (
-        lax.ppermute(y, "ty", couples(down_count, phase)) for phase, y in enumerate((y0, y1))
-    )
-    z0, z1 = (
-        lax.ppermute(z, "tx", couples(across_count, phase)) for phase, z in enumerate((z0, z1))
-    )
+    key, value, key_drift, value_drift, query, query_drift, scale = fine
+    scale = pltpu.with_memory_space_constraint(scale, pltpu.SMEM)
+    across_count = lax.axis_size("tx")
+    y1 = exchanged(y1, "ty", 1)
+    z0 = exchanged(z0, "tx", 0)
+    z1 = exchanged(z1, "tx", 1)
+    y0 = exchanged(y0, "ty", 0)
 
     flat = struct((count, width))
     sums = [struct((count, width), F32)] * 4
@@ -657,25 +667,20 @@
         functools.partial(own_kernel, head),
         [flat] * 2 + sums,
         (
-            fine_head_scale, query, query_drift, key, key_drift, value, value_drift,
+            scale, query, query_drift, key, key_drift, value, value_drift,
         ),
         1,
-        name="own_attention",
     )
     z0, z1, qn = lax.optimization_barrier((z0, z1, qn))
     corner = struct((corner_rows, width))
-    c0, c1 = near_call(
-        functools.partial(corner_kernel, rows), [corner] * 2, (z0, z1), name="corners"
-    )
-    c0, c1 = (
-        lax.ppermute(c, "ty", couples(down_count, phase)) for phase, c in enumerate((c0, c1))
-    )
-    strip_sums = near_call(
-        functools.partial(strip_kernel, head, tile),
+    c0, c1 = near_call(functools.partial(corner_kernel, rows), [corner] * 2, (z0, z1))
+    c1 = exchanged(c1, "ty", 1)
+    c0 = exchanged(c0, "ty", 0)
+    beside_sums = near_call(
+        functools.partial(beside_kernel, head, tile),
         sums,
-        (fine_head_scale, qn, qdn, z0, z1, y0, y1, *own_sums),
+        (scale, qn, qdn, z0, z1, y0, *own_sums),
         1,
-        name="strip_attention",
     )
     grid_shape = struct(queries.shape)
     pooled = struct((2 * own, width))
@@ -683,11 +688,10 @@
         functools.partial(last_kernel, head, tile),
         [grid_shape] * 2 + [pooled],
         (
-            fine_head_scale, qn, qdn, c0, c1, *strip_sums, merged_token_weight,
+            scale, qn, qdn, y1, c0, c1, *beside_sums, merged_token_weight,
         ),
         1,
         [pltpu.VMEM((2 * own, width), F32)],
-        name="last_attention",
     )
 
     (mod,) = near_call(
@@ -695,7 +699,6 @@
         [struct((2, 4 * width), F32)],
         (time_plan_index, time_modulation_weight),
         1,
-        name="modulation",
     )
     near_heads = coarse_head_scale.shape[0]
     span = near_heads * head
@@ -707,7 +710,6 @@
         functools.partial(project_kernel, head, slots),
         [struct((group, 2 * span)), struct((group, 4 * span))],
         (mod, packed, *tokens),
-        name="project",
     )
     key_blocks = row_gathered(keys, "ty")
     pieces = [struct((2 * own, width), F32)] + [struct((2 * own, width))] * (slots - 1)
@@ -716,25 +718,21 @@
         pieces,
         (coarse_head_scale, head_output_weight.reshape(span, width), query, *key_blocks),
         1,
-        name="coarse_attention",
     )
     updated, source = near_call(
         functools.partial(update_kernel, slots),
         [struct((2 * own, width), F32), struct((2 * own, width))],
         (mod, coarse, kept, *returned(sent, "tx")),
-        name="update",
     )
     kept, *sent = near_call(
         functools.partial(mlp_kernel, slots),
         pieces,
         (up_projection_weight, down_projection_weight, *gathered(source, "tx")),
-        name="mlp",
     )
     coarse_out, coarse_tangent = near_call(
         functools.partial(final_kernel, slots),
         [struct((*blocks, width))] * 2,
         (updated, kept, *returned(sent, "tx")),
-        name="final",
         far_out=True,
     )
     return (fine_out, fine_tangent, coarse_out, coarse_tangent)

time: 75.6 us -> 73.5 us (0.972)
  Pallas kernels: 19 us -> 13.4 us
  starting transfers between devices: 36 us -> 39.1 us
  waiting for transfers between devices: 17.4 us -> 18.5 us
    pallas_call x10, Pallas kernels: 17.1 us -> 11.5 us  [near_call(): pl.pallas_call(kernel, in_specs=[pl.BlockSpec(memory_space=pltpu.SMEM)] *...]
    ppermute x6, waiting for transfers between devices: 3.89 us -> 7.16 us  [gathered(): lax.ppermute(value, axis, partner(count, step))]
    ppermute x6, waiting for transfers between devices: 7.19 us -> 5.14 us  [returned(): lax.ppermute(piece, axis, partner(count, step, True))]
    ppermute x3, starting transfers between devices: 8.82 us -> 10.6 us  [row_gathered(): lax.ppermute(value, axis, partner(count, step))]
    ppermute x6, starting transfers between devices: 11.3 us -> 12.2 us  [gathered(): lax.ppermute(value, axis, partner(count, step))]
    unnamed x23 -> x21, local copies, waits for them, and re-layouts: 2.11 us -> 1.46 us
  transfers between devices with their start and end apart: 22 -> 22, of which waited for: 10 -> 11; matrix products, arithmetic and copies ran while one was open for 2% -> 2% of each run, Pallas kernels for 13% -> 7%
where the time goes in v3:
time: 73.5 us; the launch traced here: 73.3 us
  starting transfers between devices  39.1 us (53%)
  waiting for transfers between devices  18.5 us (25%)
  Pallas kernels  13.4 us (18%)
  local copies, waits for them, and re-layouts  1.47 us (2%)
  between operations  0.86 us (1%)
    ppermute x6, starting transfers between devices, gathered(): lax.ppermute(value, axis, partner(count, step))  12.2 us
    pallas_call x10, Pallas kernels, near_call(): pl.pallas_call(kernel, in_specs=[pl.BlockSpec(memory_space=pltpu.SMEM)] *...  11.5 us
    ppermute x3, starting transfers between devices, row_gathered(): lax.ppermute(value, axis, partner(count, step))  10.6 us
    ppermute x6, starting transfers between devices, returned(): lax.ppermute(piece, axis, partner(count, step, True))  8.89 us
    ppermute x6, starting transfers between devices, exchanged(): return lax.ppermute(value, axis, couples(lax.axis_size(axis), phase))  7.39 us
    ppermute x6, waiting for transfers between devices, gathered(): lax.ppermute(value, axis, partner(count, step))  7.16 us
    ppermute x6, waiting for transfers between devices, returned(): lax.ppermute(piece, axis, partner(count, step, True))  5.14 us
    ppermute x3, waiting for transfers between devices, row_gathered(): lax.ppermute(value, axis, partner(count, step))  3.75 us
  transfers between devices with their start and end apart: 22, of which 11 were waited for; matrix products, arithmetic and copies ran while one was open for 2% of the time, Pallas kernels for 7%

profile of v3, /device:TPU:0, one launch (start us, length us, event | category | flops | bytes accessed | tf_op | source)
XLA Modules:
  0.0 73.3 jit_solution(18136339068751668823)
XLA Ops:
  0.6 1.9 %pack.1 = (bf16[192,1024]{1,0:T(8,128)(2,1)S(1)}, bf16[192,1024]{1,0:T(8,128)(2,1)S(1)}, bf16[96,1024]{1,0:T(8,128)(2,1)S(1)}, bf16[96,1024]{1,0:T(8,128)(2,1)S(...) custom-call(bf16[8,16,1024]{2,1,0:T(8,128)(2,1)} %key.1, ...), custom_call_target="tpu_custom_call" | custom-call | tf_op jit(solution)/shard_map/pack/pallas_call | solution.py:637
  3.8 2.6 %collective-permute-start = (bf16[96,1024]{1,0:T(8,128)(2,1)S(1)}, bf16[96,1024]{1,0:T(8,128)(2,1)S(1)}, u32[]{:S(2)}, u32[]{:S(2)}) collective-permute-start(bf16[96,1024]{1,0:T(8,128)(2,1)S(1)} %get-tuple-element.48), channel_id=1, source_target_pairs={{0,1},{1,0},{2,3},{3,2},{4,5},{5,4},{6,7},{7,6},{8,9},{9,8},{10,11... | collective-permute-start | bytes 589832 | tf_op jit(solution)/shard_map/ppermute | solution.py:95
  7.1 2.1 %shard_map.174 = (bf16[128,1024]{1,0:T(8,128)(2,1)S(1)}, bf16[128,1024]{1,0:T(8,128)(2,1)S(1)}, f32[128,1024]{1,0:T(8,128)S(1)}, f32[128,1024]{1,0:T(8,128)S(1)}...) custom-call(f32[16]{0:T(128)S(4)} %get-tuple-element.47.scale, bf16[8,16,1024]{2,1,0:T(8,128)(2,1)S(1)} %get-tuple-element.50.q, ...), custom_call_target="tpu_custom_call" | custom-call | tf_op jit(solution)/shard_map/pallas_call | solution.py:595
  9.2 0.9 %collective-permute-done.z0 = bf16[96,1024]{1,0:T(8,128)(2,1)S(1)} collective-permute-done((bf16[96,1024]{1,0:T(8,128)(2,1)S(1)}, bf16[96,1024]{1,0:T(8,128)(2,1)S(1)}, u32[]{:S(2)}, u32[]{:S(2)}) %collective-permute-start) | collective-permute-done | bytes 196640 | tf_op jit(solution)/shard_map/ppermute | solution.py:95
  10.4 2.2 %collective-permute-start.3 = (bf16[72,1024]{1,0:T(8,128)(2,1)S(1)}, bf16[72,1024]{1,0:T(8,128)(2,1)S(1)}, u32[]{:S(2)}, u32[]{:S(2)}) collective-permute-start(bf16[72,1024]{1,0:T(8,128)(2,1)S(1)} %get-tuple-element.62), channel_id=1, source_target_pairs={{0,4},{4,0},{8,12},{12,8},{16,20},{20,16},{24,28},{28,24},{1,5},{5... | collective-permute-start | bytes 442376 | tf_op jit(solution)/shard_map/ppermute | solution.py:95
  13.3 1.5 %shard_map.176 = (f32[128,1024]{1,0:T(8,128)S(1)}, f32[128,1024]{1,0:T(8,128)S(1)}, f32[128,1024]{1,0:T(8,128)S(1)}, f32[128,1024]{1,0:T(8,128)S(1)}) custom-call(f32[16]{0:T(128)S(4)} %get-tuple-element.47.scale, bf16[128,1024]{1,0:T(8,128)(2,1)S(1)} %get-tuple-element.57.qn, bf16[128,1024]{1,0:T(8,128)(2,1)S(1)} %get-tuple-element.58.qdn, ...), custom_call_target="tpu_custom_call" | custom-call | tf_op jit(solution)/shard_map/pallas_call | solution.py:595
  14.9 2.2 %shard_map.177 = (bf16[8,16,1024]{2,1,0:T(8,128)(2,1)S(1)}, bf16[8,16,1024]{2,1,0:T(8,128)(2,1)S(1)}, bf16[16,1024]{1,0:T(8,128)(2,1)S(1)}) custom-call(f32[16]{0:T(128)S(4)} %get-tuple-element.47.scale, bf16[128,1024]{1,0:T(8,128)(2,1)S(1)} %get-tuple-element.57.qn, bf16[128,1024]{1,0:T(8,128)(2,1)S(1)} %get-tuple-element.58.qdn, ...), custom_call_target="tpu_custom_call" | custom-call | tf_op jit(solution)/shard_map/pallas_call | solution.py:595
  17.1 4.9 %collective-permute-start.6 = (bf16[16,1024]{1,0:T(8,128)(2,1)S(1)}, bf16[16,1024]{1,0:T(8,128)(2,1)S(1)}, u32[]{:S(2)}, u32[]{:S(2)}) collective-permute-start(bf16[16,1024]{1,0:T(8,128)(2,1)S(1)} %get-tuple-element.75.refs_0_.coarse), channel_id=1, source_target_pairs={{0,1},{1,0},{2,3},{3,2},{4,5},{5,4},{6,7},{7,6},{8,9},{9,8},{10,11... | collective-permute-start | bytes 98312 | tf_op jit(solution)/shard_map/ppermute | solution.py:107
  21.9 1.5 %collective-permute-start.7 = (bf16[16,1024]{1,0:T(8,128)(2,1)S(1)}, bf16[16,1024]{1,0:T(8,128)(2,1)S(1)}, u32[]{:S(2)}, u32[]{:S(2)}) collective-permute-start(bf16[16,1024]{1,0:T(8,128)(2,1)S(1)} %get-tuple-element.75.refs_0_.coarse), channel_id=1, source_target_pairs={{0,2},{1,3},{2,0},{3,1},{4,6},{5,7},{6,4},{7,5},{8,10},{9,11},{10,... | collective-permute-start | bytes 98312 | tf_op jit(solution)/shard_map/ppermute | solution.py:107
  23.5 1.4 %collective-permute-start.8 = (bf16[16,1024]{1,0:T(8,128)(2,1)S(1)}, bf16[16,1024]{1,0:T(8,128)(2,1)S(1)}, u32[]{:S(2)}, u32[]{:S(2)}) collective-permute-start(bf16[16,1024]{1,0:T(8,128)(2,1)S(1)} %get-tuple-element.75.refs_0_.coarse), channel_id=1, source_target_pairs={{0,3},{1,2},{2,1},{3,0},{4,7},{5,6},{6,5},{7,4},{8,11},{9,10},{10,... | collective-permute-start | bytes 98312 | tf_op jit(solution)/shard_map/ppermute | solution.py:107
  24.9 1.4 %shard_map.178.mod = f32[2,4096]{1,0:T(2,128)S(1)} custom-call(s32[2]{0:T(128)S(1)} %copy-done.6, f32[256,4096]{1,0:T(8,128)S(1)} %copy-done), custom_call_target="tpu_custom_call" | custom-call | tf_op jit(solution)/shard_map/pallas_call | solution.py:595
  26.8 2.4 %collective-permute-done.8.refs_3_ = bf16[16,1024]{1,0:T(8,128)(2,1)S(1)} collective-permute-done((bf16[16,1024]{1,0:T(8,128)(2,1)S(1)}, bf16[16,1024]{1,0:T(8,128)(2,1)S(1)}, u32[]{:S(2)}, u32[]{:S(2)}) %collective-permute-start.8) | collective-permute-done | bytes 32800 | tf_op jit(solution)/shard_map/ppermute | solution.py:107
  29.2 1.1 %shard_map.179 = (bf16[32,512]{1,0:T(8,128)(2,1)S(1)}, bf16[32,1024]{1,0:T(8,128)(2,1)S(1)}) custom-call(f32[2,4096]{1,0:T(2,128)S(1)} %shard_map.178.mod, bf16[768,1024]{1,0:T(8,128)(2,1)S(1)} %bitcast.4, bf16[16,1024]{1,0:T(8,128)(2,1)S(1)} %get-tuple-element.75.refs_0_.coarse, bf16[16,1024]{1,0:T(8,128)(2,1)S(1)} %collective-permute-done.6.refs_1_, ...), custom_call_target="tpu_custom_call" | custom-call | tf_op jit(solution)/shard_map/pallas_call | solution.py:595
  30.2 7.9 %collective-permute-start.9 = (bf16[32,1024]{1,0:T(8,128)(2,1)S(1)}, bf16[32,1024]{1,0:T(8,128)(2,1)S(1)}, u32[]{:S(2)}, u32[]{:S(2)}) collective-permute-start(bf16[32,1024]{1,0:T(8,128)(2,1)S(1)} %get-tuple-element.77), channel_id=1, source_target_pairs={{0,8},{4,12},{8,0},{12,4},{16,24},{20,28},{24,16},{28,20},{1,9},{5... | collective-permute-start | bytes 196616 | tf_op jit(solution)/shard_map/ppermute | solution.py:116
  38.1 1.4 %collective-permute-start.10 = (bf16[32,1024]{1,0:T(8,128)(2,1)S(1)}, bf16[32,1024]{1,0:T(8,128)(2,1)S(1)}, u32[]{:S(2)}, u32[]{:S(2)}) collective-permute-start(bf16[32,1024]{1,0:T(8,128)(2,1)S(1)} %get-tuple-element.77), channel_id=1, source_target_pairs={{0,16},{4,20},{8,24},{12,28},{16,0},{20,4},{24,8},{28,12},{1,17},{... | collective-permute-start | bytes 196616 | tf_op jit(solution)/shard_map/ppermute | solution.py:116
  39.5 1.4 %collective-permute-start.11 = (bf16[32,1024]{1,0:T(8,128)(2,1)S(1)}, bf16[32,1024]{1,0:T(8,128)(2,1)S(1)}, u32[]{:S(2)}, u32[]{:S(2)}) collective-permute-start(bf16[32,1024]{1,0:T(8,128)(2,1)S(1)} %get-tuple-element.77), channel_id=1, source_target_pairs={{0,24},{4,28},{8,16},{12,20},{16,8},{20,12},{24,0},{28,4},{1,25},{... | collective-permute-start | bytes 196616 | tf_op jit(solution)/shard_map/ppermute | solution.py:116
  40.9 1.9 %collective-permute-done.10 = bf16[32,1024]{1,0:T(8,128)(2,1)S(1)} collective-permute-done((bf16[32,1024]{1,0:T(8,128)(2,1)S(1)}, bf16[32,1024]{1,0:T(8,128)(2,1)S(1)}, u32[]{:S(2)}, u32[]{:S(2)}) %collective-permute-start.10) | collective-permute-done | bytes 65568 | tf_op jit(solution)/shard_map/ppermute | solution.py:116
  42.7 1.9 %collective-permute-done.11 = bf16[32,1024]{1,0:T(8,128)(2,1)S(1)} collective-permute-done((bf16[32,1024]{1,0:T(8,128)(2,1)S(1)}, bf16[32,1024]{1,0:T(8,128)(2,1)S(1)}, u32[]{:S(2)}, u32[]{:S(2)}) %collective-permute-start.11) | collective-permute-done | bytes 65568 | tf_op jit(solution)/shard_map/ppermute | solution.py:116
  44.6 1.5 %collective-permute-done.12.refs_1_ = bf16[128,1024]{1,0:T(8,128)(2,1)S(1)} collective-permute-done((bf16[128,1024]{1,0:T(8,128)(2,1)S(1)}, bf16[128,1024]{1,0:T(8,128)(2,1)S(1)}, u32[]{:S(2)}, u32[]{:S(2)}) %collective-permute-start.12) | collective-permute-done | bytes 262176 | tf_op jit(solution)/shard_map/ppermute | solution.py:119
  46.2 1.2 %shard_map.180 = (f32[16,1024]{1,0:T(8,128)S(1)}, bf16[16,1024]{1,0:T(8,128)(2,1)S(1)}, bf16[16,1024]{1,0:T(8,128)(2,1)S(1)}, bf16[16,1024]{1,0:T(8,128)(2,1)S(1)}) custom-call(f32[4]{0:T(128)S(1)} %copy-done.7, bf16[256,1024]{1,0:T(8,128)(2,1)S(1)} %bitcast.5, bf16[32,512]{1,0:T(8,128)(2,1)S(1)} %get-tuple-element.76.query, ...), custom_call_target="tpu_custom_call" | custom-call | tf_op jit(solution)/shard_map/pallas_call | solution.py:595
  47.6 1.8 %collective-permute-start.14 = (bf16[16,1024]{1,0:T(8,128)(2,1)S(1)}, bf16[16,1024]{1,0:T(8,128)(2,1)S(1)}, u32[]{:S(2)}, u32[]{:S(2)}) collective-permute-start(bf16[16,1024]{1,0:T(8,128)(2,1)S(1)} %get-tuple-element.80), channel_id=1, source_target_pairs={{0,2},{1,3},{2,0},{3,1},{4,6},{5,7},{6,4},{7,5},{8,10},{9,11},{10,... | collective-permute-start | bytes 98312 | tf_op jit(solution)/shard_map/ppermute | solution.py:125
  49.4 2.4 %collective-permute-start.15 = (bf16[16,1024]{1,0:T(8,128)(2,1)S(1)}, bf16[16,1024]{1,0:T(8,128)(2,1)S(1)}, u32[]{:S(2)}, u32[]{:S(2)}) collective-permute-start(bf16[16,1024]{1,0:T(8,128)(2,1)S(1)} %get-tuple-element.81), channel_id=1, source_target_pairs={{0,3},{1,2},{2,1},{3,0},{4,7},{5,6},{6,5},{7,4},{8,11},{9,10},{10,... | collective-permute-start | bytes 98312 | tf_op jit(solution)/shard_map/ppermute | solution.py:125
  51.8 0.9 %collective-permute-done.14.refs_2_ = bf16[16,1024]{1,0:T(8,128)(2,1)S(1)} collective-permute-done((bf16[16,1024]{1,0:T(8,128)(2,1)S(1)}, bf16[16,1024]{1,0:T(8,128)(2,1)S(1)}, u32[]{:S(2)}, u32[]{:S(2)}) %collective-permute-start.14) | collective-permute-done | bytes 32800 | tf_op jit(solution)/shard_map/ppermute | solution.py:125
  52.7 2.3 %collective-permute-done.15.refs_3_ = bf16[16,1024]{1,0:T(8,128)(2,1)S(1)} collective-permute-done((bf16[16,1024]{1,0:T(8,128)(2,1)S(1)}, bf16[16,1024]{1,0:T(8,128)(2,1)S(1)}, u32[]{:S(2)}, u32[]{:S(2)}) %collective-permute-start.15) | collective-permute-done | bytes 32800 | tf_op jit(solution)/shard_map/ppermute | solution.py:125
  55.4 3.0 %collective-permute-start.17 = (bf16[16,1024]{1,0:T(8,128)(2,1)S(1)}, bf16[16,1024]{1,0:T(8,128)(2,1)S(1)}, u32[]{:S(2)}, u32[]{:S(2)}) collective-permute-start(bf16[16,1024]{1,0:T(8,128)(2,1)S(1)} %get-tuple-element.83.refs_0_), channel_id=1, source_target_pairs={{0,2},{1,3},{2,0},{3,1},{4,6},{5,7},{6,4},{7,5},{8,10},{9,11},{10,... | collective-permute-start | bytes 98312 | tf_op jit(solution)/shard_map/ppermute | solution.py:107
  58.3 1.4 %collective-permute-start.18 = (bf16[16,1024]{1,0:T(8,128)(2,1)S(1)}, bf16[16,1024]{1,0:T(8,128)(2,1)S(1)}, u32[]{:S(2)}, u32[]{:S(2)}) collective-permute-start(bf16[16,1024]{1,0:T(8,128)(2,1)S(1)} %get-tuple-element.83.refs_0_), channel_id=1, source_target_pairs={{0,3},{1,2},{2,1},{3,0},{4,7},{5,6},{6,5},{7,4},{8,11},{9,10},{10,... | collective-permute-start | bytes 98312 | tf_op jit(solution)/shard_map/ppermute | solution.py:107
  60.2 3.8 %collective-permute-done.18.refs_3_ = bf16[16,1024]{1,0:T(8,128)(2,1)S(1)} collective-permute-done((bf16[16,1024]{1,0:T(8,128)(2,1)S(1)}, bf16[16,1024]{1,0:T(8,128)(2,1)S(1)}, u32[]{:S(2)}, u32[]{:S(2)}) %collective-permute-start.18) | collective-permute-done | bytes 32800 | tf_op jit(solution)/shard_map/ppermute | solution.py:107
  64.1 0.9 %shard_map.182 = (f32[16,1024]{1,0:T(8,128)S(1)}, bf16[16,1024]{1,0:T(8,128)(2,1)S(1)}, bf16[16,1024]{1,0:T(8,128)(2,1)S(1)}, bf16[16,1024]{1,0:T(8,128)(2,1)S(1)}) custom-call(bf16[1024,1024]{1,0:T(8,128)(2,1)S(1)} %copy-done.2, bf16[1024,1024]{1,0:T(8,128)(2,1)S(1)} %copy-done.3, bf16[16,1024]{1,0:T(8,128)(2,1)S(1)} %get-tuple-element.83.refs_0_, ...), custom_call_target="tpu_custom_call" | custom-call | tf_op jit(solution)/shard_map/pallas_call | solution.py:595
  65.0 1.9 %collective-permute-start.20 = (bf16[16,1024]{1,0:T(8,128)(2,1)S(1)}, bf16[16,1024]{1,0:T(8,128)(2,1)S(1)}, u32[]{:S(2)}, u32[]{:S(2)}) collective-permute-start(bf16[16,1024]{1,0:T(8,128)(2,1)S(1)} %get-tuple-element.86), channel_id=1, source_target_pairs={{0,2},{1,3},{2,0},{3,1},{4,6},{5,7},{6,4},{7,5},{8,10},{9,11},{10,... | collective-permute-start | bytes 98312 | tf_op jit(solution)/shard_map/ppermute | solution.py:125
  67.0 2.4 %collective-permute-start.21 = (bf16[16,1024]{1,0:T(8,128)(2,1)S(1)}, bf16[16,1024]{1,0:T(8,128)(2,1)S(1)}, u32[]{:S(2)}, u32[]{:S(2)}) collective-permute-start(bf16[16,1024]{1,0:T(8,128)(2,1)S(1)} %get-tuple-element.87), channel_id=1, source_target_pairs={{0,3},{1,2},{2,1},{3,0},{4,7},{5,6},{6,5},{7,4},{8,11},{9,10},{10,... | collective-permute-start | bytes 98312 | tf_op jit(solution)/shard_map/ppermute | solution.py:125
  69.4 0.7 copy.22
  70.8 1.9 %collective-permute-done.21.refs_3_ = bf16[16,1024]{1,0:T(8,128)(2,1)S(1)} collective-permute-done((bf16[16,1024]{1,0:T(8,128)(2,1)S(1)}, bf16[16,1024]{1,0:T(8,128)(2,1)S(1)}, u32[]{:S(2)}, u32[]{:S(2)}) %collective-permute-start.21) | collective-permute-done | bytes 32800 | tf_op jit(solution)/shard_map/ppermute | solution.py:125
  (45 shorter events, 5.8 us)
Async XLA Ops:
  2.5 10.7 %collective-permute-start.5 = (bf16[192,1024]{1,0:T(8,128)(2,1)S(1)}, bf16[192,1024]{1,0:T(8,128)(2,1)S(1)}, u32[]{:S(2)}, u32[]{:S(2)}) collective-permute-start(bf16[192,1024]{1,0:T(8,128)(2,1)S(1)} %get-tuple-element.64), channel_id=1, source_target_pairs={{0,4},{4,0},{8,12},{12,8},{16,20},{20,16},{24,28},{28,24},{1,5},{5... | collective-permute-start | bytes 1179656 | tf_op jit(solution)/shard_map/ppermute | solution.py:95
  3.1 11.7 %collective-permute-start.2 = (bf16[192,1024]{1,0:T(8,128)(2,1)S(1)}, bf16[192,1024]{1,0:T(8,128)(2,1)S(1)}, u32[]{:S(2)}, u32[]{:S(2)}) collective-permute-start(bf16[192,1024]{1,0:T(8,128)(2,1)S(1)} %get-tuple-element.59), channel_id=1, source_target_pairs={{4,8},{8,4},{12,16},{16,12},{20,24},{24,20},{5,9},{9,5},{13,17},{1... | collective-permute-start | bytes 1179656 | tf_op jit(solution)/shard_map/ppermute | solution.py:95
  3.8 6.3 %collective-permute-start = (bf16[96,1024]{1,0:T(8,128)(2,1)S(1)}, bf16[96,1024]{1,0:T(8,128)(2,1)S(1)}, u32[]{:S(2)}, u32[]{:S(2)}) collective-permute-start(bf16[96,1024]{1,0:T(8,128)(2,1)S(1)} %get-tuple-element.48), channel_id=1, source_target_pairs={{0,1},{1,0},{2,3},{3,2},{4,5},{5,4},{6,7},{7,6},{8,9},{9,8},{10,11... | collective-permute-start | bytes 589832 | tf_op jit(solution)/shard_map/ppermute | solution.py:95
  6.4 3.7 %collective-permute-start.1 = (bf16[96,1024]{1,0:T(8,128)(2,1)S(1)}, bf16[96,1024]{1,0:T(8,128)(2,1)S(1)}, u32[]{:S(2)}, u32[]{:S(2)}) collective-permute-start(bf16[96,1024]{1,0:T(8,128)(2,1)S(1)} %get-tuple-element.49), channel_id=1, source_target_pairs={{1,2},{2,1},{5,6},{6,5},{9,10},{10,9},{13,14},{14,13},{17,18},{18,... | collective-permute-start | bytes 589832 | tf_op jit(solution)/shard_map/ppermute | solution.py:95
  9.2 5.7 %copy-start.1 = (bf16[1024,1024]{1,0:T(8,128)(2,1)S(1)}, bf16[1024,1024]{1,0:T(8,128)(2,1)}, u32[]{:S(2)}) copy-start(bf16[1024,1024]{1,0:T(8,128)(2,1)} %weight.2) | copy-start | bytes 6291460
  10.4 4.4 %collective-permute-start.3 = (bf16[72,1024]{1,0:T(8,128)(2,1)S(1)}, bf16[72,1024]{1,0:T(8,128)(2,1)S(1)}, u32[]{:S(2)}, u32[]{:S(2)}) collective-permute-start(bf16[72,1024]{1,0:T(8,128)(2,1)S(1)} %get-tuple-element.62), channel_id=1, source_target_pairs={{0,4},{4,0},{8,12},{12,8},{16,20},{20,16},{24,28},{28,24},{1,5},{5... | collective-permute-start | bytes 442376 | tf_op jit(solution)/shard_map/ppermute | solution.py:95
  12.6 2.2 %collective-permute-start.4 = (bf16[72,1024]{1,0:T(8,128)(2,1)S(1)}, bf16[72,1024]{1,0:T(8,128)(2,1)S(1)}, u32[]{:S(2)}, u32[]{:S(2)}) collective-permute-start(bf16[72,1024]{1,0:T(8,128)(2,1)S(1)} %get-tuple-element.63), channel_id=1, source_target_pairs={{4,8},{8,4},{12,16},{16,12},{20,24},{24,20},{5,9},{9,5},{13,17},{1... | collective-permute-start | bytes 442376 | tf_op jit(solution)/shard_map/ppermute | solution.py:95
  14.9 10.0 %copy-start = (f32[256,4096]{1,0:T(8,128)S(1)}, f32[256,4096]{1,0:T(8,128)}, u32[]{:S(2)}) copy-start(f32[256,4096]{1,0:T(8,128)} %weight.3) | copy-start | bytes 12582916
  14.9 10.0 %copy-start.6 = (s32[2]{0:T(128)S(1)}, s32[2]{0:T(128)}, u32[]{:S(2)}) copy-start(s32[2]{0:T(128)} %index.1) | copy-start | bytes 28
  17.1 12.1 %copy-start.4 = (bf16[1024,4,192]{0,2,1:T(8,128)(2,1)S(1)}, bf16[1024,4,192]{0,2,1:T(8,128)(2,1)}, u32[]{:S(2)}) copy-start(bf16[1024,4,192]{0,2,1:T(8,128)(2,1)} %param.25) | copy-start | bytes 4718596
  17.1 9.3 %collective-permute-start.6 = (bf16[16,1024]{1,0:T(8,128)(2,1)S(1)}, bf16[16,1024]{1,0:T(8,128)(2,1)S(1)}, u32[]{:S(2)}, u32[]{:S(2)}) collective-permute-start(bf16[16,1024]{1,0:T(8,128)(2,1)S(1)} %get-tuple-element.75.refs_0_.coarse), channel_id=1, source_target_pairs={{0,1},{1,0},{2,3},{3,2},{4,5},{5,4},{6,7},{7,6},{8,9},{9,8},{10,11... | collective-permute-start | bytes 98312 | tf_op jit(solution)/shard_map/ppermute | solution.py:107
  21.9 4.8 %collective-permute-start.7 = (bf16[16,1024]{1,0:T(8,128)(2,1)S(1)}, bf16[16,1024]{1,0:T(8,128)(2,1)S(1)}, u32[]{:S(2)}, u32[]{:S(2)}) collective-permute-start(bf16[16,1024]{1,0:T(8,128)(2,1)S(1)} %get-tuple-element.75.refs_0_.coarse), channel_id=1, source_target_pairs={{0,2},{1,3},{2,0},{3,1},{4,6},{5,7},{6,4},{7,5},{8,10},{9,11},{10,... | collective-permute-start | bytes 98312 | tf_op jit(solution)/shard_map/ppermute | solution.py:107
  23.5 5.7 %collective-permute-start.8 = (bf16[16,1024]{1,0:T(8,128)(2,1)S(1)}, bf16[16,1024]{1,0:T(8,128)(2,1)S(1)}, u32[]{:S(2)}, u32[]{:S(2)}) collective-permute-start(bf16[16,1024]{1,0:T(8,128)(2,1)S(1)} %get-tuple-element.75.refs_0_.coarse), channel_id=1, source_target_pairs={{0,3},{1,2},{2,1},{3,0},{4,7},{5,6},{6,5},{7,4},{8,11},{9,10},{10,... | collective-permute-start | bytes 98312 | tf_op jit(solution)/shard_map/ppermute | solution.py:107
  24.9 21.3 %copy-start.5 = (bf16[4,64,1024]{2,1,0:T(8,128)(2,1)S(1)}, bf16[4,64,1024]{2,1,0:T(8,128)(2,1)}, u32[]{:S(2)}) copy-start(bf16[4,64,1024]{2,1,0:T(8,128)(2,1)} %param.27) | copy-start | bytes 1572868
  24.9 39.2 %copy-start.3 = (bf16[1024,1024]{1,0:T(8,128)(2,1)S(1)}, bf16[1024,1024]{1,0:T(8,128)(2,1)}, u32[]{:S(2)}) copy-start(bf16[1024,1024]{1,0:T(8,128)(2,1)} %down.1) | copy-start | bytes 6291460
  26.3 19.9 %copy-start.7 = (f32[4]{0:T(128)S(1)}, f32[4]{0:T(128)}, u32[]{:S(2)}) copy-start(f32[4]{0:T(128)} %scale.3) | copy-start | bytes 52
  26.3 37.7 %copy-start.2 = (bf16[1024,1024]{1,0:T(8,128)(2,1)S(1)}, bf16[1024,1024]{1,0:T(8,128)(2,1)}, u32[]{:S(2)}) copy-start(bf16[1024,1024]{1,0:T(8,128)(2,1)} %up.1) | copy-start | bytes 6291460
  30.2 10.6 %collective-permute-start.9 = (bf16[32,1024]{1,0:T(8,128)(2,1)S(1)}, bf16[32,1024]{1,0:T(8,128)(2,1)S(1)}, u32[]{:S(2)}, u32[]{:S(2)}) collective-permute-start(bf16[32,1024]{1,0:T(8,128)(2,1)S(1)} %get-tuple-element.77), channel_id=1, source_target_pairs={{0,8},{4,12},{8,0},{12,4},{16,24},{20,28},{24,16},{28,20},{1,9},{5... | collective-permute-start | bytes 196616 | tf_op jit(solution)/shard_map/ppermute | solution.py:116
  38.1 4.6 %collective-permute-start.10 = (bf16[32,1024]{1,0:T(8,128)(2,1)S(1)}, bf16[32,1024]{1,0:T(8,128)(2,1)S(1)}, u32[]{:S(2)}, u32[]{:S(2)}) collective-permute-start(bf16[32,1024]{1,0:T(8,128)(2,1)S(1)} %get-tuple-element.77), channel_id=1, source_target_pairs={{0,16},{4,20},{8,24},{12,28},{16,0},{20,4},{24,8},{28,12},{1,17},{... | collective-permute-start | bytes 196616 | tf_op jit(solution)/shard_map/ppermute | solution.py:116
  39.5 5.2 %collective-permute-start.11 = (bf16[32,1024]{1,0:T(8,128)(2,1)S(1)}, bf16[32,1024]{1,0:T(8,128)(2,1)S(1)}, u32[]{:S(2)}, u32[]{:S(2)}) collective-permute-start(bf16[32,1024]{1,0:T(8,128)(2,1)S(1)} %get-tuple-element.77), channel_id=1, source_target_pairs={{0,24},{4,28},{8,16},{12,20},{16,8},{20,12},{24,0},{28,4},{1,25},{... | collective-permute-start | bytes 196616 | tf_op jit(solution)/shard_map/ppermute | solution.py:116
  44.6 1.5 %collective-permute-start.12 = (bf16[128,1024]{1,0:T(8,128)(2,1)S(1)}, bf16[128,1024]{1,0:T(8,128)(2,1)S(1)}, u32[]{:S(2)}, u32[]{:S(2)}) collective-permute-start(bf16[128,1024]{1,0:T(8,128)(2,1)S(1)} %constant_dynamic-update-slice_fusion.refs_0_), channel_id=1, source_target_pairs={{0,4},{4,0},{8,12},{12,8},{16,20},{20,16},{24,28},{28,24},{1,5},{5... | collective-permute-start | bytes 786440 | tf_op jit(solution)/shard_map/ppermute | solution.py:119
  47.4 4.5 %collective-permute-start.13 = (bf16[16,1024]{1,0:T(8,128)(2,1)S(1)}, bf16[16,1024]{1,0:T(8,128)(2,1)S(1)}, u32[]{:S(2)}, u32[]{:S(2)}) collective-permute-start(bf16[16,1024]{1,0:T(8,128)(2,1)S(1)} %get-tuple-element.79), channel_id=1, source_target_pairs={{0,1},{1,0},{2,3},{3,2},{4,5},{5,4},{6,7},{7,6},{8,9},{9,8},{10,11... | collective-permute-start | bytes 98312 | tf_op jit(solution)/shard_map/ppermute | solution.py:125
  47.6 5.2 %collective-permute-start.14 = (bf16[16,1024]{1,0:T(8,128)(2,1)S(1)}, bf16[16,1024]{1,0:T(8,128)(2,1)S(1)}, u32[]{:S(2)}, u32[]{:S(2)}) collective-permute-start(bf16[16,1024]{1,0:T(8,128)(2,1)S(1)} %get-tuple-element.80), channel_id=1, source_target_pairs={{0,2},{1,3},{2,0},{3,1},{4,6},{5,7},{6,4},{7,5},{8,10},{9,11},{10,... | collective-permute-start | bytes 98312 | tf_op jit(solution)/shard_map/ppermute | solution.py:125
  49.4 5.7 %collective-permute-start.15 = (bf16[16,1024]{1,0:T(8,128)(2,1)S(1)}, bf16[16,1024]{1,0:T(8,128)(2,1)S(1)}, u32[]{:S(2)}, u32[]{:S(2)}) collective-permute-start(bf16[16,1024]{1,0:T(8,128)(2,1)S(1)} %get-tuple-element.81), channel_id=1, source_target_pairs={{0,3},{1,2},{2,1},{3,0},{4,7},{5,6},{6,5},{7,4},{8,11},{9,10},{10,... | collective-permute-start | bytes 98312 | tf_op jit(solution)/shard_map/ppermute | solution.py:125
  55.3 4.5 %collective-permute-start.16 = (bf16[16,1024]{1,0:T(8,128)(2,1)S(1)}, bf16[16,1024]{1,0:T(8,128)(2,1)S(1)}, u32[]{:S(2)}, u32[]{:S(2)}) collective-permute-start(bf16[16,1024]{1,0:T(8,128)(2,1)S(1)} %get-tuple-element.83.refs_0_), channel_id=1, source_target_pairs={{0,1},{1,0},{2,3},{3,2},{4,5},{5,4},{6,7},{7,6},{8,9},{9,8},{10,11... | collective-permute-start | bytes 98312 | tf_op jit(solution)/shard_map/ppermute | solution.py:107
  55.4 4.9 %collective-permute-start.17 = (bf16[16,1024]{1,0:T(8,128)(2,1)S(1)}, bf16[16,1024]{1,0:T(8,128)(2,1)S(1)}, u32[]{:S(2)}, u32[]{:S(2)}) collective-permute-start(bf16[16,1024]{1,0:T(8,128)(2,1)S(1)} %get-tuple-element.83.refs_0_), channel_id=1, source_target_pairs={{0,2},{1,3},{2,0},{3,1},{4,6},{5,7},{6,4},{7,5},{8,10},{9,11},{10,... | collective-permute-start | bytes 98312 | tf_op jit(solution)/shard_map/ppermute | solution.py:107
  58.3 5.7 %collective-permute-start.18 = (bf16[16,1024]{1,0:T(8,128)(2,1)S(1)}, bf16[16,1024]{1,0:T(8,128)(2,1)S(1)}, u32[]{:S(2)}, u32[]{:S(2)}) collective-permute-start(bf16[16,1024]{1,0:T(8,128)(2,1)S(1)} %get-tuple-element.83.refs_0_), channel_id=1, source_target_pairs={{0,3},{1,2},{2,1},{3,0},{4,7},{5,6},{6,5},{7,4},{8,11},{9,10},{10,... | collective-permute-start | bytes 98312 | tf_op jit(solution)/shard_map/ppermute | solution.py:107
  65.0 5.9 %collective-permute-start.19 = (bf16[16,1024]{1,0:T(8,128)(2,1)S(1)}, bf16[16,1024]{1,0:T(8,128)(2,1)S(1)}, u32[]{:S(2)}, u32[]{:S(2)}) collective-permute-start(bf16[16,1024]{1,0:T(8,128)(2,1)S(1)} %get-tuple-element.85), channel_id=1, source_target_pairs={{0,1},{1,0},{2,3},{3,2},{4,5},{5,4},{6,7},{7,6},{8,9},{9,8},{10,11... | collective-permute-start | bytes 98312 | tf_op jit(solution)/shard_map/ppermute | solution.py:125
  65.0 5.8 %collective-permute-start.20 = (bf16[16,1024]{1,0:T(8,128)(2,1)S(1)}, bf16[16,1024]{1,0:T(8,128)(2,1)S(1)}, u32[]{:S(2)}, u32[]{:S(2)}) collective-permute-start(bf16[16,1024]{1,0:T(8,128)(2,1)S(1)} %get-tuple-element.86), channel_id=1, source_target_pairs={{0,2},{1,3},{2,0},{3,1},{4,6},{5,7},{6,4},{7,5},{8,10},{9,11},{10,... | collective-permute-start | bytes 98312 | tf_op jit(solution)/shard_map/ppermute | solution.py:125
  67.0 5.7 %collective-permute-start.21 = (bf16[16,1024]{1,0:T(8,128)(2,1)S(1)}, bf16[16,1024]{1,0:T(8,128)(2,1)S(1)}, u32[]{:S(2)}, u32[]{:S(2)}) collective-permute-start(bf16[16,1024]{1,0:T(8,128)(2,1)S(1)} %get-tuple-element.87), channel_id=1, source_target_pairs={{0,3},{1,2},{2,1},{3,0},{4,7},{5,6},{6,5},{7,4},{8,11},{9,10},{10,... | collective-permute-start | bytes 98312 | tf_op jit(solution)/shard_map/ppermute | solution.py:125

commit v4 on v3

--- a/solution.py
+++ b/solution.py
@@ -104,7 +104,7 @@
 def gathered(value, axis):
     count = lax.axis_size(axis)
     return [value] + [
-        lax.ppermute(value, axis, partner(count, step)) for step in range(1, count)
+        lax.ppermute(value, axis, partner(count, step)) for step in range(count - 1, 0, -1)
     ]
 
 
@@ -113,7 +113,7 @@
     if count < 4 or count & (count - 1):
         return gathered(value, axis)
     part = jnp.concatenate(
-        [value] + [lax.ppermute(value, axis, partner(count, step)) for step in range(2, count, 2)],
+        [value] + [lax.ppermute(value, axis, partner(count, step)) for step in range(count - 2, 0, -2)],
         0,
     )
     return [part, lax.ppermute(part, axis, partner(count, 1))]
@@ -123,7 +123,7 @@
     count = lax.axis_size(axis)
     return [
         lax.ppermute(piece, axis, partner(count, step, True))
-        for step, piece in zip(range(1, count), pieces)
+        for step, piece in zip(range(count - 1, 0, -1), pieces)
     ]
 
 

time: 73.5 us -> 68.5 us (0.932)
  waiting for transfers between devices: 18.5 us -> 14.1 us
    ppermute x6, waiting for transfers between devices: 7.16 us -> 4.69 us  [gathered(): lax.ppermute(value, axis, partner(count, step))]
    ppermute x6, waiting for transfers between devices: 5.14 us -> 4.08 us  [returned(): lax.ppermute(piece, axis, partner(count, step, True))]
    ppermute x6, starting transfers between devices: 12.2 us -> 11.3 us  [gathered(): lax.ppermute(value, axis, partner(count, step))]
    ppermute x3, waiting for transfers between devices: 3.75 us -> 2.91 us  [row_gathered(): lax.ppermute(value, axis, partner(count, step))]
  transfers between devices with their start and end apart: 22 -> 22, of which waited for: 11 -> 11; matrix products, arithmetic and copies ran while one was open for 2% -> 2% of each run, Pallas kernels for 7% -> 8%
where the time goes in v4:
time: 68.5 us; the launch traced here: 68.3 us
  starting transfers between devices  38.5 us (56%)
  waiting for transfers between devices  14.1 us (21%)
  Pallas kernels  13.4 us (20%)
  local copies, waits for them, and re-layouts  1.47 us (2%)
  between operations  0.85 us (1%)
    pallas_call x10, Pallas kernels, near_call(): pl.pallas_call(kernel, in_specs=[pl.BlockSpec(memory_space=pltpu.SMEM)] *...  11.5 us
    ppermute x6, starting transfers between devices, gathered(): lax.ppermute(value, axis, partner(count, step))  11.3 us
    ppermute x3, starting transfers between devices, row_gathered(): lax.ppermute(value, axis, partner(count, step))  10.9 us
    ppermute x6, starting transfers between devices, returned(): lax.ppermute(piece, axis, partner(count, step, True))  8.9 us
    ppermute x6, starting transfers between devices, exchanged(): return lax.ppermute(value, axis, couples(lax.axis_size(axis), phase))  7.39 us
    ppermute x6, waiting for transfers between devices, gathered(): lax.ppermute(value, axis, partner(count, step))  4.69 us
    ppermute x6, waiting for transfers between devices, returned(): lax.ppermute(piece, axis, partner(count, step, True))  4.08 us
    ppermute x3, waiting for transfers between devices, row_gathered(): lax.ppermute(value, axis, partner(count, step))  2.91 us
  transfers between devices with their start and end apart: 22, of which 11 were waited for; matrix products, arithmetic and copies ran while one was open for 2% of the time, Pallas kernels for 8%

profile of v4, /device:TPU:0, one launch (start us, length us, event | category | flops | bytes accessed | tf_op | source)
XLA Modules:
  0.0 68.3 jit_solution(8378179406517488895)
XLA Ops:
  0.6 1.9 %pack.1 = (bf16[192,1024]{1,0:T(8,128)(2,1)S(1)}, bf16[192,1024]{1,0:T(8,128)(2,1)S(1)}, bf16[96,1024]{1,0:T(8,128)(2,1)S(1)}, bf16[96,1024]{1,0:T(8,128)(2,1)S(...) custom-call(bf16[8,16,1024]{2,1,0:T(8,128)(2,1)} %key.1, ...), custom_call_target="tpu_custom_call" | custom-call | tf_op jit(solution)/shard_map/pack/pallas_call | solution.py:637
  3.8 2.6 %collective-permute-start = (bf16[96,1024]{1,0:T(8,128)(2,1)S(1)}, bf16[96,1024]{1,0:T(8,128)(2,1)S(1)}, u32[]{:S(2)}, u32[]{:S(2)}) collective-permute-start(bf16[96,1024]{1,0:T(8,128)(2,1)S(1)} %get-tuple-element.48), channel_id=1, source_target_pairs={{0,1},{1,0},{2,3},{3,2},{4,5},{5,4},{6,7},{7,6},{8,9},{9,8},{10,11... | collective-permute-start | bytes 589832 | tf_op jit(solution)/shard_map/ppermute | solution.py:95
  7.1 2.1 %shard_map.174 = (bf16[128,1024]{1,0:T(8,128)(2,1)S(1)}, bf16[128,1024]{1,0:T(8,128)(2,1)S(1)}, f32[128,1024]{1,0:T(8,128)S(1)}, f32[128,1024]{1,0:T(8,128)S(1)}...) custom-call(f32[16]{0:T(128)S(4)} %get-tuple-element.47.scale, bf16[8,16,1024]{2,1,0:T(8,128)(2,1)S(1)} %get-tuple-element.50.q, ...), custom_call_target="tpu_custom_call" | custom-call | tf_op jit(solution)/shard_map/pallas_call | solution.py:595
  9.2 0.9 %collective-permute-done.z0 = bf16[96,1024]{1,0:T(8,128)(2,1)S(1)} collective-permute-done((bf16[96,1024]{1,0:T(8,128)(2,1)S(1)}, bf16[96,1024]{1,0:T(8,128)(2,1)S(1)}, u32[]{:S(2)}, u32[]{:S(2)}) %collective-permute-start) | collective-permute-done | bytes 196640 | tf_op jit(solution)/shard_map/ppermute | solution.py:95
  10.4 2.2 %collective-permute-start.3 = (bf16[72,1024]{1,0:T(8,128)(2,1)S(1)}, bf16[72,1024]{1,0:T(8,128)(2,1)S(1)}, u32[]{:S(2)}, u32[]{:S(2)}) collective-permute-start(bf16[72,1024]{1,0:T(8,128)(2,1)S(1)} %get-tuple-element.62), channel_id=1, source_target_pairs={{0,4},{4,0},{8,12},{12,8},{16,20},{20,16},{24,28},{28,24},{1,5},{5... | collective-permute-start | bytes 442376 | tf_op jit(solution)/shard_map/ppermute | solution.py:95
  13.3 1.5 %shard_map.176 = (f32[128,1024]{1,0:T(8,128)S(1)}, f32[128,1024]{1,0:T(8,128)S(1)}, f32[128,1024]{1,0:T(8,128)S(1)}, f32[128,1024]{1,0:T(8,128)S(1)}) custom-call(f32[16]{0:T(128)S(4)} %get-tuple-element.47.scale, bf16[128,1024]{1,0:T(8,128)(2,1)S(1)} %get-tuple-element.57.qn, bf16[128,1024]{1,0:T(8,128)(2,1)S(1)} %get-tuple-element.58.qdn, ...), custom_call_target="tpu_custom_call" | custom-call | tf_op jit(solution)/shard_map/pallas_call | solution.py:595
  14.9 2.2 %shard_map.177 = (bf16[8,16,1024]{2,1,0:T(8,128)(2,1)S(1)}, bf16[8,16,1024]{2,1,0:T(8,128)(2,1)S(1)}, bf16[16,1024]{1,0:T(8,128)(2,1)S(1)}) custom-call(f32[16]{0:T(128)S(4)} %get-tuple-element.47.scale, bf16[128,1024]{1,0:T(8,128)(2,1)S(1)} %get-tuple-element.57.qn, bf16[128,1024]{1,0:T(8,128)(2,1)S(1)} %get-tuple-element.58.qdn, ...), custom_call_target="tpu_custom_call" | custom-call | tf_op jit(solution)/shard_map/pallas_call | solution.py:595
  17.1 3.9 %collective-permute-start.6 = (bf16[16,1024]{1,0:T(8,128)(2,1)S(1)}, bf16[16,1024]{1,0:T(8,128)(2,1)S(1)}, u32[]{:S(2)}, u32[]{:S(2)}) collective-permute-start(bf16[16,1024]{1,0:T(8,128)(2,1)S(1)} %get-tuple-element.75.refs_0_.coarse), channel_id=1, source_target_pairs={{0,3},{1,2},{2,1},{3,0},{4,7},{5,6},{6,5},{7,4},{8,11},{9,10},{10,... | collective-permute-start | bytes 98312 | tf_op jit(solution)/shard_map/ppermute | solution.py:107
  21.0 2.5 %collective-permute-start.7 = (bf16[16,1024]{1,0:T(8,128)(2,1)S(1)}, bf16[16,1024]{1,0:T(8,128)(2,1)S(1)}, u32[]{:S(2)}, u32[]{:S(2)}) collective-permute-start(bf16[16,1024]{1,0:T(8,128)(2,1)S(1)} %get-tuple-element.75.refs_0_.coarse), channel_id=1, source_target_pairs={{0,2},{1,3},{2,0},{3,1},{4,6},{5,7},{6,4},{7,5},{8,10},{9,11},{10,... | collective-permute-start | bytes 98312 | tf_op jit(solution)/shard_map/ppermute | solution.py:107
  24.0 1.4 %shard_map.178.mod = f32[2,4096]{1,0:T(2,128)S(1)} custom-call(s32[2]{0:T(128)S(1)} %copy-done.6, f32[256,4096]{1,0:T(8,128)S(1)} %copy-done), custom_call_target="tpu_custom_call" | custom-call | tf_op jit(solution)/shard_map/pallas_call | solution.py:595
  25.8 1.6 %collective-permute-done.8.refs_3_ = bf16[16,1024]{1,0:T(8,128)(2,1)S(1)} collective-permute-done((bf16[16,1024]{1,0:T(8,128)(2,1)S(1)}, bf16[16,1024]{1,0:T(8,128)(2,1)S(1)}, u32[]{:S(2)}, u32[]{:S(2)}) %collective-permute-start.8) | collective-permute-done | bytes 32800 | tf_op jit(solution)/shard_map/ppermute | solution.py:107
  27.4 1.1 %shard_map.179 = (bf16[32,512]{1,0:T(8,128)(2,1)S(1)}, bf16[32,1024]{1,0:T(8,128)(2,1)S(1)}) custom-call(f32[2,4096]{1,0:T(2,128)S(1)} %shard_map.178.mod, bf16[768,1024]{1,0:T(8,128)(2,1)S(1)} %bitcast.4, bf16[16,1024]{1,0:T(8,128)(2,1)S(1)} %get-tuple-element.75.refs_0_.coarse, bf16[16,1024]{1,0:T(8,128)(2,1)S(1)} %collective-permute-done.6.refs_1_, ...), custom_call_target="tpu_custom_call" | custom-call | tf_op jit(solution)/shard_map/pallas_call | solution.py:595
  28.4 7.6 %collective-permute-start.9 = (bf16[32,1024]{1,0:T(8,128)(2,1)S(1)}, bf16[32,1024]{1,0:T(8,128)(2,1)S(1)}, u32[]{:S(2)}, u32[]{:S(2)}) collective-permute-start(bf16[32,1024]{1,0:T(8,128)(2,1)S(1)} %get-tuple-element.77), channel_id=1, source_target_pairs={{0,24},{4,28},{8,16},{12,20},{16,8},{20,12},{24,0},{28,4},{1,25},{... | collective-permute-start | bytes 196616 | tf_op jit(solution)/shard_map/ppermute | solution.py:116
  36.0 1.9 %collective-permute-start.10 = (bf16[32,1024]{1,0:T(8,128)(2,1)S(1)}, bf16[32,1024]{1,0:T(8,128)(2,1)S(1)}, u32[]{:S(2)}, u32[]{:S(2)}) collective-permute-start(bf16[32,1024]{1,0:T(8,128)(2,1)S(1)} %get-tuple-element.77), channel_id=1, source_target_pairs={{0,16},{4,20},{8,24},{12,28},{16,0},{20,4},{24,8},{28,12},{1,17},{... | collective-permute-start | bytes 196616 | tf_op jit(solution)/shard_map/ppermute | solution.py:116
  37.9 1.4 %collective-permute-start.11 = (bf16[32,1024]{1,0:T(8,128)(2,1)S(1)}, bf16[32,1024]{1,0:T(8,128)(2,1)S(1)}, u32[]{:S(2)}, u32[]{:S(2)}) collective-permute-start(bf16[32,1024]{1,0:T(8,128)(2,1)S(1)} %get-tuple-element.77), channel_id=1, source_target_pairs={{0,8},{4,12},{8,0},{12,4},{16,24},{20,28},{24,16},{28,20},{1,9},{5... | collective-permute-start | bytes 196616 | tf_op jit(solution)/shard_map/ppermute | solution.py:116
  39.4 1.0 %collective-permute-done.10 = bf16[32,1024]{1,0:T(8,128)(2,1)S(1)} collective-permute-done((bf16[32,1024]{1,0:T(8,128)(2,1)S(1)}, bf16[32,1024]{1,0:T(8,128)(2,1)S(1)}, u32[]{:S(2)}, u32[]{:S(2)}) %collective-permute-start.10) | collective-permute-done | bytes 65568 | tf_op jit(solution)/shard_map/ppermute | solution.py:116
  40.3 2.0 %collective-permute-done.11 = bf16[32,1024]{1,0:T(8,128)(2,1)S(1)} collective-permute-done((bf16[32,1024]{1,0:T(8,128)(2,1)S(1)}, bf16[32,1024]{1,0:T(8,128)(2,1)S(1)}, u32[]{:S(2)}, u32[]{:S(2)}) %collective-permute-start.11) | collective-permute-done | bytes 65568 | tf_op jit(solution)/shard_map/ppermute | solution.py:116
  42.3 1.5 %collective-permute-done.12.refs_1_ = bf16[128,1024]{1,0:T(8,128)(2,1)S(1)} collective-permute-done((bf16[128,1024]{1,0:T(8,128)(2,1)S(1)}, bf16[128,1024]{1,0:T(8,128)(2,1)S(1)}, u32[]{:S(2)}, u32[]{:S(2)}) %collective-permute-start.12) | collective-permute-done | bytes 262176 | tf_op jit(solution)/shard_map/ppermute | solution.py:119
  43.8 1.2 %shard_map.180 = (f32[16,1024]{1,0:T(8,128)S(1)}, bf16[16,1024]{1,0:T(8,128)(2,1)S(1)}, bf16[16,1024]{1,0:T(8,128)(2,1)S(1)}, bf16[16,1024]{1,0:T(8,128)(2,1)S(1)}) custom-call(f32[4]{0:T(128)S(1)} %copy-done.7, bf16[256,1024]{1,0:T(8,128)(2,1)S(1)} %bitcast.5, bf16[32,512]{1,0:T(8,128)(2,1)S(1)} %get-tuple-element.76.query, ...), custom_call_target="tpu_custom_call" | custom-call | tf_op jit(solution)/shard_map/pallas_call | solution.py:595
  45.0 2.6 %collective-permute-start.13 = (bf16[16,1024]{1,0:T(8,128)(2,1)S(1)}, bf16[16,1024]{1,0:T(8,128)(2,1)S(1)}, u32[]{:S(2)}, u32[]{:S(2)}) collective-permute-start(bf16[16,1024]{1,0:T(8,128)(2,1)S(1)} %get-tuple-element.79), channel_id=1, source_target_pairs={{0,3},{1,2},{2,1},{3,0},{4,7},{5,6},{6,5},{7,4},{8,11},{9,10},{10,... | collective-permute-start | bytes 98312 | tf_op jit(solution)/shard_map/ppermute | solution.py:125
  47.6 1.8 %collective-permute-start.15 = (bf16[16,1024]{1,0:T(8,128)(2,1)S(1)}, bf16[16,1024]{1,0:T(8,128)(2,1)S(1)}, u32[]{:S(2)}, u32[]{:S(2)}) collective-permute-start(bf16[16,1024]{1,0:T(8,128)(2,1)S(1)} %get-tuple-element.81), channel_id=1, source_target_pairs={{0,1},{1,0},{2,3},{3,2},{4,5},{5,4},{6,7},{7,6},{8,9},{9,8},{10,11... | collective-permute-start | bytes 98312 | tf_op jit(solution)/shard_map/ppermute | solution.py:125
  49.4 1.4 %collective-permute-done.13.refs_1_ = bf16[16,1024]{1,0:T(8,128)(2,1)S(1)} collective-permute-done((bf16[16,1024]{1,0:T(8,128)(2,1)S(1)}, bf16[16,1024]{1,0:T(8,128)(2,1)S(1)}, u32[]{:S(2)}, u32[]{:S(2)}) %collective-permute-start.13) | collective-permute-done | bytes 32800 | tf_op jit(solution)/shard_map/ppermute | solution.py:125
  50.9 1.6 %collective-permute-done.14.refs_2_ = bf16[16,1024]{1,0:T(8,128)(2,1)S(1)} collective-permute-done((bf16[16,1024]{1,0:T(8,128)(2,1)S(1)}, bf16[16,1024]{1,0:T(8,128)(2,1)S(1)}, u32[]{:S(2)}, u32[]{:S(2)}) %collective-permute-start.14) | collective-permute-done | bytes 32800 | tf_op jit(solution)/shard_map/ppermute | solution.py:125
  52.6 2.0 %collective-permute-start.16 = (bf16[16,1024]{1,0:T(8,128)(2,1)S(1)}, bf16[16,1024]{1,0:T(8,128)(2,1)S(1)}, u32[]{:S(2)}, u32[]{:S(2)}) collective-permute-start(bf16[16,1024]{1,0:T(8,128)(2,1)S(1)} %get-tuple-element.83.refs_0_), channel_id=1, source_target_pairs={{0,3},{1,2},{2,1},{3,0},{4,7},{5,6},{6,5},{7,4},{8,11},{9,10},{10,... | collective-permute-start | bytes 98312 | tf_op jit(solution)/shard_map/ppermute | solution.py:107
  55.1 2.0 %collective-permute-start.18 = (bf16[16,1024]{1,0:T(8,128)(2,1)S(1)}, bf16[16,1024]{1,0:T(8,128)(2,1)S(1)}, u32[]{:S(2)}, u32[]{:S(2)}) collective-permute-start(bf16[16,1024]{1,0:T(8,128)(2,1)S(1)} %get-tuple-element.83.refs_0_), channel_id=1, source_target_pairs={{0,1},{1,0},{2,3},{3,2},{4,5},{5,4},{6,7},{7,6},{8,9},{9,8},{10,11... | collective-permute-start | bytes 98312 | tf_op jit(solution)/shard_map/ppermute | solution.py:107
  57.1 1.3 %collective-permute-done.16.refs_1_ = bf16[16,1024]{1,0:T(8,128)(2,1)S(1)} collective-permute-done((bf16[16,1024]{1,0:T(8,128)(2,1)S(1)}, bf16[16,1024]{1,0:T(8,128)(2,1)S(1)}, u32[]{:S(2)}, u32[]{:S(2)}) %collective-permute-start.16) | collective-permute-done | bytes 32800 | tf_op jit(solution)/shard_map/ppermute | solution.py:107
  58.4 1.4 %collective-permute-done.17.refs_2_ = bf16[16,1024]{1,0:T(8,128)(2,1)S(1)} collective-permute-done((bf16[16,1024]{1,0:T(8,128)(2,1)S(1)}, bf16[16,1024]{1,0:T(8,128)(2,1)S(1)}, u32[]{:S(2)}, u32[]{:S(2)}) %collective-permute-start.17) | collective-permute-done | bytes 32800 | tf_op jit(solution)/shard_map/ppermute | solution.py:107
  59.8 0.9 %shard_map.182 = (f32[16,1024]{1,0:T(8,128)S(1)}, bf16[16,1024]{1,0:T(8,128)(2,1)S(1)}, bf16[16,1024]{1,0:T(8,128)(2,1)S(1)}, bf16[16,1024]{1,0:T(8,128)(2,1)S(1)}) custom-call(bf16[1024,1024]{1,0:T(8,128)(2,1)S(1)} %copy-done.2, bf16[1024,1024]{1,0:T(8,128)(2,1)S(1)} %copy-done.3, bf16[16,1024]{1,0:T(8,128)(2,1)S(1)} %get-tuple-element.83.refs_0_, ...), custom_call_target="tpu_custom_call" | custom-call | tf_op jit(solution)/shard_map/pallas_call | solution.py:595
  60.8 1.9 %collective-permute-start.19 = (bf16[16,1024]{1,0:T(8,128)(2,1)S(1)}, bf16[16,1024]{1,0:T(8,128)(2,1)S(1)}, u32[]{:S(2)}, u32[]{:S(2)}) collective-permute-start(bf16[16,1024]{1,0:T(8,128)(2,1)S(1)} %get-tuple-element.85), channel_id=1, source_target_pairs={{0,3},{1,2},{2,1},{3,0},{4,7},{5,6},{6,5},{7,4},{8,11},{9,10},{10,... | collective-permute-start | bytes 98312 | tf_op jit(solution)/shard_map/ppermute | solution.py:125
  62.7 0.8 %collective-permute-start.20 = (bf16[16,1024]{1,0:T(8,128)(2,1)S(1)}, bf16[16,1024]{1,0:T(8,128)(2,1)S(1)}, u32[]{:S(2)}, u32[]{:S(2)}) collective-permute-start(bf16[16,1024]{1,0:T(8,128)(2,1)S(1)} %get-tuple-element.86), channel_id=1, source_target_pairs={{0,2},{1,3},{2,0},{3,1},{4,6},{5,7},{6,4},{7,5},{8,10},{9,11},{10,... | collective-permute-start | bytes 98312 | tf_op jit(solution)/shard_map/ppermute | solution.py:125
  63.4 1.8 %collective-permute-start.21 = (bf16[16,1024]{1,0:T(8,128)(2,1)S(1)}, bf16[16,1024]{1,0:T(8,128)(2,1)S(1)}, u32[]{:S(2)}, u32[]{:S(2)}) collective-permute-start(bf16[16,1024]{1,0:T(8,128)(2,1)S(1)} %get-tuple-element.87), channel_id=1, source_target_pairs={{0,1},{1,0},{2,3},{3,2},{4,5},{5,4},{6,7},{7,6},{8,9},{9,8},{10,11... | collective-permute-start | bytes 98312 | tf_op jit(solution)/shard_map/ppermute | solution.py:125
  66.6 1.1 %collective-permute-done.20.refs_2_ = bf16[16,1024]{1,0:T(8,128)(2,1)S(1)} collective-permute-done((bf16[16,1024]{1,0:T(8,128)(2,1)S(1)}, bf16[16,1024]{1,0:T(8,128)(2,1)S(1)}, u32[]{:S(2)}, u32[]{:S(2)}) %collective-permute-start.20) | collective-permute-done | bytes 32800 | tf_op jit(solution)/shard_map/ppermute | solution.py:125
  (45 shorter events, 6.4 us)
Async XLA Ops:
  2.5 10.7 %collective-permute-start.5 = (bf16[192,1024]{1,0:T(8,128)(2,1)S(1)}, bf16[192,1024]{1,0:T(8,128)(2,1)S(1)}, u32[]{:S(2)}, u32[]{:S(2)}) collective-permute-start(bf16[192,1024]{1,0:T(8,128)(2,1)S(1)} %get-tuple-element.64), channel_id=1, source_target_pairs={{0,4},{4,0},{8,12},{12,8},{16,20},{20,16},{24,28},{28,24},{1,5},{5... | collective-permute-start | bytes 1179656 | tf_op jit(solution)/shard_map/ppermute | solution.py:95
  3.1 11.7 %collective-permute-start.2 = (bf16[192,1024]{1,0:T(8,128)(2,1)S(1)}, bf16[192,1024]{1,0:T(8,128)(2,1)S(1)}, u32[]{:S(2)}, u32[]{:S(2)}) collective-permute-start(bf16[192,1024]{1,0:T(8,128)(2,1)S(1)} %get-tuple-element.59), channel_id=1, source_target_pairs={{4,8},{8,4},{12,16},{16,12},{20,24},{24,20},{5,9},{9,5},{13,17},{1... | collective-permute-start | bytes 1179656 | tf_op jit(solution)/shard_map/ppermute | solution.py:95
  3.8 6.3 %collective-permute-start = (bf16[96,1024]{1,0:T(8,128)(2,1)S(1)}, bf16[96,1024]{1,0:T(8,128)(2,1)S(1)}, u32[]{:S(2)}, u32[]{:S(2)}) collective-permute-start(bf16[96,1024]{1,0:T(8,128)(2,1)S(1)} %get-tuple-element.48), channel_id=1, source_target_pairs={{0,1},{1,0},{2,3},{3,2},{4,5},{5,4},{6,7},{7,6},{8,9},{9,8},{10,11... | collective-permute-start | bytes 589832 | tf_op jit(solution)/shard_map/ppermute | solution.py:95
  6.4 3.7 %collective-permute-start.1 = (bf16[96,1024]{1,0:T(8,128)(2,1)S(1)}, bf16[96,1024]{1,0:T(8,128)(2,1)S(1)}, u32[]{:S(2)}, u32[]{:S(2)}) collective-permute-start(bf16[96,1024]{1,0:T(8,128)(2,1)S(1)} %get-tuple-element.49), channel_id=1, source_target_pairs={{1,2},{2,1},{5,6},{6,5},{9,10},{10,9},{13,14},{14,13},{17,18},{18,... | collective-permute-start | bytes 589832 | tf_op jit(solution)/shard_map/ppermute | solution.py:95
  9.2 5.7 %copy-start.1 = (bf16[1024,1024]{1,0:T(8,128)(2,1)S(1)}, bf16[1024,1024]{1,0:T(8,128)(2,1)}, u32[]{:S(2)}) copy-start(bf16[1024,1024]{1,0:T(8,128)(2,1)} %weight.2) | copy-start | bytes 6291460
  10.4 4.4 %collective-permute-start.3 = (bf16[72,1024]{1,0:T(8,128)(2,1)S(1)}, bf16[72,1024]{1,0:T(8,128)(2,1)S(1)}, u32[]{:S(2)}, u32[]{:S(2)}) collective-permute-start(bf16[72,1024]{1,0:T(8,128)(2,1)S(1)} %get-tuple-element.62), channel_id=1, source_target_pairs={{0,4},{4,0},{8,12},{12,8},{16,20},{20,16},{24,28},{28,24},{1,5},{5... | collective-permute-start | bytes 442376 | tf_op jit(solution)/shard_map/ppermute | solution.py:95
  12.6 2.2 %collective-permute-start.4 = (bf16[72,1024]{1,0:T(8,128)(2,1)S(1)}, bf16[72,1024]{1,0:T(8,128)(2,1)S(1)}, u32[]{:S(2)}, u32[]{:S(2)}) collective-permute-start(bf16[72,1024]{1,0:T(8,128)(2,1)S(1)} %get-tuple-element.63), channel_id=1, source_target_pairs={{4,8},{8,4},{12,16},{16,12},{20,24},{24,20},{5,9},{9,5},{13,17},{1... | collective-permute-start | bytes 442376 | tf_op jit(solution)/shard_map/ppermute | solution.py:95
  14.9 9.1 %copy-start = (f32[256,4096]{1,0:T(8,128)S(1)}, f32[256,4096]{1,0:T(8,128)}, u32[]{:S(2)}) copy-start(f32[256,4096]{1,0:T(8,128)} %weight.3) | copy-start | bytes 12582916
  14.9 9.1 %copy-start.6 = (s32[2]{0:T(128)S(1)}, s32[2]{0:T(128)}, u32[]{:S(2)}) copy-start(s32[2]{0:T(128)} %index.1) | copy-start | bytes 28
  17.1 10.3 %copy-start.4 = (bf16[1024,4,192]{0,2,1:T(8,128)(2,1)S(1)}, bf16[1024,4,192]{0,2,1:T(8,128)(2,1)}, u32[]{:S(2)}) copy-start(bf16[1024,4,192]{0,2,1:T(8,128)(2,1)} %param.25) | copy-start | bytes 4718596
  17.1 8.4 %collective-permute-start.6 = (bf16[16,1024]{1,0:T(8,128)(2,1)S(1)}, bf16[16,1024]{1,0:T(8,128)(2,1)S(1)}, u32[]{:S(2)}, u32[]{:S(2)}) collective-permute-start(bf16[16,1024]{1,0:T(8,128)(2,1)S(1)} %get-tuple-element.75.refs_0_.coarse), channel_id=1, source_target_pairs={{0,3},{1,2},{2,1},{3,0},{4,7},{5,6},{6,5},{7,4},{8,11},{9,10},{10,... | collective-permute-start | bytes 98312 | tf_op jit(solution)/shard_map/ppermute | solution.py:107
  21.0 4.8 %collective-permute-start.7 = (bf16[16,1024]{1,0:T(8,128)(2,1)S(1)}, bf16[16,1024]{1,0:T(8,128)(2,1)S(1)}, u32[]{:S(2)}, u32[]{:S(2)}) collective-permute-start(bf16[16,1024]{1,0:T(8,128)(2,1)S(1)} %get-tuple-element.75.refs_0_.coarse), channel_id=1, source_target_pairs={{0,2},{1,3},{2,0},{3,1},{4,6},{5,7},{6,4},{7,5},{8,10},{9,11},{10,... | collective-permute-start | bytes 98312 | tf_op jit(solution)/shard_map/ppermute | solution.py:107
  23.5 3.9 %collective-permute-start.8 = (bf16[16,1024]{1,0:T(8,128)(2,1)S(1)}, bf16[16,1024]{1,0:T(8,128)(2,1)S(1)}, u32[]{:S(2)}, u32[]{:S(2)}) collective-permute-start(bf16[16,1024]{1,0:T(8,128)(2,1)S(1)} %get-tuple-element.75.refs_0_.coarse), channel_id=1, source_target_pairs={{0,1},{1,0},{2,3},{3,2},{4,5},{5,4},{6,7},{7,6},{8,9},{9,8},{10,11... | collective-permute-start | bytes 98312 | tf_op jit(solution)/shard_map/ppermute | solution.py:107
  24.0 19.9 %copy-start.5 = (bf16[4,64,1024]{2,1,0:T(8,128)(2,1)S(1)}, bf16[4,64,1024]{2,1,0:T(8,128)(2,1)}, u32[]{:S(2)}) copy-start(bf16[4,64,1024]{2,1,0:T(8,128)(2,1)} %param.27) | copy-start | bytes 1572868
  24.0 35.9 %copy-start.3 = (bf16[1024,1024]{1,0:T(8,128)(2,1)S(1)}, bf16[1024,1024]{1,0:T(8,128)(2,1)}, u32[]{:S(2)}) copy-start(bf16[1024,1024]{1,0:T(8,128)(2,1)} %down.1) | copy-start | bytes 6291460
  25.4 18.4 %copy-start.7 = (f32[4]{0:T(128)S(1)}, f32[4]{0:T(128)}, u32[]{:S(2)}) copy-start(f32[4]{0:T(128)} %scale.3) | copy-start | bytes 52
  25.4 34.4 %copy-start.2 = (bf16[1024,1024]{1,0:T(8,128)(2,1)S(1)}, bf16[1024,1024]{1,0:T(8,128)(2,1)}, u32[]{:S(2)}) copy-start(bf16[1024,1024]{1,0:T(8,128)(2,1)} %up.1) | copy-start | bytes 6291460
  28.4 10.9 %collective-permute-start.9 = (bf16[32,1024]{1,0:T(8,128)(2,1)S(1)}, bf16[32,1024]{1,0:T(8,128)(2,1)S(1)}, u32[]{:S(2)}, u32[]{:S(2)}) collective-permute-start(bf16[32,1024]{1,0:T(8,128)(2,1)S(1)} %get-tuple-element.77), channel_id=1, source_target_pairs={{0,24},{4,28},{8,16},{12,20},{16,8},{20,12},{24,0},{28,4},{1,25},{... | collective-permute-start | bytes 196616 | tf_op jit(solution)/shard_map/ppermute | solution.py:116
  36.0 4.3 %collective-permute-start.10 = (bf16[32,1024]{1,0:T(8,128)(2,1)S(1)}, bf16[32,1024]{1,0:T(8,128)(2,1)S(1)}, u32[]{:S(2)}, u32[]{:S(2)}) collective-permute-start(bf16[32,1024]{1,0:T(8,128)(2,1)S(1)} %get-tuple-element.77), channel_id=1, source_target_pairs={{0,16},{4,20},{8,24},{12,28},{16,0},{20,4},{24,8},{28,12},{1,17},{... | collective-permute-start | bytes 196616 | tf_op jit(solution)/shard_map/ppermute | solution.py:116
  37.9 4.3 %collective-permute-start.11 = (bf16[32,1024]{1,0:T(8,128)(2,1)S(1)}, bf16[32,1024]{1,0:T(8,128)(2,1)S(1)}, u32[]{:S(2)}, u32[]{:S(2)}) collective-permute-start(bf16[32,1024]{1,0:T(8,128)(2,1)S(1)} %get-tuple-element.77), channel_id=1, source_target_pairs={{0,8},{4,12},{8,0},{12,4},{16,24},{20,28},{24,16},{28,20},{1,9},{5... | collective-permute-start | bytes 196616 | tf_op jit(solution)/shard_map/ppermute | solution.py:116
  42.3 1.5 %collective-permute-start.12 = (bf16[128,1024]{1,0:T(8,128)(2,1)S(1)}, bf16[128,1024]{1,0:T(8,128)(2,1)S(1)}, u32[]{:S(2)}, u32[]{:S(2)}) collective-permute-start(bf16[128,1024]{1,0:T(8,128)(2,1)S(1)} %constant_dynamic-update-slice_fusion.refs_0_), channel_id=1, source_target_pairs={{0,4},{4,0},{8,12},{12,8},{16,20},{20,16},{24,28},{28,24},{1,5},{5... | collective-permute-start | bytes 786440 | tf_op jit(solution)/shard_map/ppermute | solution.py:119
  45.0 5.9 %collective-permute-start.13 = (bf16[16,1024]{1,0:T(8,128)(2,1)S(1)}, bf16[16,1024]{1,0:T(8,128)(2,1)S(1)}, u32[]{:S(2)}, u32[]{:S(2)}) collective-permute-start(bf16[16,1024]{1,0:T(8,128)(2,1)S(1)} %get-tuple-element.79), channel_id=1, source_target_pairs={{0,3},{1,2},{2,1},{3,0},{4,7},{5,6},{6,5},{7,4},{8,11},{9,10},{10,... | collective-permute-start | bytes 98312 | tf_op jit(solution)/shard_map/ppermute | solution.py:125
  47.6 4.8 %collective-permute-start.14 = (bf16[16,1024]{1,0:T(8,128)(2,1)S(1)}, bf16[16,1024]{1,0:T(8,128)(2,1)S(1)}, u32[]{:S(2)}, u32[]{:S(2)}) collective-permute-start(bf16[16,1024]{1,0:T(8,128)(2,1)S(1)} %get-tuple-element.80), channel_id=1, source_target_pairs={{0,2},{1,3},{2,0},{3,1},{4,6},{5,7},{6,4},{7,5},{8,10},{9,11},{10,... | collective-permute-start | bytes 98312 | tf_op jit(solution)/shard_map/ppermute | solution.py:125
  47.6 4.8 %collective-permute-start.15 = (bf16[16,1024]{1,0:T(8,128)(2,1)S(1)}, bf16[16,1024]{1,0:T(8,128)(2,1)S(1)}, u32[]{:S(2)}, u32[]{:S(2)}) collective-permute-start(bf16[16,1024]{1,0:T(8,128)(2,1)S(1)} %get-tuple-element.81), channel_id=1, source_target_pairs={{0,1},{1,0},{2,3},{3,2},{4,5},{5,4},{6,7},{7,6},{8,9},{9,8},{10,11... | collective-permute-start | bytes 98312 | tf_op jit(solution)/shard_map/ppermute | solution.py:125
  52.6 5.8 %collective-permute-start.16 = (bf16[16,1024]{1,0:T(8,128)(2,1)S(1)}, bf16[16,1024]{1,0:T(8,128)(2,1)S(1)}, u32[]{:S(2)}, u32[]{:S(2)}) collective-permute-start(bf16[16,1024]{1,0:T(8,128)(2,1)S(1)} %get-tuple-element.83.refs_0_), channel_id=1, source_target_pairs={{0,3},{1,2},{2,1},{3,0},{4,7},{5,6},{6,5},{7,4},{8,11},{9,10},{10,... | collective-permute-start | bytes 98312 | tf_op jit(solution)/shard_map/ppermute | solution.py:107
  54.7 5.2 %collective-permute-start.17 = (bf16[16,1024]{1,0:T(8,128)(2,1)S(1)}, bf16[16,1024]{1,0:T(8,128)(2,1)S(1)}, u32[]{:S(2)}, u32[]{:S(2)}) collective-permute-start(bf16[16,1024]{1,0:T(8,128)(2,1)S(1)} %get-tuple-element.83.refs_0_), channel_id=1, source_target_pairs={{0,2},{1,3},{2,0},{3,1},{4,6},{5,7},{6,4},{7,5},{8,10},{9,11},{10,... | collective-permute-start | bytes 98312 | tf_op jit(solution)/shard_map/ppermute | solution.py:107
  55.1 4.8 %collective-permute-start.18 = (bf16[16,1024]{1,0:T(8,128)(2,1)S(1)}, bf16[16,1024]{1,0:T(8,128)(2,1)S(1)}, u32[]{:S(2)}, u32[]{:S(2)}) collective-permute-start(bf16[16,1024]{1,0:T(8,128)(2,1)S(1)} %get-tuple-element.83.refs_0_), channel_id=1, source_target_pairs={{0,1},{1,0},{2,3},{3,2},{4,5},{5,4},{6,7},{7,6},{8,9},{9,8},{10,11... | collective-permute-start | bytes 98312 | tf_op jit(solution)/shard_map/ppermute | solution.py:107
  60.8 5.9 %collective-permute-start.19 = (bf16[16,1024]{1,0:T(8,128)(2,1)S(1)}, bf16[16,1024]{1,0:T(8,128)(2,1)S(1)}, u32[]{:S(2)}, u32[]{:S(2)}) collective-permute-start(bf16[16,1024]{1,0:T(8,128)(2,1)S(1)} %get-tuple-element.85), channel_id=1, source_target_pairs={{0,3},{1,2},{2,1},{3,0},{4,7},{5,6},{6,5},{7,4},{8,11},{9,10},{10,... | collective-permute-start | bytes 98312 | tf_op jit(solution)/shard_map/ppermute | solution.py:125
  62.7 5.0 %collective-permute-start.20 = (bf16[16,1024]{1,0:T(8,128)(2,1)S(1)}, bf16[16,1024]{1,0:T(8,128)(2,1)S(1)}, u32[]{:S(2)}, u32[]{:S(2)}) collective-permute-start(bf16[16,1024]{1,0:T(8,128)(2,1)S(1)} %get-tuple-element.86), channel_id=1, source_target_pairs={{0,2},{1,3},{2,0},{3,1},{4,6},{5,7},{6,4},{7,5},{8,10},{9,11},{10,... | collective-permute-start | bytes 98312 | tf_op jit(solution)/shard_map/ppermute | solution.py:125
  63.4 4.3 %collective-permute-start.21 = (bf16[16,1024]{1,0:T(8,128)(2,1)S(1)}, bf16[16,1024]{1,0:T(8,128)(2,1)S(1)}, u32[]{:S(2)}, u32[]{:S(2)}) collective-permute-start(bf16[16,1024]{1,0:T(8,128)(2,1)S(1)} %get-tuple-element.87), channel_id=1, source_target_pairs={{0,1},{1,0},{2,3},{3,2},{4,5},{5,4},{6,7},{7,6},{8,9},{9,8},{10,11... | collective-permute-start | bytes 98312 | tf_op jit(solution)/shard_map/ppermute | solution.py:125
